TPU v7x, 32 devices: a whole 2x2x4 slice. The times are simulated.
32 devices in a mesh: pipe: 2 (over core), seq: 8 (over z, x), tp: 2 (over y).
Axes of the slice: x: 2, y: 2, z: 4, core: 2. Of those that a mesh axis runs over, the one named last changes fastest.
Arguments:
- hidden_in: bfloat16 [1, 4096, 2560], P(None, ('seq', 'tp')), may hold values from -6 to 6
- doc_ids: int32 [1, 4096], P(None, 'seq'), may hold values from 0 to 1, never falling along the last dimension, each value on 1 to 3072 neighbouring positions
- norm_gain: float32 [2, 2560], P('pipe'), may hold values from 0.1 to 1.9
- in_zx: bfloat16 [2, 2560, 2, 5120], P('pipe', None, None, 'tp'), may hold values from -0.125 to 0.125
- in_bc: bfloat16 [2, 2560, 256], P('pipe'), may hold values from -0.125 to 0.125
- in_dt: bfloat16 [2, 2560, 80], P('pipe', None, 'tp'), may hold values from -0.125 to 0.125
- conv_x: float32 [2, 4, 5120], P('pipe', None, 'tp'), may hold values from -3 to 3
- conv_bc: float32 [2, 4, 256], P('pipe'), may hold values from -3 to 3
- bias_x: float32 [2, 5120], P('pipe', 'tp'), may hold values from -3 to 3
- bias_bc: float32 [2, 256], P('pipe'), may hold values from -3 to 3
- dt_bias: float32 [2, 80], P('pipe', 'tp'), may hold values from -2 to 1
- a_log: float32 [2, 80], P('pipe', 'tp'), may hold values from -12 to 0, as said below
- d_skip: float32 [2, 80], P('pipe', 'tp'), may hold values from 0.5 to 1.5
- gated_gain: float32 [2, 5120], P('pipe', 'tp'), may hold values from 0.1 to 1.9
- out_w: bfloat16 [2, 5120, 2560], P('pipe', 'tp'), may hold values from -0.078125 to 0.078125
Outputs:
- section_out: bfloat16 [2, 1, 4096, 2560], P('pipe', None, ('seq', 'tp'))
Inputs may be any that keep to these rules, and one draw needn't show every extreme that they name: `doc_ids`: in each row the document numbers start at 0, never fall, and rise by one where a new document begins; every document spans 1 to 3072 positions. `a_log`: logarithms of rates between 0.5 / 4096 and 1.
All inputs are finite; a program needn't handle non-finite values.
Results may differ from a plain program's by a relative error of at most 0.02.
Values may be sent and summed in bfloat16 or wider, within the bound.
No kernel may reach another device: no remote copies, remote signals or barrier semaphores. Data moves between devices by JAX's collectives and lax.ppermute only.
A program may use at most 192 MiB of HBM per device.

v0:
```python
import jax
import jax.numpy as jnp
from jax import lax
from jax.sharding import PartitionSpec as P

BLOCK = 256


epsilon = 1e-05
highest = lax.Precision.HIGHEST


def shifted(block, axis, distance):
    devices = range(lax.axis_size(axis))
    route = [(i - distance, i) for i in devices if i - distance in devices]
    return lax.ppermute(block, axis, route)


def carried_in(part, axis, combine, identity):
    place = lax.axis_index(axis)
    gathered = jax.tree.map(lambda a: lax.all_gather(a, axis), part)
    state = jax.tree.map(lambda a, e: jnp.zeros_like(a) + jnp.asarray(e, a.dtype), part, identity)

    def one(step, state):
        return combine(
            state, jax.tree.map(lambda a: lax.dynamic_index_in_dim(a, step, 0, False), gathered)
        )

    return lax.fori_loop(0, place, one, state)


def conv_mix(row_block, edge_rows, row_ids, edge_ids, weight, shift_bias):
    padded = jnp.concatenate([edge_rows, row_block], 0)
    padded_ids = jnp.concatenate([edge_ids, row_ids], 0)
    row_count = row_block.shape[0]
    running = jnp.zeros_like(row_block) + shift_bias[None, :]
    for offset in range(weight.shape[0]):
        keep_mask = (padded_ids[offset : offset + row_count] == row_ids).astype(jnp.float32)
        running = (
            running
            + keep_mask[:, None] * weight[offset][None, :] * padded[offset : offset + row_count]
        )
    return jax.nn.silu(running)


def block_step(state_in, inputs, decay_rates):
    x_block, step_sizes, b_block, c_block, seg_block, prev_id = inputs
    log_decay = jnp.cumsum(step_sizes * decay_rates[:, None], axis=1)
    block_length = seg_block.shape[0]
    causal_mask = jnp.arange(block_length)[:, None] >= jnp.arange(block_length)[None, :]
    same_doc = causal_mask & (seg_block[:, None] == seg_block[None, :])
    spread = log_decay[:, :, None] - log_decay[:, None, :]
    mixing = jnp.where(same_doc[None], jnp.exp(jnp.where(same_doc[None], spread, 0.0)), 0.0)
    gram_matrix = jnp.dot(c_block, b_block.T, precision=highest)
    weights = mixing * gram_matrix[None] * step_sizes[:, None, :]
    outputs = jnp.einsum("hps,hts->hpt", x_block, weights, precision=highest)
    carried = (seg_block == prev_id).astype(jnp.float32)
    outputs = outputs + jnp.exp(log_decay)[:, None, :] * carried[None, None, :] * jnp.einsum(
        "hpn,tn->hpt", state_in, c_block, precision=highest
    )
    end_weight = (
        jnp.exp(log_decay[:, -1:] - log_decay)
        * (seg_block == seg_block[-1]).astype(jnp.float32)[None, :]
        * step_sizes
    )
    fresh_state = jnp.einsum(
        "hps,sn->hpn", x_block * end_weight[:, None, :], b_block, precision=highest
    )
    keep_all = jnp.exp(log_decay[:, -1]) * (seg_block[-1] == prev_id).astype(jnp.float32)
    return (keep_all[:, None, None] * state_in + fresh_state, outputs)


def combine_carry(earlier, latter):
    return (earlier[0] * latter[0], latter[0][:, None, None] * earlier[1] + latter[1])


def rms_rows(hidden_f, norm_scale):
    return (
        hidden_f
        * lax.rsqrt(jnp.mean(hidden_f * hidden_f, axis=1, keepdims=True) + epsilon)
        * norm_scale[None, :]
    ).astype(jnp.bfloat16)


def project_rows(normed, weight_zx, weight_bc, weight_dt):
    return jnp.concatenate(
        [
            jnp.dot(normed, weight_zx, preferred_element_type=jnp.float32),
            jnp.dot(normed, weight_bc, preferred_element_type=jnp.float32),
            jnp.dot(normed, weight_dt, preferred_element_type=jnp.float32),
        ],
        1,
    )


def mixer_block(
    projected, row_ids, kernel, kernel_bias, dt_shift, log_rate, skip_scale, gate_scale
):
    local_width = gate_scale.shape[0]
    heads_local = dt_shift.shape[0]
    head_width = local_width // heads_local
    token_count = projected.shape[0]
    state_width = (kernel.shape[1] - local_width) // 2
    edge_count = kernel.shape[0] - 1
    gate_in = projected[:, :local_width]
    pre_conv = projected[:, local_width : 2 * local_width + 2 * state_width]
    dt_raw = projected[:, 2 * local_width + 2 * state_width :]
    edge_rows, edge_ids = shifted(
        (pre_conv[token_count - edge_count :], row_ids[token_count - edge_count :]), "seq", 1
    )
    conv_out = conv_mix(pre_conv, edge_rows, row_ids, edge_ids, kernel, kernel_bias)
    x_heads = conv_out[:, :local_width].T.reshape(heads_local, head_width, token_count)
    b_conv = conv_out[:, local_width : local_width + state_width]
    c_conv = conv_out[:, local_width + state_width :]
    step_sizes = jax.nn.softplus(dt_raw + dt_shift[None, :]).T
    decay_rates = -jnp.exp(log_rate)
    first_prev = edge_ids[edge_count - 1]
    state_run = jnp.zeros((heads_local, head_width, state_width), jnp.float32)
    pieces = []
    for block_index in range(token_count // BLOCK):
        block_begin = block_index * BLOCK
        block_end = block_begin + BLOCK
        prev_id = first_prev if block_index == 0 else row_ids[block_begin - 1]
        state_run, block_out = block_step(
            state_run,
            (
                x_heads[:, :, block_begin:block_end],
                step_sizes[:, block_begin:block_end],
                b_conv[block_begin:block_end],
                c_conv[block_begin:block_end],
                row_ids[block_begin:block_end],
                prev_id,
            ),
            decay_rates,
        )
        pieces.append(block_out)
    outputs = jnp.concatenate(pieces, 2)
    log_total = jnp.cumsum(step_sizes * decay_rates[:, None], axis=1)
    carried = (row_ids == first_prev).astype(jnp.float32)
    shard_keep = jnp.exp(log_total[:, -1]) * carried[token_count - 1]
    prefix_keep, incoming = carried_in(
        (shard_keep, state_run),
        "seq",
        combine_carry,
        (jnp.ones_like(shard_keep), jnp.zeros_like(state_run)),
    )
    outputs = outputs + jnp.exp(log_total)[:, None, :] * carried[None, None, :] * jnp.einsum(
        "hpn,tn->hpt", incoming, c_conv, precision=highest
    )
    outputs = outputs + skip_scale[:, None, None] * x_heads
    gated_rows = outputs.reshape(local_width, token_count).T * jax.nn.silu(gate_in)
    total_sq = lax.psum(jnp.sum(gated_rows * gated_rows, axis=1), "tp")
    full_width = local_width * lax.axis_size("tp")
    return (
        gated_rows * lax.rsqrt(total_sq / full_width + epsilon)[:, None] * gate_scale[None, :]
    ).astype(jnp.bfloat16)


def local(
    hidden_in,
    doc_ids,
    norm_gain,
    in_zx,
    in_bc,
    in_dt,
    conv_x,
    conv_bc,
    bias_x,
    bias_bc,
    dt_bias,
    a_log,
    d_skip,
    gated_gain,
    out_w,
):
    sections = lax.axis_size("pipe")
    section_index = lax.axis_index("pipe")
    micro_count = hidden_in.shape[0]
    local_width = gated_gain.shape[1]
    weight_zx = in_zx[0].reshape(in_zx.shape[1], 2 * local_width)
    weight_bc = in_bc[0]
    weight_dt = in_dt[0]
    kernel = jnp.concatenate([conv_x[0], conv_bc[0]], 1)
    kernel_bias = jnp.concatenate([bias_x[0], bias_bc[0]], 0)
    weight_out = out_w[0]
    saved_slots = [jnp.zeros_like(hidden_in[0])]
    received = jnp.zeros_like(hidden_in[0])
    finished = received
    for tick_index in range(micro_count + sections - 1):
        if tick_index > 0:
            received = shifted(finished, "pipe", 1)
        fresh_rows = hidden_in[tick_index] if tick_index < micro_count else jnp.zeros_like(received)
        current = jnp.where(section_index == 0, fresh_rows, received)
        micro_index = tick_index - section_index
        row_ids = lax.dynamic_index_in_dim(
            doc_ids, jnp.clip(micro_index, 0, micro_count - 1), 0, keepdims=False
        ).astype(jnp.float32)
        current_f = current.astype(jnp.float32)
        normed = rms_rows(current_f, norm_gain[0])
        projected = project_rows(
            lax.all_gather(normed, "tp", axis=0, tiled=True), weight_zx, weight_bc, weight_dt
        )
        branch_in = mixer_block(
            projected, row_ids, kernel, kernel_bias, dt_bias[0], a_log[0], d_skip[0], gated_gain[0]
        )
        branch = lax.psum_scatter(
            jnp.dot(branch_in, weight_out, preferred_element_type=jnp.float32).astype(jnp.bfloat16),
            "tp",
            scatter_dimension=0,
            tiled=True,
        ).astype(jnp.float32)
        finished = (current_f + branch).astype(jnp.bfloat16)
        saved_slots[0] = jnp.where(micro_index == 0, finished, saved_slots[0])
    stacked = jnp.stack(saved_slots)
    return stacked[None]


def solution(mesh):
    placed = (
        P(None, ("seq", "tp"), None),
        P(None, "seq"),
        P("pipe", None),
        P("pipe", None, None, "tp"),
        P("pipe", None, None),
        P("pipe", None, "tp"),
        P("pipe", None, "tp"),
        P("pipe", None, None),
        P("pipe", "tp"),
        P("pipe", None),
        P("pipe", "tp"),
        P("pipe", "tp"),
        P("pipe", "tp"),
        P("pipe", "tp"),
        P("pipe", "tp", None),
    )
    return jax.shard_map(
        local,
        mesh=mesh,
        in_specs=placed,
        out_specs=P("pipe", None, ("seq", "tp"), None),
        check_vma=False,
    )
```

profile of v0, /device:TPU:1, one launch (start us, length us, event | category | flops | bytes accessed | tf_op | source)
XLA Modules:
  0.0 731.1 jit_solution(4446704095042366092)
XLA Ops:
  13.3 18.6 %copy.106 = bf16[320,8,2,2560]{3,1,2,0:T(8,128)(2,1)} copy(bf16[320,8,2,2560]{3,2,1,0:T(2,128)(2,1)} %bitcast.242) | data formatting | bytes 52428800
  39.1 13.9 %all-gather.9.cloned.1.call-done = bf16[512,2560]{1,0:T(8,128)(2,1)} async-done(((bf16[256,2560]{1,0:T(8,128)(2,1)}), bf16[512,2560]{1,0:T(8,128)(2,1)}) %all-gather.9.cloned.1.call-update) | async-done | bytes 2621456 | tf_op jit(solution)/shard_map/all_gather | solution.py:201
  53.0 17.9 %fusion.210 = f32[512,5120]{1,0:T(8,128)S(1)} fusion(bf16[512,2560]{1,0:T(8,128)(2,1)} %all-gather.9.cloned.1.call-done, bf16[2560,5120]{1,0:T(8,128)(2,1)} %bitcast.243), kind=kOutput, calls=%fused_computation.303 | convolution fusion | flops 13421772800 | bytes 39321600 | tf_op jit(solution)/shard_map/dot_general | solution.py:88
  70.9 4.5 fusion.130
  87.5 13.1 %divide_multiply_fusion.1 = f32[512,2816]{1,0:T(8,128)S(1)} fusion(f32[512,2816]{1,0:T(8,128)} %pad_maximum_fusion.3, f32[3,2816]{1,0:T(4,128)S(1)} %collective-permute-done.1, f32[2816]{0:T(1024)S(1)} %get-tuple-element.97, f32[512]{0:T(512)S(1)} %get-tuple-element.141, f32[2816]{0:T(1024)S(1)} %get-tuple-element.98, f32[512]{0:T(512)S(1)} %get-tuple-element.143, ...), kind=kLoop, calls=%fused_computation.65 | loop fusion | flops 27394048 | bytes 11632640 | tf_op jit(solution)/shard_map/jit(silu)/mul | solution.py:43
  106.1 5.9 copy.75
  112.0 4.0 fusion.120
  117.1 5.1 multiply_add_fusion.5
  127.2 19.5 %all-reduce = f32[320]{0:T(512)S(1)} all-reduce(f32[320]{0:T(512)S(1)} %dynamic-update-slice), channel_id=2, replica_groups=mesh['pipe'=2,'seq'=8,'tp'=2] {'seq'}, use_global_device_ids=true, to_apply=%add | all-reduce | flops 320 | bytes 2560
  156.4 13.5 %multiply_add_fusion.3 = f32[40,64,256]{2,1,0:T(8,128)} fusion(f32[40,64,256]{2,1,0:T(8,128)S(1)} %fusion.140, f32[40,256]{1,0:T(8,128)S(1)} %get-tuple-element.130, f32[256,256]{1,0:T(8,128)S(1)} %fusion.180, f32[40,256]{1,0:T(8,128)S(1)} %copy_bitcast_fusion.7, pred[256,256]{1,0:T(8,128)(4,1)S(1)} %fusion.143, f32[40,64,512]{2,1,0:T(8,128)S(1)} %bitcast.233, ...), kind=kOutput, calls=%fused_computation.133 | convolution fusion | flops 2027683840 | bytes 8355840 | tf_op jit(solution)/shard_map/hps,hts->hpt/dot_general | solution.py:56
  169.9 13.5 %multiply_add_fusion.2 = f32[40,64,256]{2,1,0:T(8,128)} fusion(f32[40,64,256]{2,1,0:T(8,128)S(1)} %fusion.160, f32[40,256]{1,0:T(8,128)S(1)} %get-tuple-element.129, f32[256,256]{1,0:T(8,128)S(1)} %fusion.175, f32[40,256]{1,0:T(8,128)S(1)} %copy_bitcast_fusion.6, pred[256,256]{1,0:T(8,128)(4,1)S(1)} %fusion.142, f32[40,64,512]{2,1,0:T(8,128)S(1)} %bitcast.234, ...), kind=kOutput, calls=%fused_computation.130 | convolution fusion | flops 2027683840 | bytes 8355840 | tf_op jit(solution)/shard_map/hps,hts->hpt/dot_general | solution.py:56
  183.4 90.8 %all-gather.13.cloned.1.call-done = f32[320,64,128]{2,1,0:T(8,128)} async-done(((f32[40,64,128]{2,1,0:T(8,128)}), f32[320,64,128]{2,1,0:T(8,128)}) %all-gather.13.cloned.1.call-update) | async-done | bytes 10485776 | tf_op jit(solution)/shard_map/all_gather | solution.py:21
  275.0 9.0 %fusion.44 = f32[40,64,512]{2,1,0:T(8,128)} fusion(f32[40,64,256]{2,1,0:T(8,128)} %multiply_add_fusion.2, f32[40,64,256]{2,1,0:T(8,128)} %multiply_add_fusion.3, f32[40,64,512]{2,1,0:T(8,128)} %bitcast.230, f32[40]{0:T(128)S(1)} %bitcast.261, f32[40,512]{1,0:T(8,128)S(1)} %exponential_multiply_fusion.1, f32[40,64,128]{2,1,0:T(8,128)S(1)} %get-tuple-element.93, ...), kind=kOutput, calls=%fused_computation.69 | convolution fusion | flops 2019819520 | bytes 17383584 | tf_op jit(solution)/shard_map/hpn,tn->hpt/dot_general | solution.py:147
  284.0 6.0 copy.82
  290.0 4.9 multiply_reduce_fusion.1
  298.6 16.6 %fusion.70 = bf16[512,2560]{1,0:T(8,128)(2,1)} fusion(bf16[1,2560,2560]{2,1,0:T(8,128)(2,1)} %param.33, f32[2560]{0:T(1024)S(1)} %reduce.12, f32[512]{0:T(512)S(1)} %add_rsqrt_fusion.1, f32[2560,512]{0,1:T(8,128)} %copy.82, f32[512,5120]{1,0:T(8,128)} %copy-done.1), kind=kOutput, calls=%fused_computation.102 | convolution fusion | flops 6722682880 | bytes 26226688 | tf_op jit(solution)/shard_map/dot_general | solution.py:207
  315.3 48.8 %reduce-scatter.3.cloned.1.call-done = bf16[256,2560]{1,0:T(8,128)(2,1)} async-done(((bf16[512,2560]{1,0:T(8,128)(2,1)}), bf16[256,2560]{1,0:T(8,128)(2,1)}) %reduce-scatter.3.cloned.1.call-update) | async-done | bytes 1310736 | tf_op jit(solution)/shard_map/reduce_scatter | solution.py:206
  373.5 38.2 %all-gather.11.cloned.1.call-done = bf16[512,2560]{1,0:T(8,128)(2,1)} async-done(((bf16[256,2560]{1,0:T(8,128)(2,1)}), bf16[512,2560]{1,0:T(8,128)(2,1)}) %all-gather.11.cloned.1.call-update) | async-done | bytes 2621456 | tf_op jit(solution)/shard_map/all_gather | solution.py:201
  411.8 17.9 %fusion.211 = f32[512,5120]{1,0:T(8,128)S(1)} fusion(bf16[512,2560]{1,0:T(8,128)(2,1)} %all-gather.11.cloned.1.call-done, bf16[2560,5120]{1,0:T(8,128)(2,1)} %bitcast.244), kind=kOutput, calls=%fused_computation.304 | convolution fusion | flops 13421772800 | bytes 39321600 | tf_op jit(solution)/shard_map/dot_general | solution.py:88
  429.7 4.5 fusion.128
  444.7 12.9 %divide_multiply_fusion = f32[512,2816]{1,0:T(8,128)S(1)} fusion(f32[512,2816]{1,0:T(8,128)} %pad_maximum_fusion.1, f32[3,2816]{1,0:T(4,128)S(1)} %collective-permute-done.3, f32[2816]{0:T(1024)S(1)} %get-tuple-element.97, f32[512]{0:T(512)S(1)} %get-tuple-element.141, f32[2816]{0:T(1024)S(1)} %get-tuple-element.98, f32[512]{0:T(512)S(1)} %get-tuple-element.143, ...), kind=kLoop, calls=%fused_computation.64 | loop fusion | flops 27394048 | bytes 11632640 | tf_op jit(solution)/shard_map/jit(silu)/mul | solution.py:43
  463.3 5.9 copy.84
  474.2 5.1 multiply_add_fusion.4
  482.2 18.8 %all-reduce.1 = f32[320]{0:T(512)S(1)} all-reduce(f32[320]{0:T(512)S(1)} %dynamic-update-slice.1), channel_id=4, replica_groups=mesh['pipe'=2,'seq'=8,'tp'=2] {'seq'}, use_global_device_ids=true, to_apply=%add.1 | all-reduce | flops 320 | bytes 2560
  510.8 13.5 %multiply_add_fusion.1 = f32[40,64,256]{2,1,0:T(8,128)} fusion(f32[40,64,256]{2,1,0:T(8,128)S(1)} %fusion.138, f32[40,256]{1,0:T(8,128)S(1)} %get-tuple-element.126, f32[256,256]{1,0:T(8,128)S(1)} %fusion.170, f32[40,256]{1,0:T(8,128)S(1)} %copy_bitcast_fusion.5, pred[256,256]{1,0:T(8,128)(4,1)S(1)} %fusion.143, f32[40,64,512]{2,1,0:T(8,128)S(1)} %bitcast.240, ...), kind=kOutput, calls=%fused_computation.124 | convolution fusion | flops 2027683840 | bytes 8355840 | tf_op jit(solution)/shard_map/hps,hts->hpt/dot_general | solution.py:56
  524.2 13.5 %multiply_add_fusion = f32[40,64,256]{2,1,0:T(8,128)} fusion(f32[40,64,256]{2,1,0:T(8,128)S(1)} %fusion.151, f32[40,256]{1,0:T(8,128)S(1)} %get-tuple-element.125, f32[256,256]{1,0:T(8,128)S(1)} %fusion.165, f32[40,256]{1,0:T(8,128)S(1)} %copy_bitcast_fusion.4, pred[256,256]{1,0:T(8,128)(4,1)S(1)} %fusion.142, f32[40,64,512]{2,1,0:T(8,128)S(1)} %bitcast.241, ...), kind=kOutput, calls=%fused_computation.121 | convolution fusion | flops 2027683840 | bytes 8355840 | tf_op jit(solution)/shard_map/hps,hts->hpt/dot_general | solution.py:56
  537.7 93.6 %all-gather.15.cloned.1.call-done = f32[320,64,128]{2,1,0:T(8,128)} async-done(((f32[40,64,128]{2,1,0:T(8,128)}), f32[320,64,128]{2,1,0:T(8,128)}) %all-gather.15.cloned.1.call-update) | async-done | bytes 10485776 | tf_op jit(solution)/shard_map/all_gather | solution.py:21
  631.7 8.9 %fusion.45 = f32[40,64,512]{2,1,0:T(8,128)} fusion(f32[40,64,256]{2,1,0:T(8,128)} %multiply_add_fusion, f32[40,64,256]{2,1,0:T(8,128)} %multiply_add_fusion.1, f32[40,64,512]{2,1,0:T(8,128)} %bitcast.237, f32[40,512]{1,0:T(8,128)S(1)} %exponential_multiply_fusion, f32[40]{0:T(128)S(1)} %bitcast.262, f32[40,64,128]{2,1,0:T(8,128)S(1)} %get-tuple-element.94, ...), kind=kOutput, calls=%fused_computation.71 | convolution fusion | flops 2019819520 | bytes 17383584 | tf_op jit(solution)/shard_map/hpn,tn->hpt/dot_general | solution.py:147
  640.7 5.9 copy.91
  646.6 4.9 multiply_reduce_fusion
  655.2 16.5 %fusion.73 = bf16[512,2560]{1,0:T(8,128)(2,1)} fusion(bf16[1,2560,2560]{2,1,0:T(8,128)(2,1)} %param.33, f32[512]{0:T(512)S(1)} %add_rsqrt_fusion, f32[2560]{0:T(1024)S(1)} %reduce.12, f32[2560,512]{0,1:T(8,128)} %copy.91, f32[512,5120]{1,0:T(8,128)} %copy-done.2), kind=kOutput, calls=%fused_computation.103 | convolution fusion | flops 6722682880 | bytes 26226688 | tf_op jit(solution)/shard_map/dot_general | solution.py:207
  671.8 49.0 %reduce-scatter.5.cloned.1.call-done = bf16[256,2560]{1,0:T(8,128)(2,1)} async-done(((bf16[512,2560]{1,0:T(8,128)(2,1)}), bf16[256,2560]{1,0:T(8,128)(2,1)}) %reduce-scatter.5.cloned.1.call-update) | async-done | bytes 1310736 | tf_op jit(solution)/shard_map/reduce_scatter | solution.py:206
  (186 shorter events, 98.3 us)
Async XLA Ops:
  6.5 64.4 %copy-start = (bf16[1,2560,256]{2,1,0:T(8,128)(2,1)S(1)}, bf16[1,2560,256]{2,1,0:T(8,128)(2,1)}, u32[]{:S(2)}) copy-start(bf16[1,2560,256]{2,1,0:T(8,128)(2,1)} %param.23) | copy-start | bytes 3932164
  6.5 2.7 copy-start.20
  6.5 46.5 %all-gather.9.cloned.1.call-start = ((), (), s32[]{:S(2)}) async-start(), calls=%async_computation.2 | async-start | bytes 3932160 | tf_op jit(solution)/shard_map/all_gather | solution.py:201
  9.2 265.0 %all-gather.13.cloned.1.call-start = ((), (), s32[]{:S(2)}) async-start(), calls=%async_computation.6 | async-start | bytes 11796480 | tf_op jit(solution)/shard_map/all_gather | solution.py:21
  9.4 24.8 %collective-permute-start = (f32[3]{0:T(128)S(1)}, f32[3]{0:T(128)S(1)}, u32[]{:S(2)}, u32[]{:S(2)}) collective-permute-start(f32[3]{0:T(128)S(1)} %slice_bitcast_fusion.6), channel_id=1, source_target_pairs={{0,2},{2,4},{4,6},{6,8},{8,10},{10,12},{12,14},{1,3},{3,5},{5,7},{... | collective-permute-start | bytes 44 | tf_op jit(solution)/shard_map/ppermute | solution.py:16
  13.3 18.7 %copy-start.15 = (f32[1,2560]{1,0:T(1,128)S(1)}, f32[1,2560]{1,0:T(1,128)}, u32[]{:S(2)}) copy-start(f32[1,2560]{1,0:T(1,128)} %param.27) | copy-start | bytes 30724
  13.3 20.7 %copy-start.14 = (f32[1,4,2560]{2,1,0:T(4,128)S(1)}, f32[1,4,2560]{2,1,0:T(4,128)}, u32[]{:S(2)}) copy-start(f32[1,4,2560]{2,1,0:T(4,128)} %param.25) | copy-start | bytes 122884
  13.3 20.7 %copy-start.18 = (f32[1,4,256]{2,1,0:T(4,128)S(1)}, f32[1,4,256]{2,1,0:T(4,128)}, u32[]{:S(2)}) copy-start(f32[1,4,256]{2,1,0:T(4,128)} %param.26) | copy-start | bytes 12292
  13.3 20.8 %copy-start.21 = (f32[1,256]{1,0:T(1,128)S(1)}, f32[1,256]{1,0:T(1,128)}, u32[]{:S(2)}) copy-start(f32[1,256]{1,0:T(1,128)} %param.28) | copy-start | bytes 3076
  13.3 20.8 %copy-start.22 = (f32[1,40]{1,0:T(1,128)S(1)}, f32[1,40]{1,0:T(1,128)}, u32[]{:S(2)}) copy-start(f32[1,40]{1,0:T(1,128)} %param.30) | copy-start | bytes 484
  70.9 7.5 %copy-start.1 = (f32[512,5120]{1,0:T(8,128)}, f32[512,5120]{1,0:T(8,128)S(1)}, u32[]{:S(2)}) copy-start(f32[512,5120]{1,0:T(8,128)S(1)} %fusion.210) | copy-start | bytes 31457284
  78.4 1.7 copy-start.17
  83.3 4.2 collective-permute-start.1
  100.7 2.4 copy-start.3
  112.0 10.3 %copy-start.16 = (f32[1,2560]{1,0:T(1,128)S(1)}, f32[1,2560]{1,0:T(1,128)}, u32[]{:S(2)}) copy-start(f32[1,2560]{1,0:T(1,128)} %param.32) | copy-start | bytes 30724
  112.0 10.4 %copy-start.23 = (u32[32]{0:T(128)S(1)}, u32[32]{0:T(128)}, u32[]{:S(2)}) copy-start(u32[32]{0:T(128)} %constant.100) | copy-start | bytes 388
  117.1 39.3 %slice-start = ((s8[5242880]{0:T(1024)(128)(4,1)}), s8[1048576]{0:T(1024)(128)(4,1)S(1)}, s32[]{:S(2)}) async-start(s8[5242880]{0:T(1024)(128)(4,1)} %bitcast.231), calls=%async_computation.8 | async-start | bytes 2097152
  122.2 241.9 %reduce-scatter.3.cloned.1.call-start = ((), (), s32[]{:S(2)}) async-start(), calls=%async_computation.3 | async-start | bytes 3932160 | tf_op jit(solution)/shard_map/reduce_scatter | solution.py:206
  146.8 9.5 %slice-start.1 = ((s8[5242880]{0:T(1024)(128)(4,1)}), s8[4194304]{0:T(1024)(128)(4,1)S(1)}, s32[]{:S(2)}) async-start(s8[5242880]{0:T(1024)(128)(4,1)} %bitcast.231), calls=%async_computation.9 | async-start | bytes 8388608
  298.6 65.5 %copy-start.5 = (bf16[1,256,2560]{2,1,0:T(8,128)(2,1)S(1)}, bf16[1,256,2560]{2,1,0:T(8,128)(2,1)}, u32[]{:S(2)}) copy-start(bf16[1,256,2560]{2,1,0:T(8,128)(2,1)} %param.19) | copy-start | bytes 3932164
  315.3 96.5 %all-gather.11.cloned.1.call-start = ((), (), s32[]{:S(2)}) async-start(), calls=%async_computation.4 | async-start | bytes 3932160 | tf_op jit(solution)/shard_map/all_gather | solution.py:201
  365.8 4.9 copy-start.12
  365.8 4.9 collective-permute-start.2
  373.3 258.0 %all-gather.15.cloned.1.call-start = ((), (), s32[]{:S(2)}) async-start(), calls=%async_computation.7 | async-start | bytes 11796480 | tf_op jit(solution)/shard_map/all_gather | solution.py:21
  429.6 4.6 copy-start.2
  434.2 2.9 copy-start.11
  440.5 4.2 collective-permute-start.3
  457.6 2.5 copy-start.4
  474.2 36.5 %slice-start.2 = ((s8[5242880]{0:T(1024)(128)(4,1)}), s8[1048576]{0:T(1024)(128)(4,1)S(1)}, s32[]{:S(2)}) async-start(s8[5242880]{0:T(1024)(128)(4,1)} %bitcast.238), calls=%async_computation.10 | async-start | bytes 2097152
  479.4 241.4 %reduce-scatter.5.cloned.1.call-start = ((), (), s32[]{:S(2)}) async-start(), calls=%async_computation.5 | async-start | bytes 3932160 | tf_op jit(solution)/shard_map/reduce_scatter | solution.py:206
  501.2 9.5 %slice-start.3 = ((s8[5242880]{0:T(1024)(128)(4,1)}), s8[4194304]{0:T(1024)(128)(4,1)S(1)}, s32[]{:S(2)}) async-start(s8[5242880]{0:T(1024)(128)(4,1)} %bitcast.238), calls=%async_computation.11 | async-start | bytes 8388608
  655.2 65.5 %copy-start.7 = (bf16[256,2560]{1,0:T(8,128)(2,1)S(1)}, bf16[256,2560]{1,0:T(8,128)(2,1)}, u32[]{:S(2)}) copy-start(bf16[256,2560]{1,0:T(8,128)(2,1)} %copy-done.6) | copy-start | bytes 3932164
  (6 other events, 7.3 us)
Sparse Core Ops, SparseCore 0:
  9.3 43.6 all-gather.8
  122.3 151.8 all-gather.12
  315.4 48.6 reduce-scatter.2
  373.4 38.3 all-gather.10
  479.5 151.8 all-gather.14
  671.9 48.8 reduce-scatter.4
where the time goes:
time: 739 us; the launch traced here: 731 us
  waiting for transfers between devices  340 us (46%)
  matrix products  189 us (26%)
  local copies, waits for them, and re-layouts  63.4 us (9%)
  other arithmetic  62 us (8%)
  blocking collectives  45.8 us (6%)
  between operations  18.1 us (2%)
  starting transfers between devices  12.2 us (2%)
    all_gather x2, waiting for transfers between devices, carried_in(): gathered = jax.tree.map(lambda a: lax.all_gather(a, axis), part)  184 us
    reduce_scatter x2, waiting for transfers between devices, local(): lax.psum_scatter(jnp.dot(branch_in, weight_out, preferred_element_type=jn...  97.7 us
    dot_general x4, matrix products, block_step(): outputs = jnp.einsum('hps,hts->hpt', x_block, weights, precision=highest)  54 us
    all_gather x2, waiting for transfers between devices, local(): lax.all_gather(normed, 'tp', axis=0, tiled=True)  52.1 us
    unnamed x2, blocking collectives  38.3 us
    dot_general x2, matrix products, project_rows(): jnp.dot(normed, weight_zx, preferred_element_type=jnp.float32)  35.8 us
    dot_general x2, matrix products, local(): jnp.dot(branch_in, weight_out, preferred_element_type=jnp.float32)  33.1 us
    unnamed x62, local copies, waits for them, and re-layouts  29.4 us
  transfers between devices with their start and end apart: 10, of which 9 were waited for; matrix products, arithmetic and copies ran while one was open for 14% of the time, Pallas kernels for 0%

commit v1 on v0

v1 whole, which is shorter than its diff:
```python
import functools

import jax
import jax.numpy as jnp
from jax import lax
from jax.experimental import pallas as pl
from jax.experimental.pallas import tpu as pltpu
from jax.sharding import PartitionSpec as P

AXES = ("pipe", "seq", "tp")
BLOCK = 256
HALO = 16
KEEP_ROWS = 16
LANES = 128
epsilon = 1e-05
highest = lax.Precision.HIGHEST
f32 = jnp.float32
bf16 = jnp.bfloat16


def dot(a, b):
    return jnp.dot(a, b, preferred_element_type=f32)


def cost(micros):
    return pl.CostEstimate(flops=int(micros * 2.5e8), bytes_accessed=0, transcendentals=0)


def silu(v):
    half = 0.5 * v
    return half + half * jnp.tanh(half)


def softplus(v):
    return jnp.maximum(v, 0.0) + jnp.log1p(jnp.exp(-jnp.abs(v)))


def spread_matrix(heads, width, tile):
    rows = lax.broadcasted_iota(jnp.int32, (LANES, heads * width), 0) - tile * heads
    cols = lax.broadcasted_iota(jnp.int32, (LANES, heads * width), 1)
    inside = (cols >= rows * width) & (cols < (rows + 1) * width)
    return jnp.where(inside, 1.0, 0.0).astype(bf16)


def conv_rows(raw_ref, keep_ref, taps, bias, start, stop, col):
    width = LANES
    out = bias + taps[3:4] * raw_ref[start + 8 : stop + 8, col : col + width]
    for tap in range(3):
        shifted_rows = raw_ref[start + 5 + tap : stop + 5 + tap, col : col + width]
        out = out + keep_ref[tap, start:stop] * (taps[tap : tap + 1] * shifted_rows)
    return silu(out)


def scan_kernel(rows, heads, width, shares, at_ref, *refs):
    part_refs, halo_refs = refs[:shares], refs[shares : 2 * shares]
    (
        gain_ref,
        small_ref,
        wx_ref,
        tapx_ref,
        tapbc_ref,
        biasx_ref,
        biasbc_ref,
        dtb_ref,
        rate_ref,
        idc_ref,
        lhs,
        x_ref,
        xs_ref,
        bc_ref,
        acol_ref,
        arow_ref,
        ein_ref,
        eall_ref,
        state_ref,
        sent_ref,
        raw,
        keep,
        stepc,
        wend,
        kept,
    ) = refs[2 * shares :]
    step_at = pl.program_id(0)
    blocks = rows // BLOCK
    state_width = bc_ref.shape[1] // 2
    tile_lanes = heads * width
    unit = 256 if tile_lanes % 256 == 0 else LANES
    units = tile_lanes // unit

    @pl.when(step_at == 0)
    def _():
        gain = gain_ref[...]

        def normalize(part):
            scale = lax.rsqrt(jnp.mean(part * part, axis=1, keepdims=True) + epsilon)
            return (part * scale * gain).astype(bf16)

        for share in range(shares):
            for begin in range(0, rows // shares, HALO):
                place = pl.multiple_of(at_ref[share] + begin, HALO)
                part = part_refs[share][begin : begin + HALO].astype(f32)
                lhs[pl.ds(place, HALO)] = normalize(part)
        halo = halo_refs[0][...].astype(f32)
        for other in halo_refs[1:]:
            halo = halo + other[...].astype(f32)
        lhs[rows:] = normalize(halo)
        small = dot(lhs[...], small_ref[...])
        for tap in range(3):
            keep[tap] = (idc_ref[5 + tap : 5 + tap + rows] == idc_ref[8 : 8 + rows]).astype(f32)
        raw[0:8, 0 : 2 * state_width] = small[rows + HALO - 8 :, : 2 * state_width]
        raw[8 : 8 + rows, 0 : 2 * state_width] = small[:rows, : 2 * state_width]
        for col in range(0, 2 * state_width, LANES):
            bc_ref[:, col : col + LANES] = conv_rows(
                raw,
                keep,
                tapbc_ref[:, col : col + LANES],
                biasbc_ref[:, col : col + LANES],
                0,
                rows,
                col,
            ).astype(bf16)
        step = softplus(small[:rows, 2 * state_width :] + dtb_ref[...])
        log_step = step * rate_ref[...]
        at = lax.broadcasted_iota(jnp.int32, (BLOCK, BLOCK), 0)
        to = lax.broadcasted_iota(jnp.int32, (BLOCK, BLOCK), 1)
        lower = (at >= to).astype(f32)
        first_prev = idc_ref[7:8]
        before = jnp.zeros((1, LANES), f32)
        kept[...] = jnp.zeros_like(kept)
        for block in range(blocks):
            r0, r1 = block * BLOCK, (block + 1) * BLOCK
            ids = idc_ref[8 + r0 : 8 + r1]
            prev = idc_ref[7 + r0 : 8 + r0]
            last = idc_ref[7 + r1 : 8 + r1]
            part_step = step[r0:r1]
            total = jnp.dot(lower, log_step[r0:r1], precision=highest, preferred_element_type=f32)
            end = total[BLOCK - 1 : BLOCK]
            acol_ref[r0:r1] = total
            arow_ref[:, r0:r1] = total.T
            ein_ref[r0:r1] = (jnp.exp(total) * (ids == prev).astype(f32)).astype(bf16)
            eall_ref[r0:r1] = (jnp.exp(total + before) * (ids == first_prev).astype(f32)).astype(
                bf16
            )
            stepc[r0:r1] = part_step.astype(bf16)
            wend[r0:r1] = (jnp.exp(end - total) * (ids == last).astype(f32) * part_step).astype(
                bf16
            )
            kept[block : block + 1] = jnp.exp(end) * (last == prev).astype(f32)
            before = before + end
        kept[blocks : blocks + 1] = jnp.exp(before) * (
            idc_ref[7 + rows : 8 + rows] == first_prev
        ).astype(f32)

    spread = spread_matrix(heads, width, step_at)
    kept_now = kept[...]
    high = kept_now.astype(bf16)
    low = (kept_now - high.astype(f32)).astype(bf16)
    keep_lanes = dot(high, spread) + dot(low, spread)
    step_lanes = dot(stepc[...], spread)
    wend_lanes = dot(wend[...], spread)
    for u in range(units):
        cols = slice(u * unit, (u + 1) * unit)
        fresh = dot(lhs[...], wx_ref[:, cols])
        raw[0:8, cols] = fresh[rows + HALO - 8 :]
        raw[8 : 8 + rows, cols] = fresh[:rows]
    at = lax.broadcasted_iota(jnp.int32, (KEEP_ROWS, unit), 0)
    for u in range(units):
        cols = slice(u * unit, (u + 1) * unit)
        running = None
        for block in range(blocks):
            r0, r1 = block * BLOCK, (block + 1) * BLOCK
            pieces = []
            for col in range(u * unit, (u + 1) * unit, LANES):
                x_now = conv_rows(
                    raw,
                    keep,
                    tapx_ref[:, col : col + LANES],
                    biasx_ref[:, col : col + LANES],
                    r0,
                    r1,
                    col,
                )
                x_ref[r0:r1, col : col + LANES] = x_now.astype(bf16)
                xs_ref[r0:r1, col : col + LANES] = (
                    x_now * step_lanes[r0:r1, col : col + LANES]
                ).astype(bf16)
                pieces.append((x_now * wend_lanes[r0:r1, col : col + LANES]).astype(bf16))
            local = lax.dot_general(
                bc_ref[r0:r1, 0:state_width],
                jnp.concatenate(pieces, 1),
                (((0,), (0,)), ((), ())),
                preferred_element_type=f32,
            )
            if running is not None:
                local = local + keep_lanes[block : block + 1, cols] * running
            running = local
            if block < blocks - 1:
                state_ref[block, :, cols] = running.astype(bf16)
        sent_ref[0:state_width, cols] = running.astype(bf16)
        shard_row = keep_lanes[blocks : blocks + 1, cols]
        shard_high = shard_row.astype(bf16).astype(f32)
        both = jnp.where(
            at == 0, shard_high, jnp.where(at == 1, shard_row - shard_high, 0.0)
        )
        sent_ref[state_width:, cols] = both.astype(bf16)


def scan_call(at, parts, halos, gain, small, w_zx, tapx, tapbc, biasx, biasbc, dtb, rate, idc, sizes):
    rows, heads, width, tiles, state_width = sizes
    shares, depth = len(parts), w_zx.shape[0]
    tile_lanes = heads * width
    channels = tiles * tile_lanes
    blocks = rows // BLOCK

    def whole(*shape):
        return pl.BlockSpec(shape, lambda i, at: (0,) * len(shape))

    def column(lead):
        return pl.BlockSpec((lead, tile_lanes), lambda i, at: (0, i))

    return pl.pallas_call(
        functools.partial(scan_kernel, rows, heads, width, shares),
        grid_spec=pltpu.PrefetchScalarGridSpec(
            num_scalar_prefetch=1,
            grid=(tiles,),
            in_specs=[whole(rows // shares, depth)] * shares
            + [whole(HALO, depth)] * shares
            + [
                whole(1, depth),
                whole(depth, 2 * state_width + LANES),
                pl.BlockSpec((depth, tile_lanes), lambda i, at: (0, tiles + i)),
                column(4),
                whole(4, 2 * state_width),
                column(1),
                whole(1, 2 * state_width),
                whole(1, LANES),
                whole(1, LANES),
                whole(rows + 8, LANES),
            ],
            out_specs=[
                whole(rows + HALO, depth),
                column(rows),
                column(rows),
                whole(rows, 2 * state_width),
                whole(rows, LANES),
                whole(LANES, rows),
                whole(rows, LANES),
                whole(rows, LANES),
                pl.BlockSpec(
                    (max(blocks - 1, 1), state_width, tile_lanes), lambda i, at: (0, 0, i)
                ),
                column(state_width + KEEP_ROWS),
            ],
            scratch_shapes=[
                pltpu.VMEM((rows + 8, max(tile_lanes, 2 * state_width)), f32),
                pltpu.VMEM((3, rows, LANES), f32),
                pltpu.VMEM((rows, LANES), bf16),
                pltpu.VMEM((rows, LANES), bf16),
                pltpu.VMEM((max(8, blocks + 1), LANES), f32),
            ],
        ),
        out_shape=[
            jax.ShapeDtypeStruct((rows + HALO, depth), bf16),
            jax.ShapeDtypeStruct((rows, channels), bf16),
            jax.ShapeDtypeStruct((rows, channels), bf16),
            jax.ShapeDtypeStruct((rows, 2 * state_width), bf16),
            jax.ShapeDtypeStruct((rows, LANES), f32),
            jax.ShapeDtypeStruct((LANES, rows), f32),
            jax.ShapeDtypeStruct((rows, LANES), bf16),
            jax.ShapeDtypeStruct((rows, LANES), bf16),
            jax.ShapeDtypeStruct((max(blocks - 1, 1), state_width, channels), bf16),
            jax.ShapeDtypeStruct((state_width + KEEP_ROWS, channels), bf16),
        ],
        compiler_params=pltpu.CompilerParams(
            dimension_semantics=("arbitrary",), vmem_limit_bytes=60 * 2**20
        ),
        cost_estimate=cost(15),
        name="scan",
    )(at, *parts, *halos, gain, small, w_zx, tapx, tapbc, biasx, biasbc, dtb, rate, idc)


def inner_kernel(
    rows,
    heads,
    width,
    x_ref,
    xs_ref,
    bc_ref,
    acol_ref,
    arow_ref,
    ein_ref,
    state_ref,
    skip_ref,
    idc_ref,
    idr_ref,
    y_ref,
    gram,
):
    blocks = rows // BLOCK
    state_width = bc_ref.shape[1] // 2

    @pl.when(pl.program_id(0) == 0)
    def _():
        at = lax.broadcasted_iota(jnp.int32, (BLOCK, BLOCK), 0)
        to = lax.broadcasted_iota(jnp.int32, (BLOCK, BLOCK), 1)
        for block in range(blocks):
            r0, r1 = block * BLOCK, (block + 1) * BLOCK
            b_rows = bc_ref[r0:r1, 0:state_width]
            c_rows = bc_ref[r0:r1, state_width:]
            ids = jnp.concatenate([idc_ref[8 + r0 : 8 + r1]] * (BLOCK // LANES), 1)
            same = (at >= to) & (ids == idr_ref[0:1, r0:r1])
            product = lax.dot_general(
                c_rows, b_rows, (((1,), (1,)), ((), ())), preferred_element_type=f32
            )
            gram[block] = jnp.where(same, product, 0.0)

    tile = pl.program_id(0)
    spread = spread_matrix(heads, width, tile)
    acol = pltpu.roll(acol_ref[...], lax.rem(LANES - tile * heads, LANES), 1)
    lane = lax.broadcasted_iota(jnp.int32, (BLOCK, LANES), 1)
    pack = LANES // width
    for block in range(blocks):
        r0, r1 = block * BLOCK, (block + 1) * BLOCK
        if block > 0:
            carried = dot(bc_ref[r0:r1, state_width:], state_ref[block - 1])
            carried = carried * dot(ein_ref[r0:r1], spread)
        for first in range(0, heads, pack):
            cols = slice(first * width, (first + pack) * width)
            xs_now = xs_ref[r0:r1, cols]
            total = None
            for inner in range(pack):
                head = first + inner
                gap = acol[r0:r1, head : head + 1] - arow_ref[head : head + 1, r0:r1]
                mix = (jnp.exp(jnp.minimum(gap, 0.0)) * gram[block]).astype(bf16)
                part = dot(mix, xs_now)
                total = part if total is None else jnp.where(lane < inner * width, total, part)
            total = total + skip_ref[:, cols] * x_ref[r0:r1, cols].astype(f32)
            if block > 0:
                total = total + carried[:, cols]
            y_ref[r0:r1, cols] = total.astype(bf16)


def inner_call(x, xs, bc, acol, arow, ein, states, skip, idc, idr, sizes):
    rows, heads, width, tiles, state_width = sizes
    tile_lanes = heads * width
    channels = tiles * tile_lanes
    blocks = rows // BLOCK

    def whole(*shape):
        return pl.BlockSpec(shape, lambda i: (0,) * len(shape))

    def column(lead):
        return pl.BlockSpec((lead, tile_lanes), lambda i: (0, i))

    arow_rows = heads if heads % 8 == 0 else LANES

    return pl.pallas_call(
        functools.partial(inner_kernel, rows, heads, width),
        grid=(tiles,),
        in_specs=[
            column(rows),
            column(rows),
            whole(rows, 2 * state_width),
            whole(rows, LANES),
            pl.BlockSpec((arow_rows, rows), lambda i: (i, 0)),
            whole(rows, LANES),
            pl.BlockSpec((max(blocks - 1, 1), state_width, tile_lanes), lambda i: (0, 0, i)),
            column(1),
            whole(rows + 8, LANES),
            whole(8, rows),
        ],
        out_specs=column(rows),
        out_shape=jax.ShapeDtypeStruct((rows, channels), bf16),
        scratch_shapes=[pltpu.VMEM((blocks, BLOCK, BLOCK), f32)],
        compiler_params=pltpu.CompilerParams(
            dimension_semantics=("arbitrary",), vmem_limit_bytes=60 * 2**20
        ),
        cost_estimate=cost(11),
        name="inner",
    )(x, xs, bc, acol, arow, ein, states, skip, idc, idr)


def gate_kernel(normed_ref, wz_ref, gate_ref):
    gate_ref[...] = silu(dot(normed_ref[...], wz_ref[...])).astype(bf16)


def gate_call(normed, w_zx, sizes):
    rows, heads, width, tiles, _ = sizes
    depth = normed.shape[1]
    tile_lanes = heads * width
    return pl.pallas_call(
        gate_kernel,
        grid=(tiles,),
        in_specs=[
            pl.BlockSpec((rows, depth), lambda i: (0, 0)),
            pl.BlockSpec((depth, tile_lanes), lambda i: (0, i)),
        ],
        out_specs=pl.BlockSpec((rows, tile_lanes), lambda i: (0, i)),
        out_shape=jax.ShapeDtypeStruct((rows, tiles * tile_lanes), bf16),
        compiler_params=pltpu.CompilerParams(
            dimension_semantics=("arbitrary",), vmem_limit_bytes=60 * 2**20
        ),
        cost_estimate=cost(8),
        name="gate",
    )(normed, w_zx)


def out_kernel(
    heads,
    width,
    tiles,
    at_ref,
    y_ref,
    gate_ref,
    bc_ref,
    eall_ref,
    stay_ref,
    got_ref,
    gain_ref,
    w_ref,
    p_ref,
    sq_ref,
    lhs,
    coming,
):
    state_width = bc_ref.shape[1] // 2
    tile_lanes = heads * width
    half = stay_ref.shape[1]

    @pl.when(pl.program_id(0) == 0)
    def _():
        swapped = at_ref[1] != 0
        coming[:, :half] = jnp.where(swapped, got_ref[...], stay_ref[...])
        coming[:, half:] = jnp.where(swapped, stay_ref[...], got_ref[...])
        squares = None
        for tile in range(tiles):
            cols = slice(tile * tile_lanes, (tile + 1) * tile_lanes)
            carried = dot(bc_ref[:, state_width:], coming[:, cols])
            carried = carried * dot(eall_ref[...], spread_matrix(heads, width, tile))
            gated = (y_ref[:, cols].astype(f32) + carried) * gate_ref[:, cols].astype(f32)
            part = jnp.sum(gated * gated, axis=1, keepdims=True)
            squares = part if squares is None else squares + part
            lhs[:, cols] = (gated * gain_ref[:, cols]).astype(bf16)
        sq_ref[...] = jnp.broadcast_to(squares, sq_ref.shape)

    p_ref[...] = dot(lhs[...], w_ref[...]).astype(bf16)


def out_call(at, y, gate, bc, eall, stay, got, gain, w_out, count, sizes):
    rows, heads, width, tiles, state_width = sizes
    channels, depth = w_out.shape
    piece = 512 if depth % 512 == 0 else depth

    def taken(lanes):
        return pl.BlockSpec((count, lanes), lambda i, at: (at[0], 0))

    def whole(*shape):
        return pl.BlockSpec(shape, lambda i, at: (0,) * len(shape))

    return pl.pallas_call(
        functools.partial(out_kernel, heads, width, tiles),
        grid_spec=pltpu.PrefetchScalarGridSpec(
            num_scalar_prefetch=1,
            grid=(depth // piece,),
            in_specs=[
                taken(channels),
                taken(channels),
                taken(2 * state_width),
                taken(LANES),
                whole(state_width, channels // 2),
                whole(state_width, channels // 2),
                whole(1, channels),
                pl.BlockSpec((channels, piece), lambda i, at: (0, i)),
            ],
            out_specs=[
                pl.BlockSpec((count, piece), lambda i, at: (0, i)),
                whole(count, LANES),
            ],
            scratch_shapes=[
                pltpu.VMEM((count, channels), bf16),
                pltpu.VMEM((state_width, channels), bf16),
            ],
        ),
        out_shape=[
            jax.ShapeDtypeStruct((count, depth), bf16),
            jax.ShapeDtypeStruct((count, LANES), f32),
        ],
        compiler_params=pltpu.CompilerParams(
            dimension_semantics=("arbitrary",), vmem_limit_bytes=60 * 2**20
        ),
        cost_estimate=cost(6),
        name="outp",
    )(at, y, gate, bc, eall, stay, got, gain, w_out)


class Route:
    def __init__(self, sizes):
        self.pipes, self.seqs, self.tps = sizes

    def spot(self, pipe, seq, tp):
        return (pipe * self.seqs + seq) * self.tps + tp

    def move(self, block, pairs):
        return lax.ppermute(
            block, AXES, [(self.spot(*source), self.spot(*target)) for source, target in pairs]
        )

    def every(self):
        return [(s, t) for s in range(self.seqs) for t in range(self.tps)]


def gather_rows(route, own, source_pipe, pipe, tail_after=None, ids_row=None):
    tps, seqs = route.tps, route.seqs
    parts = [own]
    if source_pipe != pipe:
        parts = [route.move(own, [((source_pipe, s, t), (pipe, s, t)) for s, t in route.every()])]
    for distance in range(1, tps):
        parts.append(
            route.move(
                own,
                [
                    ((source_pipe, s, (t + distance) % tps), (pipe, s, t))
                    for s, t in route.every()
                ],
            )
        )
    tail = own[own.shape[0] - HALO :]
    if ids_row is not None:
        tail = jnp.concatenate([tail, ids_row], 0)
    pipes = [(source_pipe, pipe)] if ids_row is None else [(p, p) for p in range(route.pipes)]
    halos = [
        route.move(
            tail,
            [((a, s, tps - 1), (b, s + 1, t)) for a, b in pipes for s in range(seqs - 1)],
        )
        for t in range(tps)
    ]
    return parts, halos


def exchange_states(route, sent, state_width, pipe, under_swap, under_scan, scan_inputs):
    seqs = route.seqs
    outer, side = seqs // 2, lax.axis_index("seq") % 2
    half = sent.shape[1] // 2
    is_first = side == 0

    def swap(block):
        return route.move(
            block, [((pipe, s, t), (pipe, s + 1 - 2 * (s % 2), t)) for s, t in route.every()]
        )

    def parted(block):
        block = block.astype(f32)
        keep = block[state_width : state_width + 1] + block[state_width + 1 : state_width + 2]
        return block[:state_width], keep

    def joined(state, keep):
        high = keep.astype(bf16)
        low = (keep - high.astype(f32)).astype(bf16)
        rest = jnp.zeros((KEEP_ROWS - 2, half), bf16)
        return jnp.concatenate([state.astype(bf16), high, low, rest], 0)

    low, high = sent[:, :half], sent[:, half:]
    mine = jnp.where(is_first, low, high)
    theirs = swap(jnp.where(is_first, high, low))
    theirs, gate = lax.optimization_barrier((theirs, under_swap()))
    early, keep_early = parted(jnp.where(is_first, mine, theirs))
    late, keep_late = parted(jnp.where(is_first, theirs, mine))
    pair = joined(keep_late * early + late, keep_early * keep_late)
    pair, scan_inputs = lax.optimization_barrier((pair, scan_inputs))
    arrivals = []
    for distance in range(1, outer):
        pairs = [
            ((pipe, s - 2 * distance, t), (pipe, s, t))
            for s, t in route.every()
            if s - 2 * distance >= 0
        ]
        arrivals.append(route.move(pair, pairs))
    arrivals, mixed = lax.optimization_barrier((arrivals, under_scan(*scan_inputs)))
    total, weight = parted(arrivals[0])
    for came in arrivals[1:]:
        came, keep_came = parted(came)
        total = total + weight * came
        weight = weight * keep_came
    after_early = keep_early * total + early
    stay = jnp.where(is_first, total, after_early).astype(bf16)
    got = swap(jnp.where(is_first, after_early, total).astype(bf16))
    return stay, got, gate, mixed


def local(
    hidden_in,
    doc_ids,
    norm_gain,
    in_zx,
    in_bc,
    in_dt,
    conv_x,
    conv_bc,
    bias_x,
    bias_bc,
    dt_bias,
    a_log,
    d_skip,
    gated_gain,
    out_w,
):
    route = Route(tuple(lax.axis_size(a) for a in AXES))
    section = lax.axis_index("pipe")
    tp = lax.axis_index("tp")
    micro_count = hidden_in.shape[0]
    channels = gated_gain.shape[1]
    local_heads = dt_bias.shape[1]
    width = channels // local_heads
    depth = in_zx.shape[1]
    rows = doc_ids.shape[1]
    own_rows = hidden_in.shape[1]
    state_width = in_bc.shape[2] // 2
    heads = 8 if local_heads % 8 == 0 else local_heads
    tiles = local_heads // heads
    sizes = (rows, heads, width, tiles, state_width)
    full_width = channels * route.tps

    def lanes(a):
        return jnp.pad(a, ((0, 0), (0, LANES - local_heads)))

    w_zx = in_zx[0].reshape(depth, 2 * channels)
    small = jnp.concatenate([in_bc[0], lanes(in_dt[0])], 1)
    dtb = lanes(dt_bias)
    rate = lanes(-jnp.exp(a_log))
    skip = jnp.repeat(d_skip, width, axis=1)
    every = route.every()
    outputs = []
    for micro in range(micro_count):
        ids = doc_ids[micro].astype(f32)
        ids_row = jnp.broadcast_to(
            jnp.pad(ids[rows - 8 :], (0, depth - 8)).astype(bf16)[None, :], (HALO, depth)
        )
        current = hidden_in[micro]
        source = 0
        result = jnp.zeros_like(current)
        for pipe in range(route.pipes):
            if source == pipe:
                parts, halos = gather_rows(route, current, source, pipe, None, ids_row)
                before = sum(h[HALO, :8].astype(f32) for h in halos)
                before = jnp.where(lax.axis_index("seq") == 0, -1.0, before)
                idc = jnp.broadcast_to(
                    jnp.concatenate([before, ids])[:, None], (rows + 8, LANES)
                )
                idr = jnp.broadcast_to(ids[None, :], (8, rows))
            else:
                parts, halos = gather_rows(route, current, source, pipe)
            residual = parts[0]
            at = ((tp + jnp.arange(route.tps, dtype=jnp.int32)) % route.tps) * own_rows
            normed, x, xs, bc, acol, arow, ein, eall, states, sent = scan_call(
                at,
                parts,
                halos,
                norm_gain,
                small,
                w_zx,
                conv_x[0],
                conv_bc[0],
                bias_x,
                bias_bc,
                dtb,
                rate,
                idc,
                sizes,
            )
            stay, got, gate, y = exchange_states(
                route,
                sent,
                state_width,
                pipe,
                lambda: gate_call(normed, w_zx, sizes),
                lambda *a: inner_call(*a, bc, acol, arow, ein, states, skip, idc, idr, sizes),
                (x, xs),
            )
            swapped = lax.axis_index("seq") % 2
            total = None
            squares = None
            for distance in range(1, route.tps):
                at = jnp.stack([(tp + distance) % route.tps, swapped]).astype(jnp.int32)
                part, sq = out_call(
                    at, y, gate, bc, eall, stay, got, gated_gain, out_w[0], own_rows, sizes
                )
                pairs = [
                    ((pipe, s, t), (pipe, s, (t + distance) % route.tps)) for s, t in every
                ]
                part = route.move(part, pairs).astype(f32)
                sq = route.move(sq, pairs)
                total = part if total is None else total + part
                squares = sq if squares is None else squares + sq
            part, sq = out_call(
                jnp.stack([tp, swapped]).astype(jnp.int32),
                y, gate, bc, eall, stay, got, gated_gain, out_w[0], own_rows, sizes
            )
            total = part.astype(f32) if total is None else total + part.astype(f32)
            squares = sq if squares is None else squares + sq
            scale = lax.rsqrt(squares[:, 0:1] / full_width + epsilon)
            current = (residual.astype(f32) + scale * total).astype(bf16)
            source = pipe
            result = jnp.where(section == pipe, current, result)
        outputs.append(result)
    return jnp.stack(outputs)[None]


def solution(mesh):
    placed = (
        P(None, ("seq", "tp"), None),
        P(None, "seq"),
        P("pipe", None),
        P("pipe", None, None, "tp"),
        P("pipe", None, None),
        P("pipe", None, "tp"),
        P("pipe", None, "tp"),
        P("pipe", None, None),
        P("pipe", "tp"),
        P("pipe", None),
        P("pipe", "tp"),
        P("pipe", "tp"),
        P("pipe", "tp"),
        P("pipe", "tp"),
        P("pipe", "tp", None),
    )
    return jax.shard_map(
        local,
        mesh=mesh,
        in_specs=placed,
        out_specs=P("pipe", None, ("seq", "tp"), None),
        check_vma=False,
    )
```

time: 739 us -> 276 us (0.37)
  waiting for transfers between devices: 340 us -> 55.3 us
  matrix products: 189 us -> 0 us
  Pallas kernels: 0 us -> 141 us
  blocking collectives: 45.8 us -> 0 us
  other arithmetic: 62 us -> 17.9 us
  local copies, waits for them, and re-layouts: 63.4 us -> 26.5 us
  starting transfers between devices: 12.2 us -> 33.5 us
  between operations: 18.1 us -> 0.54 us
    all_gather x4 -> x0, waiting for transfers between devices: 237 us -> none  [the longest x2 184 us: carried_in(): gathered = jax.tree.map(lambda a: lax.all_gather(a, axis), part)]
    dot_general x26 -> x0, matrix products: 189 us -> none  [the longest x4 54 us: block_step(): outputs = jnp.einsum('hps,hts->hpt', x_block, weights, precision=highest)]
    pallas_call x0 -> x10, Pallas kernels: none -> 141 us  [the longest x2 49.5 us: scan_call(): pl.pallas_call(functools.partial(scan_kernel, rows, heads, width, shares)...]
    reduce_scatter x2 -> x0, waiting for transfers between devices: 97.7 us -> none  [local(): lax.psum_scatter(jnp.dot(branch_in, weight_out, preferred_element_type=jn...]
    ppermute x4 -> x21, waiting for transfers between devices: 5.5 us -> 55.3 us  [move(): lax.ppermute(block, AXES, [(self.spot(*source), self.spot(*target)) for s...]
    unnamed x2 -> x0, blocking collectives: 38.3 us -> none
    mul x12 -> x1, other arithmetic: 28.1 us -> 0.59 us  [local(): at = (tp + jnp.arange(route.tps, dtype=jnp.int32)) % route.tps * own_rows]
    ppermute x4 -> x21, starting transfers between devices: 11.6 us -> 33.5 us  [move(): lax.ppermute(block, AXES, [(self.spot(*source), self.spot(*target)) for s...]
  transfers between devices with their start and end apart: 10 -> 21, of which waited for: 9 -> 4; matrix products, arithmetic and copies ran while one was open for 14% -> 11% of each run, Pallas kernels for 0% -> 25%
where the time goes in v1:
time: 276 us; the launch traced here: 275 us
  Pallas kernels  141 us (51%)
  waiting for transfers between devices  55.3 us (20%)
  starting transfers between devices  33.5 us (12%)
  local copies, waits for them, and re-layouts  26.5 us (10%)
  other arithmetic  17.9 us (6%)
    ppermute x21, waiting for transfers between devices, move(): lax.ppermute(block, AXES, [(self.spot(*source), self.spot(*target)) for s...  55.3 us
    pallas_call x2, Pallas kernels, scan_call(): pl.pallas_call(functools.partial(scan_kernel, rows, heads, width, shares)...  49.5 us
    pallas_call x4, Pallas kernels, out_call(): pl.pallas_call(functools.partial(out_kernel, heads, width, tiles), grid_s...  47.4 us
    ppermute x21, starting transfers between devices, move(): lax.ppermute(block, AXES, [(self.spot(*source), self.spot(*target)) for s...  33.5 us
    pallas_call x2, Pallas kernels, gate_call(): pl.pallas_call(gate_kernel, grid=(tiles,), in_specs=[pl.BlockSpec((rows,...  24.1 us
    unnamed x34, local copies, waits for them, and re-layouts  22.1 us
    pallas_call x2, Pallas kernels, inner_call(): pl.pallas_call(functools.partial(inner_kernel, rows, heads, width), grid=...  20 us
  transfers between devices with their start and end apart: 21, of which 4 were waited for; matrix products, arithmetic and copies ran while one was open for 11% of the time, Pallas kernels for 25%

profile of v1, /device:TPU:1, one launch (start us, length us, event | category | flops | bytes accessed | tf_op | source)
XLA Modules:
  0.0 274.7 jit_solution(10701773525725352053)
XLA Ops:
  3.9 1.3 collective-permute-start.2
  5.2 1.3 copy.17
  6.5 1.5 fusion.1.refs_5_
  8.1 18.0 %copy.18 = bf16[320,8,2,2560]{3,1,2,0:T(8,128)(2,1)} copy(bf16[320,8,2,2560]{3,2,1,0:T(2,128)(2,1)} %bitcast.31) | data formatting | bytes 52428800
  29.6 24.7 %scan.2 = (bf16[528,2560]{1,0:T(8,128)(2,1)}, bf16[512,2560]{1,0:T(8,128)(2,1)}, bf16[512,2560]{1,0:T(8,128)(2,1)}, bf16[512,256]{1,0:T(8,128)(2,1)}, f32[512,12...) custom-call(s32[2]{0:T(128)} %fusion.23.at_ref, ...), custom_call_target="tpu_custom_call" | custom-call | flops 3750000128 | tf_op jit(solution)/shard_map/scan/pallas_call | solution.py:221
  54.3 1.1 broadcast_select_fusion.3
  56.2 12.0 %gate.2.gate_ref = bf16[512,2560]{1,0:T(8,128)(2,1)} custom-call(bf16[528,2560]{1,0:T(8,128)(2,1)} %get-tuple-element.52.normed_ref, bf16[2560,5120]{1,0:T(8,128)(2,1)} %bitcast.24), custom_call_target="tpu_custom_call" | custom-call | flops 2000000000 | tf_op jit(solution)/shard_map/gate/pallas_call | solution.py:391
  72.1 10.0 %inner.2.y_ref = bf16[512,2560]{1,0:T(8,128)(2,1)} custom-call(bf16[512,2560]{1,0:T(8,128)(2,1)} %get-tuple-element.57.x_ref, bf16[512,2560]{1,0:T(8,128)(2,1)} %get-tuple-element.58.xs_ref, bf16[512,256]{1,0:T(8,128)(2,1)} %get-tuple-element.59.bc_ref, f32[512,128]{1,0:T(8,128)} %get-tuple-element.60.acol_ref, f32[128,512]{1,0:T(8,128)} %get-tuple-element.61.arow_ref, ...), custom_call_target="tpu_custom_call" | custom-call | flops 2750000128 | tf_op jit(solution)/shard_map/inner/pallas_call | solution.py:357
  85.5 11.9 %outp.4 = (bf16[256,2560]{1,0:T(8,128)(2,1)}, f32[256,128]{1,0:T(8,128)}) custom-call(s32[2]{0:T(128)} %pad_add_fusion.at_ref, bf16[512,2560]{1,0:T(8,128)(2,1)} %inner.2.y_ref, bf16[512,2560]{1,0:T(8,128)(2,1)} %gate.2.gate_ref, bf16[512,256]{1,0:T(8,128)(2,1)} %get-tuple-element.59.bc_ref, bf16[512,128]{1,0:T(8,128)(2,1)} %get-tuple-element.66.eall_ref, ...), custom_call_target="tpu_custom_call" | custom-call | flops 1500000000 | tf_op jit(solution)/shard_map/outp/pallas_call | solution.py:460
  99.6 11.8 %outp.5 = (bf16[256,2560]{1,0:T(8,128)(2,1)}, f32[256,128]{1,0:T(8,128)}) custom-call(s32[2]{0:T(128)} %pad_add_fusion.1.at_ref, bf16[512,2560]{1,0:T(8,128)(2,1)} %inner.2.y_ref, bf16[512,2560]{1,0:T(8,128)(2,1)} %gate.2.gate_ref, bf16[512,256]{1,0:T(8,128)(2,1)} %get-tuple-element.59.bc_ref, bf16[512,128]{1,0:T(8,128)(2,1)} %get-tuple-element.66.eall_ref, ...), custom_call_target="tpu_custom_call" | custom-call | flops 1500000000 | tf_op jit(solution)/shard_map/outp/pallas_call | solution.py:460
  112.5 1.9 add_convert_fusion.1
  114.5 1.3 collective-permute-start.10
  115.8 1.3 collective-permute-start.11
  118.5 31.2 %collective-permute-done.10.refs_0_ = bf16[256,2560]{1,0:T(8,128)(2,1)S(1)} collective-permute-done((bf16[256,2560]{1,0:T(8,128)(2,1)S(1)}, bf16[256,2560]{1,0:T(8,128)(2,1)S(1)}, u32[]{:S(2)}, u32[]{:S(2)}) %collective-permute-start.10) | collective-permute-done | bytes 1310752 | tf_op jit(solution)/shard_map/ppermute | solution.py:504
  149.7 15.8 %collective-permute-done.11.refs_1_ = bf16[256,2560]{1,0:T(8,128)(2,1)S(1)} collective-permute-done((bf16[256,2560]{1,0:T(8,128)(2,1)S(1)}, bf16[256,2560]{1,0:T(8,128)(2,1)S(1)}, u32[]{:S(2)}, u32[]{:S(2)}) %collective-permute-start.11) | collective-permute-done | bytes 1310752 | tf_op jit(solution)/shard_map/ppermute | solution.py:504
  165.5 1.1 copy-done.6
  166.6 24.7 %scan.3 = (bf16[528,2560]{1,0:T(8,128)(2,1)}, bf16[512,2560]{1,0:T(8,128)(2,1)}, bf16[512,2560]{1,0:T(8,128)(2,1)}, bf16[512,256]{1,0:T(8,128)(2,1)}, f32[512,12...) custom-call(s32[2]{0:T(128)} %fusion.23.at_ref, ...), custom_call_target="tpu_custom_call" | custom-call | flops 3750000128 | tf_op jit(solution)/shard_map/scan/pallas_call | solution.py:221
  191.3 1.1 broadcast_select_fusion.1
  192.5 3.3 %collective-permute-start.14 = (bf16[144,1280]{1,0:T(8,128)(2,1)S(1)}, bf16[144,1280]{1,0:T(8,128)(2,1)S(1)}, u32[]{:S(2)}, u32[]{:S(2)}) collective-permute-start(bf16[144,1280]{1,0:T(8,128)(2,1)S(1)} %broadcast_select_fusion.1), channel_id=1, source_target_pairs={{16,18},{17,19},{18,16},{19,17},{20,22},{21,23},{22,20},{23,21},{2... | collective-permute-start | bytes 1105928 | tf_op jit(solution)/shard_map/ppermute | solution.py:504
  195.8 12.0 %gate.3.gate_ref = bf16[512,2560]{1,0:T(8,128)(2,1)} custom-call(bf16[528,2560]{1,0:T(8,128)(2,1)} %get-tuple-element.75.normed_ref, bf16[2560,5120]{1,0:T(8,128)(2,1)} %bitcast.26), custom_call_target="tpu_custom_call" | custom-call | flops 2000000000 | tf_op jit(solution)/shard_map/gate/pallas_call | solution.py:391
  208.2 4.4 %collective-permute-start.15 = (bf16[144,1280]{1,0:T(8,128)(2,1)S(1)}, bf16[144,1280]{1,0:T(8,128)(2,1)S(1)}, u32[]{:S(2)}, u32[]{:S(2)}) collective-permute-start(bf16[144,1280]{1,0:T(8,128)(2,1)S(1)} %maximum_maximum_fusion.1), channel_id=1, source_target_pairs={{16,20},{17,21},{18,22},{19,23},{20,24},{21,25},{22,26},{23,27},{2... | collective-permute-start | bytes 1105928 | tf_op jit(solution)/shard_map/ppermute | solution.py:504
  212.6 5.0 %collective-permute-start.16 = (bf16[144,1280]{1,0:T(8,128)(2,1)S(1)}, bf16[144,1280]{1,0:T(8,128)(2,1)S(1)}, u32[]{:S(2)}, u32[]{:S(2)}) collective-permute-start(bf16[144,1280]{1,0:T(8,128)(2,1)S(1)} %maximum_maximum_fusion.1), channel_id=1, source_target_pairs={{16,24},{17,25},{18,26},{19,27},{20,28},{21,29},{22,30},{23,31}} | collective-permute-start | bytes 1105928 | tf_op jit(solution)/shard_map/ppermute | solution.py:504
  217.6 1.3 collective-permute-start.17
  218.9 10.0 %inner.3.y_ref = bf16[512,2560]{1,0:T(8,128)(2,1)} custom-call(bf16[512,2560]{1,0:T(8,128)(2,1)} %get-tuple-element.80.x_ref, bf16[512,2560]{1,0:T(8,128)(2,1)} %get-tuple-element.81.xs_ref, bf16[512,256]{1,0:T(8,128)(2,1)} %get-tuple-element.82.bc_ref, f32[512,128]{1,0:T(8,128)} %get-tuple-element.83.acol_ref, f32[128,512]{1,0:T(8,128)} %get-tuple-element.84.arow_ref, ...), custom_call_target="tpu_custom_call" | custom-call | flops 2750000128 | tf_op jit(solution)/shard_map/inner/pallas_call | solution.py:357
  230.2 2.2 collective-permute-start.18
  232.4 5.6 %collective-permute-done.18.got_ref = bf16[128,1280]{1,0:T(8,128)(2,1)S(1)} collective-permute-done((bf16[128,1280]{1,0:T(8,128)(2,1)S(1)}, bf16[128,1280]{1,0:T(8,128)(2,1)S(1)}, u32[]{:S(2)}, u32[]{:S(2)}) %collective-permute-start.18) | collective-permute-done | bytes 327712 | tf_op jit(solution)/shard_map/ppermute | solution.py:504
  238.7 11.8 %outp.6 = (bf16[256,2560]{1,0:T(8,128)(2,1)}, f32[256,128]{1,0:T(8,128)}) custom-call(s32[2]{0:T(128)} %pad_add_fusion.at_ref, bf16[512,2560]{1,0:T(8,128)(2,1)} %inner.3.y_ref, bf16[512,2560]{1,0:T(8,128)(2,1)} %gate.3.gate_ref, bf16[512,256]{1,0:T(8,128)(2,1)} %get-tuple-element.82.bc_ref, bf16[512,128]{1,0:T(8,128)(2,1)} %get-tuple-element.89.eall_ref, ...), custom_call_target="tpu_custom_call" | custom-call | flops 1500000000 | tf_op jit(solution)/shard_map/outp/pallas_call | solution.py:460
  250.5 1.9 collective-permute-start.20
  252.4 3.5 %collective-permute-start.19 = (f32[256,128]{1,0:T(8,128)}, f32[256,128]{1,0:T(8,128)S(1)}, u32[]{:S(2)}, u32[]{:S(2)}) collective-permute-start(f32[256,128]{1,0:T(8,128)} %get-tuple-element.93), channel_id=1, source_target_pairs={{16,17},{17,16},{18,19},{19,18},{20,21},{21,20},{22,23},{23,22},{2... | collective-permute-start | bytes 393224 | tf_op jit(solution)/shard_map/ppermute | solution.py:504
  255.9 11.8 %outp.7 = (bf16[256,2560]{1,0:T(8,128)(2,1)}, f32[256,128]{1,0:T(8,128)}) custom-call(s32[2]{0:T(128)} %pad_add_fusion.1.at_ref, bf16[512,2560]{1,0:T(8,128)(2,1)} %inner.3.y_ref, bf16[512,2560]{1,0:T(8,128)(2,1)} %gate.3.gate_ref, bf16[512,256]{1,0:T(8,128)(2,1)} %get-tuple-element.82.bc_ref, bf16[512,128]{1,0:T(8,128)(2,1)} %get-tuple-element.89.eall_ref, ...), custom_call_target="tpu_custom_call" | custom-call | flops 1500000000 | tf_op jit(solution)/shard_map/outp/pallas_call | solution.py:460
  267.7 2.7 collective-permute-done.19
  271.5 3.2 %fusion.3 = bf16[1,1,256,2560]{3,2,1,0:T(8,128)(2,1)} fusion(bf16[256,2560]{1,0:T(8,128)(2,1)} %get-tuple-element.96, bf16[256,2560]{1,0:T(8,128)(2,1)S(1)} %collective-permute-done.20, bf16[256,2560]{1,0:T(8,128)(2,1)S(1)} %copy-done.2, bf16[256,2560]{1,0:T(8,128)(2,1)S(1)} %add_convert_fusion.1, f32[256]{0:T(256)S(1)} %fusion.13, pred[]{:T(512)S(6)} %eq.26, ...), kind=kLoop, calls=%fused_computation.6 | loop fusion | flops 5898240 | bytes 6554626 | tf_op jit(solution)/shard_map/broadcast_in_dim;stack | solution.py:706
  (101 shorter events, 23.1 us)
Async XLA Ops:
  0.0 6.5 %copy-start.7 = (bf16[1,2560,256]{2,1,0:T(8,128)(2,1)S(1)}, bf16[1,2560,256]{2,1,0:T(8,128)(2,1)}, u32[]{:S(2)}) copy-start(bf16[1,2560,256]{2,1,0:T(8,128)(2,1)} %param.19) | copy-start | bytes 3932164
  0.0 28.4 %collective-permute-start = (bf16[256,2560]{1,0:T(8,128)(2,1)}, bf16[256,2560]{1,0:T(8,128)(2,1)S(1)}, u32[]{:S(2)}, u32[]{:S(2)}) collective-permute-start(bf16[256,2560]{1,0:T(8,128)(2,1)} %bitcast.32), channel_id=1, source_target_pairs={{1,0},{0,1},{3,2},{2,3},{5,4},{4,5},{7,6},{6,7},{9,8},{8,9},{11,10... | collective-permute-start | bytes 3932168 | tf_op jit(solution)/shard_map/ppermute | solution.py:504
  3.2 24.4 %collective-permute-start.1 = (bf16[32,2560]{1,0:T(8,128)(2,1)}, bf16[32,2560]{1,0:T(8,128)(2,1)S(1)}, u32[]{:S(2)}, u32[]{:S(2)}) collective-permute-start(bf16[32,2560]{1,0:T(8,128)(2,1)} %pad_maximum_fusion), channel_id=1, source_target_pairs={{1,2},{3,4},{5,6},{7,8},{9,10},{11,12},{13,14},{17,18},{19,20},{21... | collective-permute-start | bytes 491528 | tf_op jit(solution)/shard_map/ppermute | solution.py:504
  3.9 23.8 %collective-permute-start.2 = (bf16[32,2560]{1,0:T(8,128)(2,1)}, bf16[32,2560]{1,0:T(8,128)(2,1)}, u32[]{:S(2)}, u32[]{:S(2)}) collective-permute-start(bf16[32,2560]{1,0:T(8,128)(2,1)} %pad_maximum_fusion), channel_id=1, source_target_pairs={{1,3},{3,5},{5,7},{7,9},{9,11},{11,13},{13,15},{17,19},{19,21},{21... | collective-permute-start | bytes 491528 | tf_op jit(solution)/shard_map/ppermute | solution.py:504
  8.1 18.5 %copy-start.15 = (f32[1,40]{1,0:T(1,128)S(1)}, f32[1,40]{1,0:T(1,128)}, u32[]{:S(2)}) copy-start(f32[1,40]{1,0:T(1,128)} %param.25) | copy-start | bytes 484
  27.7 1.7 copy-start.10
  55.5 12.8 %collective-permute-start.3 = (bf16[144,1280]{1,0:T(8,128)(2,1)S(1)}, bf16[144,1280]{1,0:T(8,128)(2,1)S(1)}, u32[]{:S(2)}, u32[]{:S(2)}) collective-permute-start(bf16[144,1280]{1,0:T(8,128)(2,1)S(1)} %broadcast_select_fusion.3), channel_id=1, source_target_pairs={{0,2},{1,3},{2,0},{3,1},{4,6},{5,7},{6,4},{7,5},{8,10},{9,11},{10,... | collective-permute-start | bytes 1105928 | tf_op jit(solution)/shard_map/ppermute | solution.py:504
  56.2 12.0 %copy-start.3 = (bf16[144,2560]{1,0:T(8,128)(2,1)S(1)}, bf16[144,2560]{1,0:T(8,128)(2,1)}, u32[]{:S(2)}) copy-start(bf16[144,2560]{1,0:T(8,128)(2,1)} %get-tuple-element.51) | copy-start | bytes 2211844
  68.3 2.5 copy-start.13
  68.7 13.4 %collective-permute-start.4 = (bf16[144,1280]{1,0:T(8,128)(2,1)S(1)}, bf16[144,1280]{1,0:T(8,128)(2,1)S(1)}, u32[]{:S(2)}, u32[]{:S(2)}) collective-permute-start(bf16[144,1280]{1,0:T(8,128)(2,1)S(1)} %maximum_maximum_fusion), channel_id=1, source_target_pairs={{0,4},{1,5},{2,6},{3,7},{4,8},{5,9},{6,10},{7,11},{8,12},{9,13},{1... | collective-permute-start | bytes 1105928 | tf_op jit(solution)/shard_map/ppermute | solution.py:504
  69.4 12.8 %collective-permute-start.5 = (bf16[144,1280]{1,0:T(8,128)(2,1)S(1)}, bf16[144,1280]{1,0:T(8,128)(2,1)S(1)}, u32[]{:S(2)}, u32[]{:S(2)}) collective-permute-start(bf16[144,1280]{1,0:T(8,128)(2,1)S(1)} %maximum_maximum_fusion), channel_id=1, source_target_pairs={{0,8},{1,9},{2,10},{3,11},{4,12},{5,13},{6,14},{7,15}} | collective-permute-start | bytes 1105928 | tf_op jit(solution)/shard_map/ppermute | solution.py:504
  70.1 12.1 %collective-permute-start.6 = (bf16[144,1280]{1,0:T(8,128)(2,1)S(1)}, bf16[144,1280]{1,0:T(8,128)(2,1)S(1)}, u32[]{:S(2)}, u32[]{:S(2)}) collective-permute-start(bf16[144,1280]{1,0:T(8,128)(2,1)S(1)} %maximum_maximum_fusion), channel_id=1, source_target_pairs={{0,12},{1,13},{2,14},{3,15}} | collective-permute-start | bytes 1105928 | tf_op jit(solution)/shard_map/ppermute | solution.py:504
  83.3 1.5 collective-permute-start.7
  97.5 15.1 %collective-permute-start.9 = (bf16[256,2560]{1,0:T(8,128)(2,1)}, bf16[256,2560]{1,0:T(8,128)(2,1)S(1)}, u32[]{:S(2)}, u32[]{:S(2)}) collective-permute-start(bf16[256,2560]{1,0:T(8,128)(2,1)} %get-tuple-element.72), channel_id=1, source_target_pairs={{0,1},{1,0},{2,3},{3,2},{4,5},{5,4},{6,7},{7,6},{8,9},{9,8},{10,11... | collective-permute-start | bytes 3932168 | tf_op jit(solution)/shard_map/ppermute | solution.py:504
  98.8 13.7 %copy-start = (bf16[1,256,2560]{2,1,0:T(8,128)(2,1)S(1)}, bf16[1,256,2560]{2,1,0:T(8,128)(2,1)}, u32[]{:S(2)}) copy-start(bf16[1,256,2560]{2,1,0:T(8,128)(2,1)} %param.15) | copy-start | bytes 3932164
  98.8 12.6 %collective-permute-start.8 = (f32[256,128]{1,0:T(8,128)}, f32[256,128]{1,0:T(8,128)S(1)}, u32[]{:S(2)}, u32[]{:S(2)}) collective-permute-start(f32[256,128]{1,0:T(8,128)} %get-tuple-element.70), channel_id=1, source_target_pairs={{0,1},{1,0},{2,3},{3,2},{4,5},{5,4},{6,7},{7,6},{8,9},{9,8},{10,11... | collective-permute-start | bytes 393224 | tf_op jit(solution)/shard_map/ppermute | solution.py:504
  114.5 35.2 %collective-permute-start.10 = (bf16[256,2560]{1,0:T(8,128)(2,1)S(1)}, bf16[256,2560]{1,0:T(8,128)(2,1)S(1)}, u32[]{:S(2)}, u32[]{:S(2)}) collective-permute-start(bf16[256,2560]{1,0:T(8,128)(2,1)S(1)} %add_convert_fusion.1), channel_id=1, source_target_pairs={{0,16},{1,17},{2,18},{3,19},{4,20},{5,21},{6,22},{7,23},{8,24},{9,... | collective-permute-start | bytes 3932168 | tf_op jit(solution)/shard_map/ppermute | solution.py:504
  115.8 49.7 %collective-permute-start.11 = (bf16[256,2560]{1,0:T(8,128)(2,1)S(1)}, bf16[256,2560]{1,0:T(8,128)(2,1)S(1)}, u32[]{:S(2)}, u32[]{:S(2)}) collective-permute-start(bf16[256,2560]{1,0:T(8,128)(2,1)S(1)} %add_convert_fusion.1), channel_id=1, source_target_pairs={{1,16},{0,17},{3,18},{2,19},{5,20},{4,21},{7,22},{6,23},{9,24},{8,... | collective-permute-start | bytes 3932168 | tf_op jit(solution)/shard_map/ppermute | solution.py:504
  117.1 1.4 collective-permute-start.12
  117.7 0.7 collective-permute-start.13
  118.4 47.0 %copy-start.11 = (bf16[16,2560]{1,0:T(8,128)(2,1)}, bf16[16,2560]{1,0:T(8,128)(2,1)S(1)}, u32[]{:S(2)}) copy-start(bf16[16,2560]{1,0:T(8,128)(2,1)S(1)} %collective-permute-done.12.refs_2_) | copy-start | bytes 245764
  118.4 47.0 %copy-start.12 = (bf16[16,2560]{1,0:T(8,128)(2,1)}, bf16[16,2560]{1,0:T(8,128)(2,1)S(1)}, u32[]{:S(2)}) copy-start(bf16[16,2560]{1,0:T(8,128)(2,1)S(1)} %collective-permute-done.13.refs_3_) | copy-start | bytes 245764
  149.7 15.8 %copy-start.1 = (bf16[256,2560]{1,0:T(8,128)(2,1)}, bf16[256,2560]{1,0:T(8,128)(2,1)S(1)}, u32[]{:S(2)}) copy-start(bf16[256,2560]{1,0:T(8,128)(2,1)S(1)} %collective-permute-done.10.refs_0_) | copy-start | bytes 3932164
  192.5 15.4 %collective-permute-start.14 = (bf16[144,1280]{1,0:T(8,128)(2,1)S(1)}, bf16[144,1280]{1,0:T(8,128)(2,1)S(1)}, u32[]{:S(2)}, u32[]{:S(2)}) collective-permute-start(bf16[144,1280]{1,0:T(8,128)(2,1)S(1)} %broadcast_select_fusion.1), channel_id=1, source_target_pairs={{16,18},{17,19},{18,16},{19,17},{20,22},{21,23},{22,20},{23,21},{2... | collective-permute-start | bytes 1105928 | tf_op jit(solution)/shard_map/ppermute | solution.py:504
  195.8 12.1 %copy-start.4 = (bf16[144,2560]{1,0:T(8,128)(2,1)S(1)}, bf16[144,2560]{1,0:T(8,128)(2,1)}, u32[]{:S(2)}) copy-start(bf16[144,2560]{1,0:T(8,128)(2,1)} %get-tuple-element.74) | copy-start | bytes 2211844
  208.2 20.7 %collective-permute-start.15 = (bf16[144,1280]{1,0:T(8,128)(2,1)S(1)}, bf16[144,1280]{1,0:T(8,128)(2,1)S(1)}, u32[]{:S(2)}, u32[]{:S(2)}) collective-permute-start(bf16[144,1280]{1,0:T(8,128)(2,1)S(1)} %maximum_maximum_fusion.1), channel_id=1, source_target_pairs={{16,20},{17,21},{18,22},{19,23},{20,24},{21,25},{22,26},{23,27},{2... | collective-permute-start | bytes 1105928 | tf_op jit(solution)/shard_map/ppermute | solution.py:504
  212.6 16.4 %collective-permute-start.16 = (bf16[144,1280]{1,0:T(8,128)(2,1)S(1)}, bf16[144,1280]{1,0:T(8,128)(2,1)S(1)}, u32[]{:S(2)}, u32[]{:S(2)}) collective-permute-start(bf16[144,1280]{1,0:T(8,128)(2,1)S(1)} %maximum_maximum_fusion.1), channel_id=1, source_target_pairs={{16,24},{17,25},{18,26},{19,27},{20,28},{21,29},{22,30},{23,31}} | collective-permute-start | bytes 1105928 | tf_op jit(solution)/shard_map/ppermute | solution.py:504
  217.6 11.4 %collective-permute-start.17 = (bf16[144,1280]{1,0:T(8,128)(2,1)S(1)}, bf16[144,1280]{1,0:T(8,128)(2,1)S(1)}, u32[]{:S(2)}, u32[]{:S(2)}) collective-permute-start(bf16[144,1280]{1,0:T(8,128)(2,1)S(1)} %maximum_maximum_fusion.1), channel_id=1, source_target_pairs={{16,28},{17,29},{18,30},{19,31}} | collective-permute-start | bytes 1105928 | tf_op jit(solution)/shard_map/ppermute | solution.py:504
  230.2 7.8 %collective-permute-start.18 = (bf16[128,1280]{1,0:T(8,128)(2,1)S(1)}, bf16[128,1280]{1,0:T(8,128)(2,1)S(1)}, u32[]{:S(2)}, u32[]{:S(2)}) collective-permute-start(bf16[128,1280]{1,0:T(8,128)(2,1)S(1)} %get-tuple-element.109), channel_id=1, source_target_pairs={{16,18},{17,19},{18,16},{19,17},{20,22},{21,23},{22,20},{23,21},{2... | collective-permute-start | bytes 983048 | tf_op jit(solution)/shard_map/ppermute | solution.py:504
  250.5 21.0 %collective-permute-start.20 = (bf16[256,2560]{1,0:T(8,128)(2,1)}, bf16[256,2560]{1,0:T(8,128)(2,1)S(1)}, u32[]{:S(2)}, u32[]{:S(2)}) collective-permute-start(bf16[256,2560]{1,0:T(8,128)(2,1)} %get-tuple-element.95), channel_id=1, source_target_pairs={{16,17},{17,16},{18,19},{19,18},{20,21},{21,20},{22,23},{23,22},{2... | collective-permute-start | bytes 3932168 | tf_op jit(solution)/shard_map/ppermute | solution.py:504
  252.4 19.1 %copy-start.2 = (bf16[256,2560]{1,0:T(8,128)(2,1)S(1)}, bf16[256,2560]{1,0:T(8,128)(2,1)}, u32[]{:S(2)}) copy-start(bf16[256,2560]{1,0:T(8,128)(2,1)} %copy-done.1) | copy-start | bytes 3932164
  252.4 18.0 %collective-permute-start.19 = (f32[256,128]{1,0:T(8,128)}, f32[256,128]{1,0:T(8,128)S(1)}, u32[]{:S(2)}, u32[]{:S(2)}) collective-permute-start(f32[256,128]{1,0:T(8,128)} %get-tuple-element.93), channel_id=1, source_target_pairs={{16,17},{17,16},{18,19},{19,18},{20,21},{21,20},{22,23},{23,22},{2... | collective-permute-start | bytes 393224 | tf_op jit(solution)/shard_map/ppermute | solution.py:504
  (5 other events, 5.3 us)

commit v2 on v1

--- a/solution.py
+++ b/solution.py
@@ -11,6 +11,7 @@
 BLOCK = 256
 HALO = 16
 KEEP_ROWS = 16
+CUTS = 4
 LANES = 128
 epsilon = 1e-05
 highest = lax.Precision.HIGHEST
@@ -40,6 +41,20 @@
     cols = lax.broadcasted_iota(jnp.int32, (LANES, heads * width), 1)
     inside = (cols >= rows * width) & (cols < (rows + 1) * width)
     return jnp.where(inside, 1.0, 0.0).astype(bf16)
+
+
+def weight_copies(source, held, sems, tile, first):
+    depth, lanes = held.shape[1:]
+    cut = depth // CUTS
+    col = pl.multiple_of((first + tile) * lanes, LANES)
+    return [
+        pltpu.make_async_copy(
+            source.at[pl.ds(k * cut, cut), pl.ds(col, lanes)],
+            held.at[tile, pl.ds(k * cut, cut)],
+            sems.at[tile, k],
+        )
+        for k in range(CUTS)
+    ]
 
 
 def conv_rows(raw_ref, keep_ref, taps, bias, start, stop, col):
@@ -64,7 +79,7 @@
         dtb_ref,
         rate_ref,
         idc_ref,
-        lhs,
+        normed_ref,
         x_ref,
         xs_ref,
         bc_ref,
@@ -79,7 +94,12 @@
         stepc,
         wend,
         kept,
+        lhs,
+        held,
+        sems,
+        out_sem,
     ) = refs[2 * shares :]
+    tiles = held.shape[0]
     step_at = pl.program_id(0)
     blocks = rows // BLOCK
     state_width = bc_ref.shape[1] // 2
@@ -87,8 +107,13 @@
     unit = 256 if tile_lanes % 256 == 0 else LANES
     units = tile_lanes // unit
 
+    saved = pltpu.make_async_copy(lhs, normed_ref, out_sem)
+
     @pl.when(step_at == 0)
     def _():
+        for tile in range(tiles):
+            for copy in weight_copies(wx_ref, held, sems, tile, tiles):
+                copy.start()
         gain = gain_ref[...]
 
         def normalize(part):
@@ -104,6 +129,7 @@
         for other in halo_refs[1:]:
             halo = halo + other[...].astype(f32)
         lhs[rows:] = normalize(halo)
+        saved.start()
         small = dot(lhs[...], small_ref[...])
         for tap in range(3):
             keep[tap] = (idc_ref[5 + tap : 5 + tap + rows] == idc_ref[8 : 8 + rows]).astype(f32)
@@ -158,9 +184,11 @@
     keep_lanes = dot(high, spread) + dot(low, spread)
     step_lanes = dot(stepc[...], spread)
     wend_lanes = dot(wend[...], spread)
+    for copy in weight_copies(wx_ref, held, sems, step_at, tiles):
+        copy.wait()
     for u in range(units):
         cols = slice(u * unit, (u + 1) * unit)
-        fresh = dot(lhs[...], wx_ref[:, cols])
+        fresh = dot(lhs[...], held[step_at, :, cols])
         raw[0:8, cols] = fresh[rows + HALO - 8 :]
         raw[8 : 8 + rows, cols] = fresh[:rows]
     at = lax.broadcasted_iota(jnp.int32, (KEEP_ROWS, unit), 0)
@@ -204,6 +232,10 @@
         )
         sent_ref[state_width:, cols] = both.astype(bf16)
 
+    @pl.when(step_at == tiles - 1)
+    def _():
+        saved.wait()
+
 
 def scan_call(at, parts, halos, gain, small, w_zx, tapx, tapbc, biasx, biasbc, dtb, rate, idc, sizes):
     rows, heads, width, tiles, state_width = sizes
@@ -228,7 +260,7 @@
             + [
                 whole(1, depth),
                 whole(depth, 2 * state_width + LANES),
-                pl.BlockSpec((depth, tile_lanes), lambda i, at: (0, tiles + i)),
+                pl.BlockSpec(memory_space=pltpu.HBM),
                 column(4),
                 whole(4, 2 * state_width),
                 column(1),
@@ -238,7 +270,7 @@
                 whole(rows + 8, LANES),
             ],
             out_specs=[
-                whole(rows + HALO, depth),
+                pl.BlockSpec(memory_space=pltpu.HBM),
                 column(rows),
                 column(rows),
                 whole(rows, 2 * state_width),
@@ -257,6 +289,10 @@
                 pltpu.VMEM((rows, LANES), bf16),
                 pltpu.VMEM((rows, LANES), bf16),
                 pltpu.VMEM((max(8, blocks + 1), LANES), f32),
+                pltpu.VMEM((rows + HALO, depth), bf16),
+                pltpu.VMEM((tiles, depth, tile_lanes), bf16),
+                pltpu.SemaphoreType.DMA((tiles, CUTS)),
+                pltpu.SemaphoreType.DMA,
             ],
         ),
         out_shape=[
@@ -380,8 +416,30 @@
     )(x, xs, bc, acol, arow, ein, states, skip, idc, idr)
 
 
-def gate_kernel(normed_ref, wz_ref, gate_ref):
-    gate_ref[...] = silu(dot(normed_ref[...], wz_ref[...])).astype(bf16)
+def gate_kernel(normed_ref, wz_ref, gate_ref, lhs, held, sems, row_sems):
+    tile = pl.program_id(0)
+    rows = lhs.shape[0]
+    cut = rows // CUTS
+    loads = [
+        pltpu.make_async_copy(
+            normed_ref.at[pl.ds(k * cut, cut)], lhs.at[pl.ds(k * cut, cut)], row_sems.at[k]
+        )
+        for k in range(CUTS)
+    ]
+
+    @pl.when(tile == 0)
+    def _():
+        for copy in loads:
+            copy.start()
+        for other in range(held.shape[0]):
+            for copy in weight_copies(wz_ref, held, sems, other, 0):
+                copy.start()
+        for copy in loads:
+            copy.wait()
+
+    for copy in weight_copies(wz_ref, held, sems, tile, 0):
+        copy.wait()
+    gate_ref[...] = silu(dot(lhs[...], held[tile])).astype(bf16)
 
 
 def gate_call(normed, w_zx, sizes):
@@ -391,11 +449,14 @@
     return pl.pallas_call(
         gate_kernel,
         grid=(tiles,),
-        in_specs=[
-            pl.BlockSpec((rows, depth), lambda i: (0, 0)),
-            pl.BlockSpec((depth, tile_lanes), lambda i: (0, i)),
+        in_specs=[pl.BlockSpec(memory_space=pltpu.HBM)] * 2,
+        out_specs=pl.BlockSpec((rows, tile_lanes), lambda i: (0, i)),
+        scratch_shapes=[
+            pltpu.VMEM((rows, depth), bf16),
+            pltpu.VMEM((tiles, depth, tile_lanes), bf16),
+            pltpu.SemaphoreType.DMA((tiles, CUTS)),
+            pltpu.SemaphoreType.DMA((CUTS,)),
         ],
-        out_specs=pl.BlockSpec((rows, tile_lanes), lambda i: (0, i)),
         out_shape=jax.ShapeDtypeStruct((rows, tiles * tile_lanes), bf16),
         compiler_params=pltpu.CompilerParams(
             dimension_semantics=("arbitrary",), vmem_limit_bytes=60 * 2**20
@@ -422,13 +483,32 @@
     sq_ref,
     lhs,
     coming,
+    y_held,
+    gate_held,
+    held,
+    sems,
+    row_sems,
 ):
     state_width = bc_ref.shape[1] // 2
     tile_lanes = heads * width
     half = stay_ref.shape[1]
-
-    @pl.when(pl.program_id(0) == 0)
+    piece = pl.program_id(0)
+    count = lhs.shape[0]
+    mine = pl.ds(pl.multiple_of(at_ref[0] * count, count), count)
+    loads = [
+        pltpu.make_async_copy(y_ref.at[mine], y_held, row_sems.at[0]),
+        pltpu.make_async_copy(gate_ref.at[mine], gate_held, row_sems.at[1]),
+    ]
+
+    @pl.when(piece == 0)
     def _():
+        for copy in loads:
+            copy.start()
+        for other in range(held.shape[0]):
+            for copy in weight_copies(w_ref, held, sems, other, 0):
+                copy.start()
+        for copy in loads:
+            copy.wait()
         swapped = at_ref[1] != 0
         coming[:, :half] = jnp.where(swapped, got_ref[...], stay_ref[...])
         coming[:, half:] = jnp.where(swapped, stay_ref[...], got_ref[...])
@@ -437,13 +517,15 @@
             cols = slice(tile * tile_lanes, (tile + 1) * tile_lanes)
             carried = dot(bc_ref[:, state_width:], coming[:, cols])
             carried = carried * dot(eall_ref[...], spread_matrix(heads, width, tile))
-            gated = (y_ref[:, cols].astype(f32) + carried) * gate_ref[:, cols].astype(f32)
+            gated = (y_held[:, cols].astype(f32) + carried) * gate_held[:, cols].astype(f32)
             part = jnp.sum(gated * gated, axis=1, keepdims=True)
             squares = part if squares is None else squares + part
             lhs[:, cols] = (gated * gain_ref[:, cols]).astype(bf16)
         sq_ref[...] = jnp.broadcast_to(squares, sq_ref.shape)
 
-    p_ref[...] = dot(lhs[...], w_ref[...]).astype(bf16)
+    for copy in weight_copies(w_ref, held, sems, piece, 0):
+        copy.wait()
+    p_ref[...] = dot(lhs[...], held[piece]).astype(bf16)
 
 
 def out_call(at, y, gate, bc, eall, stay, got, gain, w_out, count, sizes):
@@ -463,14 +545,14 @@
             num_scalar_prefetch=1,
             grid=(depth // piece,),
             in_specs=[
-                taken(channels),
-                taken(channels),
+                pl.BlockSpec(memory_space=pltpu.HBM),
+                pl.BlockSpec(memory_space=pltpu.HBM),
                 taken(2 * state_width),
                 taken(LANES),
                 whole(state_width, channels // 2),
                 whole(state_width, channels // 2),
                 whole(1, channels),
-                pl.BlockSpec((channels, piece), lambda i, at: (0, i)),
+                pl.BlockSpec(memory_space=pltpu.HBM),
             ],
             out_specs=[
                 pl.BlockSpec((count, piece), lambda i, at: (0, i)),
@@ -479,6 +561,11 @@
             scratch_shapes=[
                 pltpu.VMEM((count, channels), bf16),
                 pltpu.VMEM((state_width, channels), bf16),
+                pltpu.VMEM((count, channels), bf16),
+                pltpu.VMEM((count, channels), bf16),
+                pltpu.VMEM((depth // piece, channels, piece), bf16),
+                pltpu.SemaphoreType.DMA((depth // piece, CUTS)),
+                pltpu.SemaphoreType.DMA((2,)),
             ],
         ),
         out_shape=[

time: 276 us -> 284 us (1.029)
  Pallas kernels: 141 us -> 154 us
  waiting for transfers between devices: 55.3 us -> 50.7 us
    pallas_call x4, Pallas kernels: 47.4 us -> 55.9 us  [out_call(): pl.pallas_call(functools.partial(out_kernel, heads, width, tiles), grid_s...]
    pallas_call x2, Pallas kernels: 24.1 us -> 29 us  [gate_call(): pl.pallas_call(gate_kernel, grid=(tiles,), in_specs=[pl.BlockSpec(memory_...]
    ppermute x21, waiting for transfers between devices: 55.3 us -> 50.7 us  [move(): lax.ppermute(block, AXES, [(self.spot(*source), self.spot(*target)) for s...]
  transfers between devices with their start and end apart: 21 -> 21, of which waited for: 4 -> 4; matrix products, arithmetic and copies ran while one was open for 11% -> 11% of each run, Pallas kernels for 25% -> 27%
where the time goes in v2:
time: 284 us; the launch traced here: 283 us
  Pallas kernels  154 us (54%)
  waiting for transfers between devices  50.7 us (18%)
  starting transfers between devices  33.6 us (12%)
  local copies, waits for them, and re-layouts  26.5 us (9%)
  other arithmetic  17.9 us (6%)
    pallas_call x4, Pallas kernels, out_call(): pl.pallas_call(functools.partial(out_kernel, heads, width, tiles), grid_s...  55.9 us
    ppermute x21, waiting for transfers between devices, move(): lax.ppermute(block, AXES, [(self.spot(*source), self.spot(*target)) for s...  50.7 us
    pallas_call x2, Pallas kernels, scan_call(): pl.pallas_call(functools.partial(scan_kernel, rows, heads, width, shares)...  49.1 us
    ppermute x21, starting transfers between devices, move(): lax.ppermute(block, AXES, [(self.spot(*source), self.spot(*target)) for s...  33.6 us
    pallas_call x2, Pallas kernels, gate_call(): pl.pallas_call(gate_kernel, grid=(tiles,), in_specs=[pl.BlockSpec(memory_...  29 us
    unnamed x34, local copies, waits for them, and re-layouts  22.1 us
    pallas_call x2, Pallas kernels, inner_call(): pl.pallas_call(functools.partial(inner_kernel, rows, heads, width), grid=...  20 us
  transfers between devices with their start and end apart: 21, of which 4 were waited for; matrix products, arithmetic and copies ran while one was open for 11% of the time, Pallas kernels for 27%

profile of v2, /device:TPU:1, one launch (start us, length us, event | category | flops | bytes accessed | tf_op | source)
XLA Modules:
  0.0 283.4 jit_solution(15142084243354046742)
XLA Ops:
  3.9 1.3 collective-permute-start.2
  5.2 1.3 copy.17
  6.5 1.5 fusion.1.refs_5_
  8.1 18.0 %copy.18 = bf16[320,8,2,2560]{3,1,2,0:T(8,128)(2,1)} copy(bf16[320,8,2,2560]{3,2,1,0:T(2,128)(2,1)} %bitcast.31) | data formatting | bytes 52428800
  29.6 24.5 %scan.2 = (bf16[528,2560]{1,0:T(8,128)(2,1)}, bf16[512,2560]{1,0:T(8,128)(2,1)}, bf16[512,2560]{1,0:T(8,128)(2,1)}, bf16[512,256]{1,0:T(8,128)(2,1)}, f32[512,12...) custom-call(s32[2]{0:T(128)} %fusion.23.at_ref, ...), custom_call_target="tpu_custom_call" | custom-call | flops 3750000128 | tf_op jit(solution)/shard_map/scan/pallas_call | solution.py:253
  54.1 1.1 broadcast_select_fusion.3
  56.1 14.5 %gate.2.gate_ref = bf16[512,2560]{1,0:T(8,128)(2,1)} custom-call(bf16[528,2560]{1,0:T(8,128)(2,1)} %get-tuple-element.52.normed_ref, bf16[2560,5120]{1,0:T(8,128)(2,1)} %bitcast.24), custom_call_target="tpu_custom_call" | custom-call | flops 2000000000 | tf_op jit(solution)/shard_map/gate/pallas_call | solution.py:449
  74.6 10.0 %inner.2.y_ref = bf16[512,2560]{1,0:T(8,128)(2,1)} custom-call(bf16[512,2560]{1,0:T(8,128)(2,1)} %get-tuple-element.57.x_ref, bf16[512,2560]{1,0:T(8,128)(2,1)} %get-tuple-element.58.xs_ref, bf16[512,256]{1,0:T(8,128)(2,1)} %get-tuple-element.59.bc_ref, f32[512,128]{1,0:T(8,128)} %get-tuple-element.60.acol_ref, f32[128,512]{1,0:T(8,128)} %get-tuple-element.61.arow_ref, ...), custom_call_target="tpu_custom_call" | custom-call | flops 2750000128 | tf_op jit(solution)/shard_map/inner/pallas_call | solution.py:393
  87.9 14.0 %outp.4 = (bf16[256,2560]{1,0:T(8,128)(2,1)}, f32[256,128]{1,0:T(8,128)}) custom-call(s32[2]{0:T(128)} %pad_add_fusion.at_ref, bf16[512,2560]{1,0:T(8,128)(2,1)} %inner.2.y_ref, bf16[512,2560]{1,0:T(8,128)(2,1)} %gate.2.gate_ref, bf16[512,256]{1,0:T(8,128)(2,1)} %get-tuple-element.59.bc_ref, bf16[512,128]{1,0:T(8,128)(2,1)} %get-tuple-element.66.eall_ref, ...), custom_call_target="tpu_custom_call" | custom-call | flops 1500000000 | tf_op jit(solution)/shard_map/outp/pallas_call | solution.py:542
  104.1 13.9 %outp.5 = (bf16[256,2560]{1,0:T(8,128)(2,1)}, f32[256,128]{1,0:T(8,128)}) custom-call(s32[2]{0:T(128)} %pad_add_fusion.1.at_ref, bf16[512,2560]{1,0:T(8,128)(2,1)} %inner.2.y_ref, bf16[512,2560]{1,0:T(8,128)(2,1)} %gate.2.gate_ref, bf16[512,256]{1,0:T(8,128)(2,1)} %get-tuple-element.59.bc_ref, bf16[512,128]{1,0:T(8,128)(2,1)} %get-tuple-element.66.eall_ref, ...), custom_call_target="tpu_custom_call" | custom-call | flops 1500000000 | tf_op jit(solution)/shard_map/outp/pallas_call | solution.py:542
  118.1 1.0 fusion.17
  119.1 1.9 add_convert_fusion.1
  121.0 1.3 collective-permute-start.10
  122.3 1.3 collective-permute-start.11
  125.2 29.1 %collective-permute-done.10.refs_0_ = bf16[256,2560]{1,0:T(8,128)(2,1)S(1)} collective-permute-done((bf16[256,2560]{1,0:T(8,128)(2,1)S(1)}, bf16[256,2560]{1,0:T(8,128)(2,1)S(1)}, u32[]{:S(2)}, u32[]{:S(2)}) %collective-permute-start.10) | collective-permute-done | bytes 1310752 | tf_op jit(solution)/shard_map/ppermute | solution.py:591
  154.3 15.8 %collective-permute-done.11.refs_1_ = bf16[256,2560]{1,0:T(8,128)(2,1)S(1)} collective-permute-done((bf16[256,2560]{1,0:T(8,128)(2,1)S(1)}, bf16[256,2560]{1,0:T(8,128)(2,1)S(1)}, u32[]{:S(2)}, u32[]{:S(2)}) %collective-permute-start.11) | collective-permute-done | bytes 1310752 | tf_op jit(solution)/shard_map/ppermute | solution.py:591
  170.1 1.1 copy-done.6
  171.2 24.6 %scan.3 = (bf16[528,2560]{1,0:T(8,128)(2,1)}, bf16[512,2560]{1,0:T(8,128)(2,1)}, bf16[512,2560]{1,0:T(8,128)(2,1)}, bf16[512,256]{1,0:T(8,128)(2,1)}, f32[512,12...) custom-call(s32[2]{0:T(128)} %fusion.23.at_ref, ...), custom_call_target="tpu_custom_call" | custom-call | flops 3750000128 | tf_op jit(solution)/shard_map/scan/pallas_call | solution.py:253
  195.8 1.1 broadcast_select_fusion.1
  196.9 3.1 %collective-permute-start.14 = (bf16[144,1280]{1,0:T(8,128)(2,1)S(1)}, bf16[144,1280]{1,0:T(8,128)(2,1)S(1)}, u32[]{:S(2)}, u32[]{:S(2)}) collective-permute-start(bf16[144,1280]{1,0:T(8,128)(2,1)S(1)} %broadcast_select_fusion.1), channel_id=1, source_target_pairs={{16,18},{17,19},{18,16},{19,17},{20,22},{21,23},{22,20},{23,21},{2... | collective-permute-start | bytes 1105928 | tf_op jit(solution)/shard_map/ppermute | solution.py:591
  200.0 14.5 %gate.3.gate_ref = bf16[512,2560]{1,0:T(8,128)(2,1)} custom-call(bf16[528,2560]{1,0:T(8,128)(2,1)} %get-tuple-element.75.normed_ref, bf16[2560,5120]{1,0:T(8,128)(2,1)} %bitcast.26), custom_call_target="tpu_custom_call" | custom-call | flops 2000000000 | tf_op jit(solution)/shard_map/gate/pallas_call | solution.py:449
  215.0 4.2 %collective-permute-start.15 = (bf16[144,1280]{1,0:T(8,128)(2,1)S(1)}, bf16[144,1280]{1,0:T(8,128)(2,1)S(1)}, u32[]{:S(2)}, u32[]{:S(2)}) collective-permute-start(bf16[144,1280]{1,0:T(8,128)(2,1)S(1)} %maximum_maximum_fusion.1), channel_id=1, source_target_pairs={{16,20},{17,21},{18,22},{19,23},{20,24},{21,25},{22,26},{23,27},{2... | collective-permute-start | bytes 1105928 | tf_op jit(solution)/shard_map/ppermute | solution.py:591
  219.2 5.0 %collective-permute-start.16 = (bf16[144,1280]{1,0:T(8,128)(2,1)S(1)}, bf16[144,1280]{1,0:T(8,128)(2,1)S(1)}, u32[]{:S(2)}, u32[]{:S(2)}) collective-permute-start(bf16[144,1280]{1,0:T(8,128)(2,1)S(1)} %maximum_maximum_fusion.1), channel_id=1, source_target_pairs={{16,24},{17,25},{18,26},{19,27},{20,28},{21,29},{22,30},{23,31}} | collective-permute-start | bytes 1105928 | tf_op jit(solution)/shard_map/ppermute | solution.py:591
  224.2 1.3 collective-permute-start.17
  225.5 10.0 %inner.3.y_ref = bf16[512,2560]{1,0:T(8,128)(2,1)} custom-call(bf16[512,2560]{1,0:T(8,128)(2,1)} %get-tuple-element.80.x_ref, bf16[512,2560]{1,0:T(8,128)(2,1)} %get-tuple-element.81.xs_ref, bf16[512,256]{1,0:T(8,128)(2,1)} %get-tuple-element.82.bc_ref, f32[512,128]{1,0:T(8,128)} %get-tuple-element.83.acol_ref, f32[128,512]{1,0:T(8,128)} %get-tuple-element.84.arow_ref, ...), custom_call_target="tpu_custom_call" | custom-call | flops 2750000128 | tf_op jit(solution)/shard_map/inner/pallas_call | solution.py:393
  236.7 2.5 collective-permute-start.18
  239.2 5.3 %collective-permute-done.18.got_ref = bf16[128,1280]{1,0:T(8,128)(2,1)S(1)} collective-permute-done((bf16[128,1280]{1,0:T(8,128)(2,1)S(1)}, bf16[128,1280]{1,0:T(8,128)(2,1)S(1)}, u32[]{:S(2)}, u32[]{:S(2)}) %collective-permute-start.18) | collective-permute-done | bytes 327712 | tf_op jit(solution)/shard_map/ppermute | solution.py:591
  245.3 13.9 %outp.6 = (bf16[256,2560]{1,0:T(8,128)(2,1)}, f32[256,128]{1,0:T(8,128)}) custom-call(s32[2]{0:T(128)} %pad_add_fusion.at_ref, bf16[512,2560]{1,0:T(8,128)(2,1)} %inner.3.y_ref, bf16[512,2560]{1,0:T(8,128)(2,1)} %gate.3.gate_ref, bf16[512,256]{1,0:T(8,128)(2,1)} %get-tuple-element.82.bc_ref, bf16[512,128]{1,0:T(8,128)(2,1)} %get-tuple-element.89.eall_ref, ...), custom_call_target="tpu_custom_call" | custom-call | flops 1500000000 | tf_op jit(solution)/shard_map/outp/pallas_call | solution.py:542
  259.2 1.9 collective-permute-start.20
  261.2 3.5 %collective-permute-start.19 = (f32[256,128]{1,0:T(8,128)}, f32[256,128]{1,0:T(8,128)S(1)}, u32[]{:S(2)}, u32[]{:S(2)}) collective-permute-start(f32[256,128]{1,0:T(8,128)} %get-tuple-element.93), channel_id=1, source_target_pairs={{16,17},{17,16},{18,19},{19,18},{20,21},{21,20},{22,23},{23,22},{2... | collective-permute-start | bytes 393224 | tf_op jit(solution)/shard_map/ppermute | solution.py:591
  264.7 14.0 %outp.7 = (bf16[256,2560]{1,0:T(8,128)(2,1)}, f32[256,128]{1,0:T(8,128)}) custom-call(s32[2]{0:T(128)} %pad_add_fusion.1.at_ref, bf16[512,2560]{1,0:T(8,128)(2,1)} %inner.3.y_ref, bf16[512,2560]{1,0:T(8,128)(2,1)} %gate.3.gate_ref, bf16[512,256]{1,0:T(8,128)(2,1)} %get-tuple-element.82.bc_ref, bf16[512,128]{1,0:T(8,128)(2,1)} %get-tuple-element.89.eall_ref, ...), custom_call_target="tpu_custom_call" | custom-call | flops 1500000000 | tf_op jit(solution)/shard_map/outp/pallas_call | solution.py:542
  280.2 3.2 %fusion.3 = bf16[1,1,256,2560]{3,2,1,0:T(8,128)(2,1)} fusion(bf16[256,2560]{1,0:T(8,128)(2,1)} %get-tuple-element.96, bf16[256,2560]{1,0:T(8,128)(2,1)S(1)} %collective-permute-done.20, bf16[256,2560]{1,0:T(8,128)(2,1)S(1)} %copy-done.2, bf16[256,2560]{1,0:T(8,128)(2,1)S(1)} %add_convert_fusion.1, f32[256]{0:T(256)S(1)} %fusion.13, pred[]{:T(512)S(6)} %eq.26, ...), kind=kLoop, calls=%fused_computation.6 | loop fusion | flops 5898240 | bytes 6554626 | tf_op jit(solution)/shard_map/broadcast_in_dim;stack | solution.py:793
  (101 shorter events, 22.8 us)
Async XLA Ops:
  0.0 6.5 %copy-start.7 = (bf16[1,2560,256]{2,1,0:T(8,128)(2,1)S(1)}, bf16[1,2560,256]{2,1,0:T(8,128)(2,1)}, u32[]{:S(2)}) copy-start(bf16[1,2560,256]{2,1,0:T(8,128)(2,1)} %param.19) | copy-start | bytes 3932164
  0.0 28.4 %collective-permute-start = (bf16[256,2560]{1,0:T(8,128)(2,1)}, bf16[256,2560]{1,0:T(8,128)(2,1)S(1)}, u32[]{:S(2)}, u32[]{:S(2)}) collective-permute-start(bf16[256,2560]{1,0:T(8,128)(2,1)} %bitcast.32), channel_id=1, source_target_pairs={{1,0},{0,1},{3,2},{2,3},{5,4},{4,5},{7,6},{6,7},{9,8},{8,9},{11,10... | collective-permute-start | bytes 3932168 | tf_op jit(solution)/shard_map/ppermute | solution.py:591
  3.2 24.4 %collective-permute-start.1 = (bf16[32,2560]{1,0:T(8,128)(2,1)}, bf16[32,2560]{1,0:T(8,128)(2,1)S(1)}, u32[]{:S(2)}, u32[]{:S(2)}) collective-permute-start(bf16[32,2560]{1,0:T(8,128)(2,1)} %pad_maximum_fusion), channel_id=1, source_target_pairs={{1,2},{3,4},{5,6},{7,8},{9,10},{11,12},{13,14},{17,18},{19,20},{21... | collective-permute-start | bytes 491528 | tf_op jit(solution)/shard_map/ppermute | solution.py:591
  3.9 23.8 %collective-permute-start.2 = (bf16[32,2560]{1,0:T(8,128)(2,1)}, bf16[32,2560]{1,0:T(8,128)(2,1)}, u32[]{:S(2)}, u32[]{:S(2)}) collective-permute-start(bf16[32,2560]{1,0:T(8,128)(2,1)} %pad_maximum_fusion), channel_id=1, source_target_pairs={{1,3},{3,5},{5,7},{7,9},{9,11},{11,13},{13,15},{17,19},{19,21},{21... | collective-permute-start | bytes 491528 | tf_op jit(solution)/shard_map/ppermute | solution.py:591
  8.1 18.5 %copy-start.15 = (f32[1,40]{1,0:T(1,128)S(1)}, f32[1,40]{1,0:T(1,128)}, u32[]{:S(2)}) copy-start(f32[1,40]{1,0:T(1,128)} %param.25) | copy-start | bytes 484
  27.7 1.7 copy-start.10
  55.3 15.3 %collective-permute-start.3 = (bf16[144,1280]{1,0:T(8,128)(2,1)S(1)}, bf16[144,1280]{1,0:T(8,128)(2,1)S(1)}, u32[]{:S(2)}, u32[]{:S(2)}) collective-permute-start(bf16[144,1280]{1,0:T(8,128)(2,1)S(1)} %broadcast_select_fusion.3), channel_id=1, source_target_pairs={{0,2},{1,3},{2,0},{3,1},{4,6},{5,7},{6,4},{7,5},{8,10},{9,11},{10,... | collective-permute-start | bytes 1105928 | tf_op jit(solution)/shard_map/ppermute | solution.py:591
  56.1 14.5 %copy-start.3 = (bf16[144,2560]{1,0:T(8,128)(2,1)S(1)}, bf16[144,2560]{1,0:T(8,128)(2,1)}, u32[]{:S(2)}) copy-start(bf16[144,2560]{1,0:T(8,128)(2,1)} %get-tuple-element.51) | copy-start | bytes 2211844
  70.6 2.7 copy-start.13
  71.0 13.6 %collective-permute-start.4 = (bf16[144,1280]{1,0:T(8,128)(2,1)S(1)}, bf16[144,1280]{1,0:T(8,128)(2,1)S(1)}, u32[]{:S(2)}, u32[]{:S(2)}) collective-permute-start(bf16[144,1280]{1,0:T(8,128)(2,1)S(1)} %maximum_maximum_fusion), channel_id=1, source_target_pairs={{0,4},{1,5},{2,6},{3,7},{4,8},{5,9},{6,10},{7,11},{8,12},{9,13},{1... | collective-permute-start | bytes 1105928 | tf_op jit(solution)/shard_map/ppermute | solution.py:591
  71.7 12.9 %collective-permute-start.5 = (bf16[144,1280]{1,0:T(8,128)(2,1)S(1)}, bf16[144,1280]{1,0:T(8,128)(2,1)S(1)}, u32[]{:S(2)}, u32[]{:S(2)}) collective-permute-start(bf16[144,1280]{1,0:T(8,128)(2,1)S(1)} %maximum_maximum_fusion), channel_id=1, source_target_pairs={{0,8},{1,9},{2,10},{3,11},{4,12},{5,13},{6,14},{7,15}} | collective-permute-start | bytes 1105928 | tf_op jit(solution)/shard_map/ppermute | solution.py:591
  72.4 12.3 %collective-permute-start.6 = (bf16[144,1280]{1,0:T(8,128)(2,1)S(1)}, bf16[144,1280]{1,0:T(8,128)(2,1)S(1)}, u32[]{:S(2)}, u32[]{:S(2)}) collective-permute-start(bf16[144,1280]{1,0:T(8,128)(2,1)S(1)} %maximum_maximum_fusion), channel_id=1, source_target_pairs={{0,12},{1,13},{2,14},{3,15}} | collective-permute-start | bytes 1105928 | tf_op jit(solution)/shard_map/ppermute | solution.py:591
  85.8 1.3 collective-permute-start.7
  101.9 17.2 %collective-permute-start.9 = (bf16[256,2560]{1,0:T(8,128)(2,1)}, bf16[256,2560]{1,0:T(8,128)(2,1)S(1)}, u32[]{:S(2)}, u32[]{:S(2)}) collective-permute-start(bf16[256,2560]{1,0:T(8,128)(2,1)} %get-tuple-element.72), channel_id=1, source_target_pairs={{0,1},{1,0},{2,3},{3,2},{4,5},{5,4},{6,7},{7,6},{8,9},{9,8},{10,11... | collective-permute-start | bytes 3932168 | tf_op jit(solution)/shard_map/ppermute | solution.py:591
  103.3 15.8 %copy-start = (bf16[1,256,2560]{2,1,0:T(8,128)(2,1)S(1)}, bf16[1,256,2560]{2,1,0:T(8,128)(2,1)}, u32[]{:S(2)}) copy-start(bf16[1,256,2560]{2,1,0:T(8,128)(2,1)} %param.15) | copy-start | bytes 3932164
  103.3 14.8 %collective-permute-start.8 = (f32[256,128]{1,0:T(8,128)}, f32[256,128]{1,0:T(8,128)S(1)}, u32[]{:S(2)}, u32[]{:S(2)}) collective-permute-start(f32[256,128]{1,0:T(8,128)} %get-tuple-element.70), channel_id=1, source_target_pairs={{0,1},{1,0},{2,3},{3,2},{4,5},{5,4},{6,7},{7,6},{8,9},{9,8},{10,11... | collective-permute-start | bytes 393224 | tf_op jit(solution)/shard_map/ppermute | solution.py:591
  121.0 33.3 %collective-permute-start.10 = (bf16[256,2560]{1,0:T(8,128)(2,1)S(1)}, bf16[256,2560]{1,0:T(8,128)(2,1)S(1)}, u32[]{:S(2)}, u32[]{:S(2)}) collective-permute-start(bf16[256,2560]{1,0:T(8,128)(2,1)S(1)} %add_convert_fusion.1), channel_id=1, source_target_pairs={{0,16},{1,17},{2,18},{3,19},{4,20},{5,21},{6,22},{7,23},{8,24},{9,... | collective-permute-start | bytes 3932168 | tf_op jit(solution)/shard_map/ppermute | solution.py:591
  122.3 47.8 %collective-permute-start.11 = (bf16[256,2560]{1,0:T(8,128)(2,1)S(1)}, bf16[256,2560]{1,0:T(8,128)(2,1)S(1)}, u32[]{:S(2)}, u32[]{:S(2)}) collective-permute-start(bf16[256,2560]{1,0:T(8,128)(2,1)S(1)} %add_convert_fusion.1), channel_id=1, source_target_pairs={{1,16},{0,17},{3,18},{2,19},{5,20},{4,21},{7,22},{6,23},{9,24},{8,... | collective-permute-start | bytes 3932168 | tf_op jit(solution)/shard_map/ppermute | solution.py:591
  123.6 1.6 collective-permute-start.12
  124.3 0.9 collective-permute-start.13
  125.2 44.9 %copy-start.11 = (bf16[16,2560]{1,0:T(8,128)(2,1)}, bf16[16,2560]{1,0:T(8,128)(2,1)S(1)}, u32[]{:S(2)}) copy-start(bf16[16,2560]{1,0:T(8,128)(2,1)S(1)} %collective-permute-done.12.refs_2_) | copy-start | bytes 245764
  125.2 44.9 %copy-start.12 = (bf16[16,2560]{1,0:T(8,128)(2,1)}, bf16[16,2560]{1,0:T(8,128)(2,1)S(1)}, u32[]{:S(2)}) copy-start(bf16[16,2560]{1,0:T(8,128)(2,1)S(1)} %collective-permute-done.13.refs_3_) | copy-start | bytes 245764
  154.3 15.8 %copy-start.1 = (bf16[256,2560]{1,0:T(8,128)(2,1)}, bf16[256,2560]{1,0:T(8,128)(2,1)S(1)}, u32[]{:S(2)}) copy-start(bf16[256,2560]{1,0:T(8,128)(2,1)S(1)} %collective-permute-done.10.refs_0_) | copy-start | bytes 3932164
  196.9 17.6 %collective-permute-start.14 = (bf16[144,1280]{1,0:T(8,128)(2,1)S(1)}, bf16[144,1280]{1,0:T(8,128)(2,1)S(1)}, u32[]{:S(2)}, u32[]{:S(2)}) collective-permute-start(bf16[144,1280]{1,0:T(8,128)(2,1)S(1)} %broadcast_select_fusion.1), channel_id=1, source_target_pairs={{16,18},{17,19},{18,16},{19,17},{20,22},{21,23},{22,20},{23,21},{2... | collective-permute-start | bytes 1105928 | tf_op jit(solution)/shard_map/ppermute | solution.py:591
  200.0 14.5 %copy-start.4 = (bf16[144,2560]{1,0:T(8,128)(2,1)S(1)}, bf16[144,2560]{1,0:T(8,128)(2,1)}, u32[]{:S(2)}) copy-start(bf16[144,2560]{1,0:T(8,128)(2,1)} %get-tuple-element.74) | copy-start | bytes 2211844
  215.0 20.6 %collective-permute-start.15 = (bf16[144,1280]{1,0:T(8,128)(2,1)S(1)}, bf16[144,1280]{1,0:T(8,128)(2,1)S(1)}, u32[]{:S(2)}, u32[]{:S(2)}) collective-permute-start(bf16[144,1280]{1,0:T(8,128)(2,1)S(1)} %maximum_maximum_fusion.1), channel_id=1, source_target_pairs={{16,20},{17,21},{18,22},{19,23},{20,24},{21,25},{22,26},{23,27},{2... | collective-permute-start | bytes 1105928 | tf_op jit(solution)/shard_map/ppermute | solution.py:591
  219.2 16.4 %collective-permute-start.16 = (bf16[144,1280]{1,0:T(8,128)(2,1)S(1)}, bf16[144,1280]{1,0:T(8,128)(2,1)S(1)}, u32[]{:S(2)}, u32[]{:S(2)}) collective-permute-start(bf16[144,1280]{1,0:T(8,128)(2,1)S(1)} %maximum_maximum_fusion.1), channel_id=1, source_target_pairs={{16,24},{17,25},{18,26},{19,27},{20,28},{21,29},{22,30},{23,31}} | collective-permute-start | bytes 1105928 | tf_op jit(solution)/shard_map/ppermute | solution.py:591
  224.2 11.4 %collective-permute-start.17 = (bf16[144,1280]{1,0:T(8,128)(2,1)S(1)}, bf16[144,1280]{1,0:T(8,128)(2,1)S(1)}, u32[]{:S(2)}, u32[]{:S(2)}) collective-permute-start(bf16[144,1280]{1,0:T(8,128)(2,1)S(1)} %maximum_maximum_fusion.1), channel_id=1, source_target_pairs={{16,28},{17,29},{18,30},{19,31}} | collective-permute-start | bytes 1105928 | tf_op jit(solution)/shard_map/ppermute | solution.py:591
  236.7 7.8 %collective-permute-start.18 = (bf16[128,1280]{1,0:T(8,128)(2,1)S(1)}, bf16[128,1280]{1,0:T(8,128)(2,1)S(1)}, u32[]{:S(2)}, u32[]{:S(2)}) collective-permute-start(bf16[128,1280]{1,0:T(8,128)(2,1)S(1)} %get-tuple-element.109), channel_id=1, source_target_pairs={{16,18},{17,19},{18,16},{19,17},{20,22},{21,23},{22,20},{23,21},{2... | collective-permute-start | bytes 983048 | tf_op jit(solution)/shard_map/ppermute | solution.py:591
  259.2 21.0 %collective-permute-start.20 = (bf16[256,2560]{1,0:T(8,128)(2,1)}, bf16[256,2560]{1,0:T(8,128)(2,1)S(1)}, u32[]{:S(2)}, u32[]{:S(2)}) collective-permute-start(bf16[256,2560]{1,0:T(8,128)(2,1)} %get-tuple-element.95), channel_id=1, source_target_pairs={{16,17},{17,16},{18,19},{19,18},{20,21},{21,20},{22,23},{23,22},{2... | collective-permute-start | bytes 3932168 | tf_op jit(solution)/shard_map/ppermute | solution.py:591
  261.1 19.1 %copy-start.2 = (bf16[256,2560]{1,0:T(8,128)(2,1)S(1)}, bf16[256,2560]{1,0:T(8,128)(2,1)}, u32[]{:S(2)}) copy-start(bf16[256,2560]{1,0:T(8,128)(2,1)} %copy-done.1) | copy-start | bytes 3932164
  261.2 18.0 %collective-permute-start.19 = (f32[256,128]{1,0:T(8,128)}, f32[256,128]{1,0:T(8,128)S(1)}, u32[]{:S(2)}, u32[]{:S(2)}) collective-permute-start(f32[256,128]{1,0:T(8,128)} %get-tuple-element.93), channel_id=1, source_target_pairs={{16,17},{17,16},{18,19},{19,18},{20,21},{21,20},{22,23},{23,22},{2... | collective-permute-start | bytes 393224 | tf_op jit(solution)/shard_map/ppermute | solution.py:591
  (5 other events, 5.3 us)

commit v3 on v1

--- a/solution.py
+++ b/solution.py
@@ -11,6 +11,8 @@
 BLOCK = 256
 HALO = 16
 KEEP_ROWS = 16
+SLOTS = 3
+STRIP = 64
 LANES = 128
 epsilon = 1e-05
 highest = lax.Precision.HIGHEST
@@ -40,6 +42,37 @@
     cols = lax.broadcasted_iota(jnp.int32, (LANES, heads * width), 1)
     inside = (cols >= rows * width) & (cols < (rows + 1) * width)
     return jnp.where(inside, 1.0, 0.0).astype(bf16)
+
+
+def stream(step_at, count, source, held, sems, place, meanwhile=None):
+    slots = held.shape[0]
+
+    def copy(tile):
+        slot = lax.rem(tile, slots)
+        return pltpu.make_async_copy(source.at[place(tile)], held.at[slot], sems.at[slot])
+
+    @pl.when(step_at == 0)
+    def _():
+        for tile in range(min(slots - 1, count)):
+            copy(tile).start()
+        if meanwhile is not None:
+            meanwhile()
+
+    if count >= slots:
+
+        @pl.when(step_at + slots - 1 < count)
+        def _():
+            copy(step_at + slots - 1).start()
+
+    copy(step_at).wait()
+    return held.at[lax.rem(step_at, slots)]
+
+
+def column_tile(depth, lanes, first):
+    return lambda tile: (
+        pl.ds(0, depth),
+        pl.ds(pl.multiple_of(first + tile * lanes, LANES), lanes),
+    )
 
 
 def conv_rows(raw_ref, keep_ref, taps, bias, start, stop, col):
@@ -55,7 +88,8 @@
     part_refs, halo_refs = refs[:shares], refs[shares : 2 * shares]
     (
         gain_ref,
-        small_ref,
+        wbc_ref,
+        wdt_ref,
         wx_ref,
         tapx_ref,
         tapbc_ref,
@@ -64,7 +98,7 @@
         dtb_ref,
         rate_ref,
         idc_ref,
-        lhs,
+        normed_ref,
         x_ref,
         xs_ref,
         bc_ref,
@@ -79,6 +113,13 @@
         stepc,
         wend,
         kept,
+        lhs,
+        weighted,
+        step_lanes,
+        wend_lanes,
+        held,
+        sems,
+        out_sem,
     ) = refs[2 * shares :]
     step_at = pl.program_id(0)
     blocks = rows // BLOCK
@@ -86,6 +127,8 @@
     tile_lanes = heads * width
     unit = 256 if tile_lanes % 256 == 0 else LANES
     units = tile_lanes // unit
+
+    saved = pltpu.make_async_copy(lhs, normed_ref, out_sem)
 
     @pl.when(step_at == 0)
     def _():
@@ -104,22 +147,28 @@
         for other in halo_refs[1:]:
             halo = halo + other[...].astype(f32)
         lhs[rows:] = normalize(halo)
-        small = dot(lhs[...], small_ref[...])
+        saved.start()
+        small = dot(lhs[...], wbc_ref[...])
+        dt_raw = lax.dot_general(
+            lhs[0:rows], wdt_ref[...], (((1,), (1,)), ((), ())), preferred_element_type=f32
+        )
         for tap in range(3):
             keep[tap] = (idc_ref[5 + tap : 5 + tap + rows] == idc_ref[8 : 8 + rows]).astype(f32)
-        raw[0:8, 0 : 2 * state_width] = small[rows + HALO - 8 :, : 2 * state_width]
-        raw[8 : 8 + rows, 0 : 2 * state_width] = small[:rows, : 2 * state_width]
+        raw[0:8, 0 : 2 * state_width] = small[rows + HALO - 8 :]
+        raw[8 : 8 + rows, 0 : 2 * state_width] = small[:rows]
         for col in range(0, 2 * state_width, LANES):
-            bc_ref[:, col : col + LANES] = conv_rows(
-                raw,
-                keep,
-                tapbc_ref[:, col : col + LANES],
-                biasbc_ref[:, col : col + LANES],
-                0,
-                rows,
-                col,
-            ).astype(bf16)
-        step = softplus(small[:rows, 2 * state_width :] + dtb_ref[...])
+            strip_cols = slice(col, col + LANES)
+            for a in range(0, rows, STRIP):
+                bc_ref[a : a + STRIP, strip_cols] = conv_rows(
+                    raw,
+                    keep,
+                    tapbc_ref[:, strip_cols],
+                    biasbc_ref[:, strip_cols],
+                    a,
+                    a + STRIP,
+                    col,
+                ).astype(bf16)
+        step = softplus(dt_raw + dtb_ref[...])
         log_step = step * rate_ref[...]
         at = lax.broadcasted_iota(jnp.int32, (BLOCK, BLOCK), 0)
         to = lax.broadcasted_iota(jnp.int32, (BLOCK, BLOCK), 1)
@@ -156,11 +205,16 @@
     high = kept_now.astype(bf16)
     low = (kept_now - high.astype(f32)).astype(bf16)
     keep_lanes = dot(high, spread) + dot(low, spread)
-    step_lanes = dot(stepc[...], spread)
-    wend_lanes = dot(wend[...], spread)
+    step_lanes[...] = dot(stepc[...], spread)
+    wend_lanes[...] = dot(wend[...], spread)
+    tiles = wx_ref.shape[1] // (2 * tile_lanes)
+    depth = wx_ref.shape[0]
+    weights = stream(
+        step_at, tiles, wx_ref, held, sems, column_tile(depth, tile_lanes, tiles * tile_lanes)
+    )
     for u in range(units):
         cols = slice(u * unit, (u + 1) * unit)
-        fresh = dot(lhs[...], wx_ref[:, cols])
+        fresh = dot(lhs[...], weights[:, cols])
         raw[0:8, cols] = fresh[rows + HALO - 8 :]
         raw[8 : 8 + rows, cols] = fresh[:rows]
     at = lax.broadcasted_iota(jnp.int32, (KEEP_ROWS, unit), 0)
@@ -169,25 +223,19 @@
         running = None
         for block in range(blocks):
             r0, r1 = block * BLOCK, (block + 1) * BLOCK
-            pieces = []
             for col in range(u * unit, (u + 1) * unit, LANES):
-                x_now = conv_rows(
-                    raw,
-                    keep,
-                    tapx_ref[:, col : col + LANES],
-                    biasx_ref[:, col : col + LANES],
-                    r0,
-                    r1,
-                    col,
-                )
-                x_ref[r0:r1, col : col + LANES] = x_now.astype(bf16)
-                xs_ref[r0:r1, col : col + LANES] = (
-                    x_now * step_lanes[r0:r1, col : col + LANES]
-                ).astype(bf16)
-                pieces.append((x_now * wend_lanes[r0:r1, col : col + LANES]).astype(bf16))
+                strip_cols = slice(col, col + LANES)
+                taps = tapx_ref[:, strip_cols]
+                bias = biasx_ref[:, strip_cols]
+                for a in range(r0, r1, STRIP):
+                    b = a + STRIP
+                    x_now = conv_rows(raw, keep, taps, bias, a, b, col)
+                    x_ref[a:b, strip_cols] = x_now.astype(bf16)
+                    xs_ref[a:b, strip_cols] = (x_now * step_lanes[a:b, strip_cols]).astype(bf16)
+                    weighted[a:b, strip_cols] = (x_now * wend_lanes[a:b, strip_cols]).astype(bf16)
             local = lax.dot_general(
                 bc_ref[r0:r1, 0:state_width],
-                jnp.concatenate(pieces, 1),
+                weighted[r0:r1, cols],
                 (((0,), (0,)), ((), ())),
                 preferred_element_type=f32,
             )
@@ -204,8 +252,12 @@
         )
         sent_ref[state_width:, cols] = both.astype(bf16)
 
-
-def scan_call(at, parts, halos, gain, small, w_zx, tapx, tapbc, biasx, biasbc, dtb, rate, idc, sizes):
+    @pl.when(step_at == pl.num_programs(0) - 1)
+    def _():
+        saved.wait()
+
+
+def scan_call(at, parts, halos, gain, wbc, wdt, w_zx, tapx, tapbc, biasx, biasbc, dtb, rate, idc, sizes):
     rows, heads, width, tiles, state_width = sizes
     shares, depth = len(parts), w_zx.shape[0]
     tile_lanes = heads * width
@@ -227,8 +279,9 @@
             + [whole(HALO, depth)] * shares
             + [
                 whole(1, depth),
-                whole(depth, 2 * state_width + LANES),
-                pl.BlockSpec((depth, tile_lanes), lambda i, at: (0, tiles + i)),
+                whole(depth, 2 * state_width),
+                whole(LANES, depth),
+                pl.BlockSpec(memory_space=pltpu.HBM),
                 column(4),
                 whole(4, 2 * state_width),
                 column(1),
@@ -238,9 +291,9 @@
                 whole(rows + 8, LANES),
             ],
             out_specs=[
-                whole(rows + HALO, depth),
-                column(rows),
-                column(rows),
+                pl.BlockSpec(memory_space=pltpu.HBM),
+                pl.BlockSpec((None, rows, tile_lanes), lambda i, at: (i, 0, 0)),
+                pl.BlockSpec((None, rows, tile_lanes), lambda i, at: (i, 0, 0)),
                 whole(rows, 2 * state_width),
                 whole(rows, LANES),
                 whole(LANES, rows),
@@ -257,12 +310,19 @@
                 pltpu.VMEM((rows, LANES), bf16),
                 pltpu.VMEM((rows, LANES), bf16),
                 pltpu.VMEM((max(8, blocks + 1), LANES), f32),
+                pltpu.VMEM((rows + HALO, depth), bf16),
+                pltpu.VMEM((rows, tile_lanes), bf16),
+                pltpu.VMEM((rows, tile_lanes), f32),
+                pltpu.VMEM((rows, tile_lanes), f32),
+                pltpu.VMEM((SLOTS, depth, tile_lanes), bf16),
+                pltpu.SemaphoreType.DMA((SLOTS,)),
+                pltpu.SemaphoreType.DMA,
             ],
         ),
         out_shape=[
             jax.ShapeDtypeStruct((rows + HALO, depth), bf16),
-            jax.ShapeDtypeStruct((rows, channels), bf16),
-            jax.ShapeDtypeStruct((rows, channels), bf16),
+            jax.ShapeDtypeStruct((tiles, rows, tile_lanes), bf16),
+            jax.ShapeDtypeStruct((tiles, rows, tile_lanes), bf16),
             jax.ShapeDtypeStruct((rows, 2 * state_width), bf16),
             jax.ShapeDtypeStruct((rows, LANES), f32),
             jax.ShapeDtypeStruct((LANES, rows), f32),
@@ -276,7 +336,7 @@
         ),
         cost_estimate=cost(15),
         name="scan",
-    )(at, *parts, *halos, gain, small, w_zx, tapx, tapbc, biasx, biasbc, dtb, rate, idc)
+    )(at, *parts, *halos, gain, wbc, wdt, w_zx, tapx, tapbc, biasx, biasbc, dtb, rate, idc)
 
 
 def inner_kernel(
@@ -295,6 +355,7 @@
     idr_ref,
     y_ref,
     gram,
+    mix,
 ):
     blocks = rows // BLOCK
     state_width = bc_ref.shape[1] // 2
@@ -330,9 +391,12 @@
             total = None
             for inner in range(pack):
                 head = first + inner
-                gap = acol[r0:r1, head : head + 1] - arow_ref[head : head + 1, r0:r1]
-                mix = (jnp.exp(jnp.minimum(gap, 0.0)) * gram[block]).astype(bf16)
-                part = dot(mix, xs_now)
+                row = arow_ref[head : head + 1, r0:r1]
+                for a in range(0, BLOCK, STRIP):
+                    gap = acol[r0 + a : r0 + a + STRIP, head : head + 1] - row
+                    weight = jnp.exp(jnp.minimum(gap, 0.0)) * gram[block, a : a + STRIP]
+                    mix[head % 4, a : a + STRIP] = weight.astype(bf16)
+                part = dot(mix[head % 4], xs_now)
                 total = part if total is None else jnp.where(lane < inner * width, total, part)
             total = total + skip_ref[:, cols] * x_ref[r0:r1, cols].astype(f32)
             if block > 0:
@@ -343,7 +407,6 @@
 def inner_call(x, xs, bc, acol, arow, ein, states, skip, idc, idr, sizes):
     rows, heads, width, tiles, state_width = sizes
     tile_lanes = heads * width
-    channels = tiles * tile_lanes
     blocks = rows // BLOCK
 
     def whole(*shape):
@@ -352,14 +415,15 @@
     def column(lead):
         return pl.BlockSpec((lead, tile_lanes), lambda i: (0, i))
 
+    tiled = pl.BlockSpec((None, rows, tile_lanes), lambda i: (i, 0, 0))
     arow_rows = heads if heads % 8 == 0 else LANES
 
     return pl.pallas_call(
         functools.partial(inner_kernel, rows, heads, width),
         grid=(tiles,),
         in_specs=[
-            column(rows),
-            column(rows),
+            tiled,
+            tiled,
             whole(rows, 2 * state_width),
             whole(rows, LANES),
             pl.BlockSpec((arow_rows, rows), lambda i: (i, 0)),
@@ -369,9 +433,12 @@
             whole(rows + 8, LANES),
             whole(8, rows),
         ],
-        out_specs=column(rows),
-        out_shape=jax.ShapeDtypeStruct((rows, channels), bf16),
-        scratch_shapes=[pltpu.VMEM((blocks, BLOCK, BLOCK), f32)],
+        out_specs=tiled,
+        out_shape=jax.ShapeDtypeStruct((tiles, rows, tile_lanes), bf16),
+        scratch_shapes=[
+            pltpu.VMEM((blocks, BLOCK, BLOCK), f32),
+            pltpu.VMEM((4, BLOCK, BLOCK), bf16),
+        ],
         compiler_params=pltpu.CompilerParams(
             dimension_semantics=("arbitrary",), vmem_limit_bytes=60 * 2**20
         ),
@@ -380,8 +447,11 @@
     )(x, xs, bc, acol, arow, ein, states, skip, idc, idr)
 
 
-def gate_kernel(normed_ref, wz_ref, gate_ref):
-    gate_ref[...] = silu(dot(normed_ref[...], wz_ref[...])).astype(bf16)
+def gate_kernel(tiles, normed_ref, wz_ref, gate_ref, held, sems):
+    depth, tile_lanes = held.shape[1:]
+    place = column_tile(depth, tile_lanes, 0)
+    weights = stream(pl.program_id(0), tiles, wz_ref, held, sems, place)
+    gate_ref[...] = silu(dot(normed_ref[...], weights[...])).astype(bf16)
 
 
 def gate_call(normed, w_zx, sizes):
@@ -389,14 +459,18 @@
     depth = normed.shape[1]
     tile_lanes = heads * width
     return pl.pallas_call(
-        gate_kernel,
+        functools.partial(gate_kernel, tiles),
         grid=(tiles,),
         in_specs=[
             pl.BlockSpec((rows, depth), lambda i: (0, 0)),
-            pl.BlockSpec((depth, tile_lanes), lambda i: (0, i)),
+            pl.BlockSpec(memory_space=pltpu.HBM),
         ],
-        out_specs=pl.BlockSpec((rows, tile_lanes), lambda i: (0, i)),
-        out_shape=jax.ShapeDtypeStruct((rows, tiles * tile_lanes), bf16),
+        scratch_shapes=[
+            pltpu.VMEM((SLOTS, depth, tile_lanes), bf16),
+            pltpu.SemaphoreType.DMA((SLOTS,)),
+        ],
+        out_specs=pl.BlockSpec((None, rows, tile_lanes), lambda i: (i, 0, 0)),
+        out_shape=jax.ShapeDtypeStruct((tiles, rows, tile_lanes), bf16),
         compiler_params=pltpu.CompilerParams(
             dimension_semantics=("arbitrary",), vmem_limit_bytes=60 * 2**20
         ),
@@ -408,7 +482,6 @@
 def out_kernel(
     heads,
     width,
-    tiles,
     at_ref,
     y_ref,
     gate_ref,
@@ -422,13 +495,16 @@
     sq_ref,
     lhs,
     coming,
+    held,
+    sems,
 ):
     state_width = bc_ref.shape[1] // 2
-    tile_lanes = heads * width
     half = stay_ref.shape[1]
-
-    @pl.when(pl.program_id(0) == 0)
-    def _():
+    tiles, _, tile_lanes = y_ref.shape
+    piece = pl.program_id(0)
+    channels, lanes = held.shape[1:]
+
+    def prepare():
         swapped = at_ref[1] != 0
         coming[:, :half] = jnp.where(swapped, got_ref[...], stay_ref[...])
         coming[:, half:] = jnp.where(swapped, stay_ref[...], got_ref[...])
@@ -437,19 +513,22 @@
             cols = slice(tile * tile_lanes, (tile + 1) * tile_lanes)
             carried = dot(bc_ref[:, state_width:], coming[:, cols])
             carried = carried * dot(eall_ref[...], spread_matrix(heads, width, tile))
-            gated = (y_ref[:, cols].astype(f32) + carried) * gate_ref[:, cols].astype(f32)
+            gated = (y_ref[tile].astype(f32) + carried) * gate_ref[tile].astype(f32)
             part = jnp.sum(gated * gated, axis=1, keepdims=True)
             squares = part if squares is None else squares + part
             lhs[:, cols] = (gated * gain_ref[:, cols]).astype(bf16)
         sq_ref[...] = jnp.broadcast_to(squares, sq_ref.shape)
 
-    p_ref[...] = dot(lhs[...], w_ref[...]).astype(bf16)
+    weights = stream(
+        piece, w_ref.shape[1] // lanes, w_ref, held, sems, column_tile(channels, lanes, 0), prepare
+    )
+    p_ref[...] = dot(lhs[...], weights[...]).astype(bf16)
 
 
 def out_call(at, y, gate, bc, eall, stay, got, gain, w_out, count, sizes):
     rows, heads, width, tiles, state_width = sizes
     channels, depth = w_out.shape
-    piece = 512 if depth % 512 == 0 else depth
+    tile_lanes = heads * width
 
     def taken(lanes):
         return pl.BlockSpec((count, lanes), lambda i, at: (at[0], 0))
@@ -457,20 +536,22 @@
     def whole(*shape):
         return pl.BlockSpec(shape, lambda i, at: (0,) * len(shape))
 
+    piece = 512 if depth % 512 == 0 else depth
+    tiled = pl.BlockSpec((tiles, count, tile_lanes), lambda i, at: (0, at[0], 0))
     return pl.pallas_call(
-        functools.partial(out_kernel, heads, width, tiles),
+        functools.partial(out_kernel, heads, width),
         grid_spec=pltpu.PrefetchScalarGridSpec(
             num_scalar_prefetch=1,
             grid=(depth // piece,),
             in_specs=[
-                taken(channels),
-                taken(channels),
+                tiled,
+                tiled,
                 taken(2 * state_width),
                 taken(LANES),
                 whole(state_width, channels // 2),
                 whole(state_width, channels // 2),
                 whole(1, channels),
-                pl.BlockSpec((channels, piece), lambda i, at: (0, i)),
+                pl.BlockSpec(memory_space=pltpu.HBM),
             ],
             out_specs=[
                 pl.BlockSpec((count, piece), lambda i, at: (0, i)),
@@ -479,6 +560,8 @@
             scratch_shapes=[
                 pltpu.VMEM((count, channels), bf16),
                 pltpu.VMEM((state_width, channels), bf16),
+                pltpu.VMEM((SLOTS, channels, piece), bf16),
+                pltpu.SemaphoreType.DMA((SLOTS,)),
             ],
         ),
         out_shape=[
@@ -625,7 +708,7 @@
         return jnp.pad(a, ((0, 0), (0, LANES - local_heads)))
 
     w_zx = in_zx[0].reshape(depth, 2 * channels)
-    small = jnp.concatenate([in_bc[0], lanes(in_dt[0])], 1)
+    wdt = jnp.pad(in_dt[0].T, ((0, LANES - local_heads), (0, 0)))
     dtb = lanes(dt_bias)
     rate = lanes(-jnp.exp(a_log))
     skip = jnp.repeat(d_skip, width, axis=1)
@@ -657,7 +740,8 @@
                 parts,
                 halos,
                 norm_gain,
-                small,
+                in_bc[0],
+                wdt,
                 w_zx,
                 conv_x[0],
                 conv_bc[0],

time: 276 us -> 273 us (0.989)
  Pallas kernels: 141 us -> 136 us
  waiting for transfers between devices: 55.3 us -> 60.2 us
    pallas_call x6, Pallas kernels: 71.4 us -> 63.7 us  [the longest x4 39.1 us: out_call(): pl.pallas_call(functools.partial(out_kernel, heads, width), grid_spec=plt...]
    ppermute x21, waiting for transfers between devices: 55.3 us -> 60.2 us  [move(): lax.ppermute(block, AXES, [(self.spot(*source), self.spot(*target)) for s...]
    pallas_call x2, Pallas kernels: 49.5 us -> 52.6 us  [scan_call(): pl.pallas_call(functools.partial(scan_kernel, rows, heads, width, shares)...]
    unnamed x34 -> x33, local copies, waits for them, and re-layouts: 22.1 us -> 21 us
  transfers between devices with their start and end apart: 21 -> 21, of which waited for: 4 -> 4; matrix products, arithmetic and copies ran while one was open for 11% -> 10% of each run, Pallas kernels for 25% -> 24%
where the time goes in v3:
time: 273 us; the launch traced here: 272 us
  Pallas kernels  136 us (50%)
  waiting for transfers between devices  60.2 us (22%)
  starting transfers between devices  32.9 us (12%)
  local copies, waits for them, and re-layouts  26.4 us (10%)
  other arithmetic  15.5 us (6%)
    ppermute x21, waiting for transfers between devices, move(): lax.ppermute(block, AXES, [(self.spot(*source), self.spot(*target)) for s...  60.2 us
    pallas_call x2, Pallas kernels, scan_call(): pl.pallas_call(functools.partial(scan_kernel, rows, heads, width, shares)...  52.6 us
    pallas_call x4, Pallas kernels, out_call(): pl.pallas_call(functools.partial(out_kernel, heads, width), grid_spec=plt...  39.1 us
    ppermute x21, starting transfers between devices, move(): lax.ppermute(block, AXES, [(self.spot(*source), self.spot(*target)) for s...  32.9 us
    pallas_call x2, Pallas kernels, gate_call(): pl.pallas_call(functools.partial(gate_kernel, tiles), grid=(tiles,), in_s...  24.6 us
    unnamed x33, local copies, waits for them, and re-layouts  21 us
    pallas_call x2, Pallas kernels, inner_call(): pl.pallas_call(functools.partial(inner_kernel, rows, heads, width), grid=...  19.8 us
  transfers between devices with their start and end apart: 21, of which 4 were waited for; matrix products, arithmetic and copies ran while one was open for 10% of the time, Pallas kernels for 24%

profile of v3, /device:TPU:1, one launch (start us, length us, event | category | flops | bytes accessed | tf_op | source)
XLA Modules:
  0.0 271.7 jit_solution(2363212216337318939)
XLA Ops:
  4.5 18.1 %copy.16 = bf16[320,8,2,2560]{3,1,2,0:T(8,128)(2,1)} copy(bf16[320,8,2,2560]{3,2,1,0:T(2,128)(2,1)} %bitcast.33) | data formatting | bytes 52428800
  26.4 26.3 %scan.2 = (bf16[528,2560]{1,0:T(8,128)(2,1)}, bf16[5,512,512]{2,1,0:T(8,128)(2,1)}, bf16[5,512,512]{2,1,0:T(8,128)(2,1)}, bf16[512,256]{1,0:T(8,128)(2,1)}, f32[...) custom-call(s32[2]{0:T(128)} %fusion.21.at_ref, ...), custom_call_target="tpu_custom_call" | custom-call | flops 3750000128 | tf_op jit(solution)/shard_map/scan/pallas_call | solution.py:273
  52.7 1.1 broadcast_select_fusion.3
  54.6 12.3 %gate.2.gate_ref = bf16[5,512,512]{2,1,0:T(8,128)(2,1)} custom-call(bf16[528,2560]{1,0:T(8,128)(2,1)} %get-tuple-element.52.normed_ref, bf16[2560,5120]{1,0:T(8,128)(2,1)} %bitcast.26), custom_call_target="tpu_custom_call" | custom-call | flops 2000000000 | tf_op jit(solution)/shard_map/gate/pallas_call | solution.py:461
  70.8 9.9 %inner.2.y_ref = bf16[5,512,512]{2,1,0:T(8,128)(2,1)} custom-call(bf16[5,512,512]{2,1,0:T(8,128)(2,1)} %get-tuple-element.57.x_ref, bf16[5,512,512]{2,1,0:T(8,128)(2,1)} %get-tuple-element.58.xs_ref, bf16[512,256]{1,0:T(8,128)(2,1)} %get-tuple-element.59.bc_ref, f32[512,128]{1,0:T(8,128)} %get-tuple-element.60.acol_ref, ...), custom_call_target="tpu_custom_call" | custom-call | flops 2750000128 | tf_op jit(solution)/shard_map/inner/pallas_call | solution.py:421
  84.1 9.8 %outp.4 = (bf16[256,2560]{1,0:T(8,128)(2,1)}, f32[256,128]{1,0:T(8,128)}) custom-call(s32[2]{0:T(128)} %pad_add_fusion.at_ref, bf16[5,512,512]{2,1,0:T(8,128)(2,1)} %inner.2.y_ref, bf16[5,512,512]{2,1,0:T(8,128)(2,1)} %gate.2.gate_ref, bf16[512,256]{1,0:T(8,128)(2,1)} %get-tuple-element.59.bc_ref, bf16[512,128]{1,0:T(8,128)(2,1)} %get-tuple-element.66.eall_ref, ...), custom_call_target="tpu_custom_call" | custom-call | flops 1500000000 | tf_op jit(solution)/shard_map/outp/pallas_call | solution.py:541
  96.0 9.8 %outp.5 = (bf16[256,2560]{1,0:T(8,128)(2,1)}, f32[256,128]{1,0:T(8,128)}) custom-call(s32[2]{0:T(128)} %pad_add_fusion.1.at_ref, bf16[5,512,512]{2,1,0:T(8,128)(2,1)} %inner.2.y_ref, bf16[5,512,512]{2,1,0:T(8,128)(2,1)} %gate.2.gate_ref, bf16[512,256]{1,0:T(8,128)(2,1)} %get-tuple-element.59.bc_ref, bf16[512,128]{1,0:T(8,128)(2,1)} %get-tuple-element.66.eall_ref, ...), custom_call_target="tpu_custom_call" | custom-call | flops 1500000000 | tf_op jit(solution)/shard_map/outp/pallas_call | solution.py:541
  105.8 1.0 fusion.15
  106.9 1.9 add_convert_fusion.1
  108.8 1.3 collective-permute-start.10
  110.1 1.3 collective-permute-start.11
  112.8 34.0 %collective-permute-done.10.refs_0_ = bf16[256,2560]{1,0:T(8,128)(2,1)S(1)} collective-permute-done((bf16[256,2560]{1,0:T(8,128)(2,1)S(1)}, bf16[256,2560]{1,0:T(8,128)(2,1)S(1)}, u32[]{:S(2)}, u32[]{:S(2)}) %collective-permute-start.10) | collective-permute-done | bytes 1310752 | tf_op jit(solution)/shard_map/ppermute | solution.py:587
  146.8 15.8 %collective-permute-done.11.refs_1_ = bf16[256,2560]{1,0:T(8,128)(2,1)S(1)} collective-permute-done((bf16[256,2560]{1,0:T(8,128)(2,1)S(1)}, bf16[256,2560]{1,0:T(8,128)(2,1)S(1)}, u32[]{:S(2)}, u32[]{:S(2)}) %collective-permute-start.11) | collective-permute-done | bytes 1310752 | tf_op jit(solution)/shard_map/ppermute | solution.py:587
  162.6 1.1 copy-done.6
  163.7 26.3 %scan.3 = (bf16[528,2560]{1,0:T(8,128)(2,1)}, bf16[5,512,512]{2,1,0:T(8,128)(2,1)}, bf16[5,512,512]{2,1,0:T(8,128)(2,1)}, bf16[512,256]{1,0:T(8,128)(2,1)}, f32[...) custom-call(s32[2]{0:T(128)} %fusion.21.at_ref, ...), custom_call_target="tpu_custom_call" | custom-call | flops 3750000128 | tf_op jit(solution)/shard_map/scan/pallas_call | solution.py:273
  190.0 1.1 broadcast_select_fusion.1
  191.2 3.3 %collective-permute-start.14 = (bf16[144,1280]{1,0:T(8,128)(2,1)S(1)}, bf16[144,1280]{1,0:T(8,128)(2,1)S(1)}, u32[]{:S(2)}, u32[]{:S(2)}) collective-permute-start(bf16[144,1280]{1,0:T(8,128)(2,1)S(1)} %broadcast_select_fusion.1), channel_id=1, source_target_pairs={{16,18},{17,19},{18,16},{19,17},{20,22},{21,23},{22,20},{23,21},{2... | collective-permute-start | bytes 1105928 | tf_op jit(solution)/shard_map/ppermute | solution.py:587
  194.5 12.3 %gate.3.gate_ref = bf16[5,512,512]{2,1,0:T(8,128)(2,1)} custom-call(bf16[528,2560]{1,0:T(8,128)(2,1)} %get-tuple-element.75.normed_ref, bf16[2560,5120]{1,0:T(8,128)(2,1)} %bitcast.28), custom_call_target="tpu_custom_call" | custom-call | flops 2000000000 | tf_op jit(solution)/shard_map/gate/pallas_call | solution.py:461
  207.2 4.5 %collective-permute-start.15 = (bf16[144,1280]{1,0:T(8,128)(2,1)S(1)}, bf16[144,1280]{1,0:T(8,128)(2,1)S(1)}, u32[]{:S(2)}, u32[]{:S(2)}) collective-permute-start(bf16[144,1280]{1,0:T(8,128)(2,1)S(1)} %maximum_maximum_fusion.1), channel_id=1, source_target_pairs={{16,20},{17,21},{18,22},{19,23},{20,24},{21,25},{22,26},{23,27},{2... | collective-permute-start | bytes 1105928 | tf_op jit(solution)/shard_map/ppermute | solution.py:587
  211.7 5.0 %collective-permute-start.16 = (bf16[144,1280]{1,0:T(8,128)(2,1)S(1)}, bf16[144,1280]{1,0:T(8,128)(2,1)S(1)}, u32[]{:S(2)}, u32[]{:S(2)}) collective-permute-start(bf16[144,1280]{1,0:T(8,128)(2,1)S(1)} %maximum_maximum_fusion.1), channel_id=1, source_target_pairs={{16,24},{17,25},{18,26},{19,27},{20,28},{21,29},{22,30},{23,31}} | collective-permute-start | bytes 1105928 | tf_op jit(solution)/shard_map/ppermute | solution.py:587
  216.7 1.3 collective-permute-start.17
  218.1 9.9 %inner.3.y_ref = bf16[5,512,512]{2,1,0:T(8,128)(2,1)} custom-call(bf16[5,512,512]{2,1,0:T(8,128)(2,1)} %get-tuple-element.80.x_ref, bf16[5,512,512]{2,1,0:T(8,128)(2,1)} %get-tuple-element.81.xs_ref, bf16[512,256]{1,0:T(8,128)(2,1)} %get-tuple-element.82.bc_ref, f32[512,128]{1,0:T(8,128)} %get-tuple-element.83.acol_ref, ...), custom_call_target="tpu_custom_call" | custom-call | flops 2750000128 | tf_op jit(solution)/shard_map/inner/pallas_call | solution.py:421
  228.2 1.0 select_convert_fusion
  229.2 2.2 collective-permute-start.18
  231.4 5.6 %collective-permute-done.18.got_ref = bf16[128,1280]{1,0:T(8,128)(2,1)S(1)} collective-permute-done((bf16[128,1280]{1,0:T(8,128)(2,1)S(1)}, bf16[128,1280]{1,0:T(8,128)(2,1)S(1)}, u32[]{:S(2)}, u32[]{:S(2)}) %collective-permute-start.18) | collective-permute-done | bytes 327712 | tf_op jit(solution)/shard_map/ppermute | solution.py:587
  237.7 9.8 %outp.6 = (bf16[256,2560]{1,0:T(8,128)(2,1)}, f32[256,128]{1,0:T(8,128)}) custom-call(s32[2]{0:T(128)} %pad_add_fusion.at_ref, bf16[5,512,512]{2,1,0:T(8,128)(2,1)} %inner.3.y_ref, bf16[5,512,512]{2,1,0:T(8,128)(2,1)} %gate.3.gate_ref, bf16[512,256]{1,0:T(8,128)(2,1)} %get-tuple-element.82.bc_ref, bf16[512,128]{1,0:T(8,128)(2,1)} %get-tuple-element.89.eall_ref, ...), custom_call_target="tpu_custom_call" | custom-call | flops 1500000000 | tf_op jit(solution)/shard_map/outp/pallas_call | solution.py:541
  247.5 1.9 collective-permute-start.20
  249.4 3.5 %collective-permute-start.19 = (f32[256,128]{1,0:T(8,128)}, f32[256,128]{1,0:T(8,128)S(1)}, u32[]{:S(2)}, u32[]{:S(2)}) collective-permute-start(f32[256,128]{1,0:T(8,128)} %get-tuple-element.93), channel_id=1, source_target_pairs={{16,17},{17,16},{18,19},{19,18},{20,21},{21,20},{22,23},{23,22},{2... | collective-permute-start | bytes 393224 | tf_op jit(solution)/shard_map/ppermute | solution.py:587
  252.9 9.8 %outp.7 = (bf16[256,2560]{1,0:T(8,128)(2,1)}, f32[256,128]{1,0:T(8,128)}) custom-call(s32[2]{0:T(128)} %pad_add_fusion.1.at_ref, bf16[5,512,512]{2,1,0:T(8,128)(2,1)} %inner.3.y_ref, bf16[5,512,512]{2,1,0:T(8,128)(2,1)} %gate.3.gate_ref, bf16[512,256]{1,0:T(8,128)(2,1)} %get-tuple-element.82.bc_ref, bf16[512,128]{1,0:T(8,128)(2,1)} %get-tuple-element.89.eall_ref, ...), custom_call_target="tpu_custom_call" | custom-call | flops 1500000000 | tf_op jit(solution)/shard_map/outp/pallas_call | solution.py:541
  262.7 4.7 %collective-permute-done.19 = f32[256,128]{1,0:T(8,128)S(1)} collective-permute-done((f32[256,128]{1,0:T(8,128)}, f32[256,128]{1,0:T(8,128)S(1)}, u32[]{:S(2)}, u32[]{:S(2)}) %collective-permute-start.19) | collective-permute-done | bytes 131104 | tf_op jit(solution)/shard_map/ppermute | solution.py:587
  267.4 1.0 fusion.11
  268.5 3.2 %fusion.1 = bf16[1,1,256,2560]{3,2,1,0:T(8,128)(2,1)} fusion(bf16[256,2560]{1,0:T(8,128)(2,1)} %get-tuple-element.96, bf16[256,2560]{1,0:T(8,128)(2,1)S(1)} %collective-permute-done.20, bf16[256,2560]{1,0:T(8,128)(2,1)S(1)} %copy-done.2, bf16[256,2560]{1,0:T(8,128)(2,1)S(1)} %add_convert_fusion.1, f32[256]{0:T(256)S(1)} %fusion.11, pred[]{:T(512)S(6)} %eq.26, ...), kind=kLoop, calls=%fused_computation.3 | loop fusion | flops 5898240 | bytes 6554626 | tf_op jit(solution)/shard_map/broadcast_in_dim;stack | solution.py:790
  (100 shorter events, 20.8 us)
Async XLA Ops:
  0.0 25.2 %collective-permute-start = (bf16[256,2560]{1,0:T(8,128)(2,1)}, bf16[256,2560]{1,0:T(8,128)(2,1)S(1)}, u32[]{:S(2)}, u32[]{:S(2)}) collective-permute-start(bf16[256,2560]{1,0:T(8,128)(2,1)} %bitcast.34), channel_id=1, source_target_pairs={{1,0},{0,1},{3,2},{2,3},{5,4},{4,5},{7,6},{6,7},{9,8},{8,9},{11,10... | collective-permute-start | bytes 3932168 | tf_op jit(solution)/shard_map/ppermute | solution.py:587
  2.4 22.7 %collective-permute-start.1 = (bf16[32,2560]{1,0:T(8,128)(2,1)S(1)}, bf16[32,2560]{1,0:T(8,128)(2,1)S(1)}, u32[]{:S(2)}, u32[]{:S(2)}) collective-permute-start(bf16[32,2560]{1,0:T(8,128)(2,1)S(1)} %pad_maximum_fusion), channel_id=1, source_target_pairs={{1,2},{3,4},{5,6},{7,8},{9,10},{11,12},{13,14},{17,18},{19,20},{21... | collective-permute-start | bytes 491528 | tf_op jit(solution)/shard_map/ppermute | solution.py:587
  3.1 22.0 %collective-permute-start.2 = (bf16[32,2560]{1,0:T(8,128)(2,1)S(1)}, bf16[32,2560]{1,0:T(8,128)(2,1)S(1)}, u32[]{:S(2)}, u32[]{:S(2)}) collective-permute-start(bf16[32,2560]{1,0:T(8,128)(2,1)S(1)} %pad_maximum_fusion), channel_id=1, source_target_pairs={{1,3},{3,5},{5,7},{7,9},{9,11},{11,13},{13,15},{17,19},{19,21},{21... | collective-permute-start | bytes 491528 | tf_op jit(solution)/shard_map/ppermute | solution.py:587
  4.5 18.1 %copy-start.9 = (bf16[1,2560,40]{1,2,0:T(8,128)(2,1)S(1)}, bf16[1,2560,40]{1,2,0:T(8,128)(2,1)}, u32[]{:S(2)}) copy-start(bf16[1,2560,40]{1,2,0:T(8,128)(2,1)} %param.20) | copy-start | bytes 614404
  4.5 19.6 %copy-start.15 = (f32[1,40]{1,0:T(1,128)S(1)}, f32[1,40]{1,0:T(1,128)}, u32[]{:S(2)}) copy-start(f32[1,40]{1,0:T(1,128)} %param.25) | copy-start | bytes 484
  53.8 13.1 %collective-permute-start.3 = (bf16[144,1280]{1,0:T(8,128)(2,1)S(1)}, bf16[144,1280]{1,0:T(8,128)(2,1)S(1)}, u32[]{:S(2)}, u32[]{:S(2)}) collective-permute-start(bf16[144,1280]{1,0:T(8,128)(2,1)S(1)} %broadcast_select_fusion.3), channel_id=1, source_target_pairs={{0,2},{1,3},{2,0},{3,1},{4,6},{5,7},{6,4},{7,5},{8,10},{9,11},{10,... | collective-permute-start | bytes 1105928 | tf_op jit(solution)/shard_map/ppermute | solution.py:587
  54.6 12.3 %copy-start.3 = (bf16[144,2560]{1,0:T(8,128)(2,1)S(1)}, bf16[144,2560]{1,0:T(8,128)(2,1)}, u32[]{:S(2)}) copy-start(bf16[144,2560]{1,0:T(8,128)(2,1)} %get-tuple-element.51) | copy-start | bytes 2211844
  66.9 2.5 copy-start.14
  67.4 13.3 %collective-permute-start.4 = (bf16[144,1280]{1,0:T(8,128)(2,1)S(1)}, bf16[144,1280]{1,0:T(8,128)(2,1)S(1)}, u32[]{:S(2)}, u32[]{:S(2)}) collective-permute-start(bf16[144,1280]{1,0:T(8,128)(2,1)S(1)} %maximum_maximum_fusion), channel_id=1, source_target_pairs={{0,4},{1,5},{2,6},{3,7},{4,8},{5,9},{6,10},{7,11},{8,12},{9,13},{1... | collective-permute-start | bytes 1105928 | tf_op jit(solution)/shard_map/ppermute | solution.py:587
  68.0 12.7 %collective-permute-start.5 = (bf16[144,1280]{1,0:T(8,128)(2,1)S(1)}, bf16[144,1280]{1,0:T(8,128)(2,1)S(1)}, u32[]{:S(2)}, u32[]{:S(2)}) collective-permute-start(bf16[144,1280]{1,0:T(8,128)(2,1)S(1)} %maximum_maximum_fusion), channel_id=1, source_target_pairs={{0,8},{1,9},{2,10},{3,11},{4,12},{5,13},{6,14},{7,15}} | collective-permute-start | bytes 1105928 | tf_op jit(solution)/shard_map/ppermute | solution.py:587
  68.7 12.0 %collective-permute-start.6 = (bf16[144,1280]{1,0:T(8,128)(2,1)S(1)}, bf16[144,1280]{1,0:T(8,128)(2,1)S(1)}, u32[]{:S(2)}, u32[]{:S(2)}) collective-permute-start(bf16[144,1280]{1,0:T(8,128)(2,1)S(1)} %maximum_maximum_fusion), channel_id=1, source_target_pairs={{0,12},{1,13},{2,14},{3,15}} | collective-permute-start | bytes 1105928 | tf_op jit(solution)/shard_map/ppermute | solution.py:587
  81.8 1.5 collective-permute-start.7
  93.9 12.9 %collective-permute-start.9 = (bf16[256,2560]{1,0:T(8,128)(2,1)}, bf16[256,2560]{1,0:T(8,128)(2,1)S(1)}, u32[]{:S(2)}, u32[]{:S(2)}) collective-permute-start(bf16[256,2560]{1,0:T(8,128)(2,1)} %get-tuple-element.72), channel_id=1, source_target_pairs={{0,1},{1,0},{2,3},{3,2},{4,5},{5,4},{6,7},{7,6},{8,9},{9,8},{10,11... | collective-permute-start | bytes 3932168 | tf_op jit(solution)/shard_map/ppermute | solution.py:587
  95.2 11.6 %copy-start = (bf16[1,256,2560]{2,1,0:T(8,128)(2,1)S(1)}, bf16[1,256,2560]{2,1,0:T(8,128)(2,1)}, u32[]{:S(2)}) copy-start(bf16[1,256,2560]{2,1,0:T(8,128)(2,1)} %param.15) | copy-start | bytes 3932164
  95.2 10.6 %collective-permute-start.8 = (f32[256,128]{1,0:T(8,128)}, f32[256,128]{1,0:T(8,128)S(1)}, u32[]{:S(2)}, u32[]{:S(2)}) collective-permute-start(f32[256,128]{1,0:T(8,128)} %get-tuple-element.70), channel_id=1, source_target_pairs={{0,1},{1,0},{2,3},{3,2},{4,5},{5,4},{6,7},{7,6},{8,9},{9,8},{10,11... | collective-permute-start | bytes 393224 | tf_op jit(solution)/shard_map/ppermute | solution.py:587
  108.8 38.1 %collective-permute-start.10 = (bf16[256,2560]{1,0:T(8,128)(2,1)S(1)}, bf16[256,2560]{1,0:T(8,128)(2,1)S(1)}, u32[]{:S(2)}, u32[]{:S(2)}) collective-permute-start(bf16[256,2560]{1,0:T(8,128)(2,1)S(1)} %add_convert_fusion.1), channel_id=1, source_target_pairs={{0,16},{1,17},{2,18},{3,19},{4,20},{5,21},{6,22},{7,23},{8,24},{9,... | collective-permute-start | bytes 3932168 | tf_op jit(solution)/shard_map/ppermute | solution.py:587
  110.1 52.5 %collective-permute-start.11 = (bf16[256,2560]{1,0:T(8,128)(2,1)S(1)}, bf16[256,2560]{1,0:T(8,128)(2,1)S(1)}, u32[]{:S(2)}, u32[]{:S(2)}) collective-permute-start(bf16[256,2560]{1,0:T(8,128)(2,1)S(1)} %add_convert_fusion.1), channel_id=1, source_target_pairs={{1,16},{0,17},{3,18},{2,19},{5,20},{4,21},{7,22},{6,23},{9,24},{8,... | collective-permute-start | bytes 3932168 | tf_op jit(solution)/shard_map/ppermute | solution.py:587
  111.4 1.4 collective-permute-start.12
  112.1 0.7 collective-permute-start.13
  112.7 49.8 %copy-start.12 = (bf16[16,2560]{1,0:T(8,128)(2,1)}, bf16[16,2560]{1,0:T(8,128)(2,1)S(1)}, u32[]{:S(2)}) copy-start(bf16[16,2560]{1,0:T(8,128)(2,1)S(1)} %collective-permute-done.12.refs_2_) | copy-start | bytes 245764
  112.8 49.8 %copy-start.13 = (bf16[16,2560]{1,0:T(8,128)(2,1)}, bf16[16,2560]{1,0:T(8,128)(2,1)S(1)}, u32[]{:S(2)}) copy-start(bf16[16,2560]{1,0:T(8,128)(2,1)S(1)} %collective-permute-done.13.refs_3_) | copy-start | bytes 245764
  146.8 15.8 %copy-start.1 = (bf16[256,2560]{1,0:T(8,128)(2,1)}, bf16[256,2560]{1,0:T(8,128)(2,1)S(1)}, u32[]{:S(2)}) copy-start(bf16[256,2560]{1,0:T(8,128)(2,1)S(1)} %collective-permute-done.10.refs_0_) | copy-start | bytes 3932164
  162.6 1.2 copy-start.6
  191.2 15.6 %collective-permute-start.14 = (bf16[144,1280]{1,0:T(8,128)(2,1)S(1)}, bf16[144,1280]{1,0:T(8,128)(2,1)S(1)}, u32[]{:S(2)}, u32[]{:S(2)}) collective-permute-start(bf16[144,1280]{1,0:T(8,128)(2,1)S(1)} %broadcast_select_fusion.1), channel_id=1, source_target_pairs={{16,18},{17,19},{18,16},{19,17},{20,22},{21,23},{22,20},{23,21},{2... | collective-permute-start | bytes 1105928 | tf_op jit(solution)/shard_map/ppermute | solution.py:587
  194.5 12.4 %copy-start.4 = (bf16[144,2560]{1,0:T(8,128)(2,1)S(1)}, bf16[144,2560]{1,0:T(8,128)(2,1)}, u32[]{:S(2)}) copy-start(bf16[144,2560]{1,0:T(8,128)(2,1)} %get-tuple-element.74) | copy-start | bytes 2211844
  207.2 20.8 %collective-permute-start.15 = (bf16[144,1280]{1,0:T(8,128)(2,1)S(1)}, bf16[144,1280]{1,0:T(8,128)(2,1)S(1)}, u32[]{:S(2)}, u32[]{:S(2)}) collective-permute-start(bf16[144,1280]{1,0:T(8,128)(2,1)S(1)} %maximum_maximum_fusion.1), channel_id=1, source_target_pairs={{16,20},{17,21},{18,22},{19,23},{20,24},{21,25},{22,26},{23,27},{2... | collective-permute-start | bytes 1105928 | tf_op jit(solution)/shard_map/ppermute | solution.py:587
  211.7 16.3 %collective-permute-start.16 = (bf16[144,1280]{1,0:T(8,128)(2,1)S(1)}, bf16[144,1280]{1,0:T(8,128)(2,1)S(1)}, u32[]{:S(2)}, u32[]{:S(2)}) collective-permute-start(bf16[144,1280]{1,0:T(8,128)(2,1)S(1)} %maximum_maximum_fusion.1), channel_id=1, source_target_pairs={{16,24},{17,25},{18,26},{19,27},{20,28},{21,29},{22,30},{23,31}} | collective-permute-start | bytes 1105928 | tf_op jit(solution)/shard_map/ppermute | solution.py:587
  216.7 11.3 %collective-permute-start.17 = (bf16[144,1280]{1,0:T(8,128)(2,1)S(1)}, bf16[144,1280]{1,0:T(8,128)(2,1)S(1)}, u32[]{:S(2)}, u32[]{:S(2)}) collective-permute-start(bf16[144,1280]{1,0:T(8,128)(2,1)S(1)} %maximum_maximum_fusion.1), channel_id=1, source_target_pairs={{16,28},{17,29},{18,30},{19,31}} | collective-permute-start | bytes 1105928 | tf_op jit(solution)/shard_map/ppermute | solution.py:587
  229.2 7.8 %collective-permute-start.18 = (bf16[128,1280]{1,0:T(8,128)(2,1)S(1)}, bf16[128,1280]{1,0:T(8,128)(2,1)S(1)}, u32[]{:S(2)}, u32[]{:S(2)}) collective-permute-start(bf16[128,1280]{1,0:T(8,128)(2,1)S(1)} %get-tuple-element.109), channel_id=1, source_target_pairs={{16,18},{17,19},{18,16},{19,17},{20,22},{21,23},{22,20},{23,21},{2... | collective-permute-start | bytes 983048 | tf_op jit(solution)/shard_map/ppermute | solution.py:587
  247.5 21.0 %collective-permute-start.20 = (bf16[256,2560]{1,0:T(8,128)(2,1)}, bf16[256,2560]{1,0:T(8,128)(2,1)S(1)}, u32[]{:S(2)}, u32[]{:S(2)}) collective-permute-start(bf16[256,2560]{1,0:T(8,128)(2,1)} %get-tuple-element.95), channel_id=1, source_target_pairs={{16,17},{17,16},{18,19},{19,18},{20,21},{21,20},{22,23},{23,22},{2... | collective-permute-start | bytes 3932168 | tf_op jit(solution)/shard_map/ppermute | solution.py:587
  249.4 19.1 %copy-start.2 = (bf16[256,2560]{1,0:T(8,128)(2,1)S(1)}, bf16[256,2560]{1,0:T(8,128)(2,1)}, u32[]{:S(2)}) copy-start(bf16[256,2560]{1,0:T(8,128)(2,1)} %copy-done.1) | copy-start | bytes 3932164
  249.4 18.0 %collective-permute-start.19 = (f32[256,128]{1,0:T(8,128)}, f32[256,128]{1,0:T(8,128)S(1)}, u32[]{:S(2)}, u32[]{:S(2)}) collective-permute-start(f32[256,128]{1,0:T(8,128)} %get-tuple-element.93), channel_id=1, source_target_pairs={{16,17},{17,16},{18,19},{19,18},{20,21},{21,20},{22,23},{23,22},{2... | collective-permute-start | bytes 393224 | tf_op jit(solution)/shard_map/ppermute | solution.py:587
  (5 other events, 4.8 us)

commit v4 on v3

--- a/solution.py
+++ b/solution.py
@@ -100,22 +100,20 @@
         idc_ref,
         normed_ref,
         x_ref,
-        xs_ref,
         bc_ref,
         acol_ref,
         arow_ref,
+        srow_ref,
         ein_ref,
         eall_ref,
         state_ref,
         sent_ref,
         raw,
         keep,
-        stepc,
         wend,
         kept,
         lhs,
         weighted,
-        step_lanes,
         wend_lanes,
         held,
         sems,
@@ -130,8 +128,7 @@
 
     saved = pltpu.make_async_copy(lhs, normed_ref, out_sem)
 
-    @pl.when(step_at == 0)
-    def _():
+    def first():
         gain = gain_ref[...]
 
         def normalize(part):
@@ -186,11 +183,11 @@
             end = total[BLOCK - 1 : BLOCK]
             acol_ref[r0:r1] = total
             arow_ref[:, r0:r1] = total.T
+            srow_ref[:, r0:r1] = part_step.T
             ein_ref[r0:r1] = (jnp.exp(total) * (ids == prev).astype(f32)).astype(bf16)
             eall_ref[r0:r1] = (jnp.exp(total + before) * (ids == first_prev).astype(f32)).astype(
                 bf16
             )
-            stepc[r0:r1] = part_step.astype(bf16)
             wend[r0:r1] = (jnp.exp(end - total) * (ids == last).astype(f32) * part_step).astype(
                 bf16
             )
@@ -200,18 +197,16 @@
             idc_ref[7 + rows : 8 + rows] == first_prev
         ).astype(f32)
 
+    depth = wx_ref.shape[0]
+    tiles = wx_ref.shape[1] // (2 * tile_lanes)
+    place = column_tile(depth, tile_lanes, tiles * tile_lanes)
+    weights = stream(step_at, tiles, wx_ref, held, sems, place, first)
     spread = spread_matrix(heads, width, step_at)
     kept_now = kept[...]
     high = kept_now.astype(bf16)
     low = (kept_now - high.astype(f32)).astype(bf16)
     keep_lanes = dot(high, spread) + dot(low, spread)
-    step_lanes[...] = dot(stepc[...], spread)
     wend_lanes[...] = dot(wend[...], spread)
-    tiles = wx_ref.shape[1] // (2 * tile_lanes)
-    depth = wx_ref.shape[0]
-    weights = stream(
-        step_at, tiles, wx_ref, held, sems, column_tile(depth, tile_lanes, tiles * tile_lanes)
-    )
     for u in range(units):
         cols = slice(u * unit, (u + 1) * unit)
         fresh = dot(lhs[...], weights[:, cols])
@@ -231,7 +226,6 @@
                     b = a + STRIP
                     x_now = conv_rows(raw, keep, taps, bias, a, b, col)
                     x_ref[a:b, strip_cols] = x_now.astype(bf16)
-                    xs_ref[a:b, strip_cols] = (x_now * step_lanes[a:b, strip_cols]).astype(bf16)
                     weighted[a:b, strip_cols] = (x_now * wend_lanes[a:b, strip_cols]).astype(bf16)
             local = lax.dot_general(
                 bc_ref[r0:r1, 0:state_width],
@@ -293,9 +287,9 @@
             out_specs=[
                 pl.BlockSpec(memory_space=pltpu.HBM),
                 pl.BlockSpec((None, rows, tile_lanes), lambda i, at: (i, 0, 0)),
-                pl.BlockSpec((None, rows, tile_lanes), lambda i, at: (i, 0, 0)),
                 whole(rows, 2 * state_width),
                 whole(rows, LANES),
+                whole(LANES, rows),
                 whole(LANES, rows),
                 whole(rows, LANES),
                 whole(rows, LANES),
@@ -308,11 +302,9 @@
                 pltpu.VMEM((rows + 8, max(tile_lanes, 2 * state_width)), f32),
                 pltpu.VMEM((3, rows, LANES), f32),
                 pltpu.VMEM((rows, LANES), bf16),
-                pltpu.VMEM((rows, LANES), bf16),
                 pltpu.VMEM((max(8, blocks + 1), LANES), f32),
                 pltpu.VMEM((rows + HALO, depth), bf16),
                 pltpu.VMEM((rows, tile_lanes), bf16),
-                pltpu.VMEM((rows, tile_lanes), f32),
                 pltpu.VMEM((rows, tile_lanes), f32),
                 pltpu.VMEM((SLOTS, depth, tile_lanes), bf16),
                 pltpu.SemaphoreType.DMA((SLOTS,)),
@@ -322,9 +314,9 @@
         out_shape=[
             jax.ShapeDtypeStruct((rows + HALO, depth), bf16),
             jax.ShapeDtypeStruct((tiles, rows, tile_lanes), bf16),
-            jax.ShapeDtypeStruct((tiles, rows, tile_lanes), bf16),
             jax.ShapeDtypeStruct((rows, 2 * state_width), bf16),
             jax.ShapeDtypeStruct((rows, LANES), f32),
+            jax.ShapeDtypeStruct((LANES, rows), f32),
             jax.ShapeDtypeStruct((LANES, rows), f32),
             jax.ShapeDtypeStruct((rows, LANES), bf16),
             jax.ShapeDtypeStruct((rows, LANES), bf16),
@@ -344,10 +336,10 @@
     heads,
     width,
     x_ref,
-    xs_ref,
     bc_ref,
     acol_ref,
     arow_ref,
+    srow_ref,
     ein_ref,
     state_ref,
     skip_ref,
@@ -387,24 +379,25 @@
             carried = carried * dot(ein_ref[r0:r1], spread)
         for first in range(0, heads, pack):
             cols = slice(first * width, (first + pack) * width)
-            xs_now = xs_ref[r0:r1, cols]
+            x_now = x_ref[r0:r1, cols]
             total = None
             for inner in range(pack):
                 head = first + inner
                 row = arow_ref[head : head + 1, r0:r1]
+                step = srow_ref[head : head + 1, r0:r1]
                 for a in range(0, BLOCK, STRIP):
                     gap = acol[r0 + a : r0 + a + STRIP, head : head + 1] - row
                     weight = jnp.exp(jnp.minimum(gap, 0.0)) * gram[block, a : a + STRIP]
-                    mix[head % 4, a : a + STRIP] = weight.astype(bf16)
-                part = dot(mix[head % 4], xs_now)
+                    mix[head % 4, a : a + STRIP] = (weight * step).astype(bf16)
+                part = dot(mix[head % 4], x_now)
                 total = part if total is None else jnp.where(lane < inner * width, total, part)
-            total = total + skip_ref[:, cols] * x_ref[r0:r1, cols].astype(f32)
+            total = total + skip_ref[:, cols] * x_now.astype(f32)
             if block > 0:
                 total = total + carried[:, cols]
             y_ref[r0:r1, cols] = total.astype(bf16)
 
 
-def inner_call(x, xs, bc, acol, arow, ein, states, skip, idc, idr, sizes):
+def inner_call(x, bc, acol, arow, srow, ein, states, skip, idc, idr, sizes):
     rows, heads, width, tiles, state_width = sizes
     tile_lanes = heads * width
     blocks = rows // BLOCK
@@ -423,9 +416,9 @@
         grid=(tiles,),
         in_specs=[
             tiled,
-            tiled,
             whole(rows, 2 * state_width),
             whole(rows, LANES),
+            pl.BlockSpec((arow_rows, rows), lambda i: (i, 0)),
             pl.BlockSpec((arow_rows, rows), lambda i: (i, 0)),
             whole(rows, LANES),
             pl.BlockSpec((max(blocks - 1, 1), state_width, tile_lanes), lambda i: (0, 0, i)),
@@ -444,7 +437,7 @@
         ),
         cost_estimate=cost(11),
         name="inner",
-    )(x, xs, bc, acol, arow, ein, states, skip, idc, idr)
+    )(x, bc, acol, arow, srow, ein, states, skip, idc, idr)
 
 
 def gate_kernel(tiles, normed_ref, wz_ref, gate_ref, held, sems):
@@ -735,7 +728,7 @@
                 parts, halos = gather_rows(route, current, source, pipe)
             residual = parts[0]
             at = ((tp + jnp.arange(route.tps, dtype=jnp.int32)) % route.tps) * own_rows
-            normed, x, xs, bc, acol, arow, ein, eall, states, sent = scan_call(
+            normed, x, bc, acol, arow, srow, ein, eall, states, sent = scan_call(
                 at,
                 parts,
                 halos,
@@ -758,8 +751,8 @@
                 state_width,
                 pipe,
                 lambda: gate_call(normed, w_zx, sizes),
-                lambda *a: inner_call(*a, bc, acol, arow, ein, states, skip, idc, idr, sizes),
-                (x, xs),
+                lambda a: inner_call(a, bc, acol, arow, srow, ein, states, skip, idc, idr, sizes),
+                (x,),
             )
             swapped = lax.axis_index("seq") % 2
             total = None

time: 273 us -> 267 us (0.978)
  Pallas kernels: 136 us -> 131 us
    pallas_call x2, Pallas kernels: 52.6 us -> 46.5 us  [scan_call(): pl.pallas_call(functools.partial(scan_kernel, rows, heads, width, shares)...]
where the time goes in v4:
time: 267 us; the launch traced here: 266 us
  Pallas kernels  131 us (49%)
  waiting for transfers between devices  60.2 us (23%)
  starting transfers between devices  32.3 us (12%)
  local copies, waits for them, and re-layouts  26.3 us (10%)
  other arithmetic  15.6 us (6%)
    ppermute x21, waiting for transfers between devices, move(): lax.ppermute(block, AXES, [(self.spot(*source), self.spot(*target)) for s...  60.2 us
    pallas_call x2, Pallas kernels, scan_call(): pl.pallas_call(functools.partial(scan_kernel, rows, heads, width, shares)...  46.5 us
    pallas_call x4, Pallas kernels, out_call(): pl.pallas_call(functools.partial(out_kernel, heads, width), grid_spec=plt...  39.1 us
    ppermute x21, starting transfers between devices, move(): lax.ppermute(block, AXES, [(self.spot(*source), self.spot(*target)) for s...  32.3 us
    pallas_call x2, Pallas kernels, gate_call(): pl.pallas_call(functools.partial(gate_kernel, tiles), grid=(tiles,), in_s...  24.6 us
    pallas_call x2, Pallas kernels, inner_call(): pl.pallas_call(functools.partial(inner_kernel, rows, heads, width), grid=...  21 us
    unnamed x33, local copies, waits for them, and re-layouts  21 us
  transfers between devices with their start and end apart: 21, of which 4 were waited for; matrix products, arithmetic and copies ran while one was open for 10% of the time, Pallas kernels for 24%

profile of v4, /device:TPU:1, one launch (start us, length us, event | category | flops | bytes accessed | tf_op | source)
XLA Modules:
  0.0 266.2 jit_solution(3430255328303940977)
XLA Ops:
  4.5 18.1 %copy.16 = bf16[320,8,2,2560]{3,1,2,0:T(8,128)(2,1)} copy(bf16[320,8,2,2560]{3,2,1,0:T(2,128)(2,1)} %bitcast.33) | data formatting | bytes 52428800
  26.4 23.2 %scan.2 = (bf16[528,2560]{1,0:T(8,128)(2,1)}, bf16[5,512,512]{2,1,0:T(8,128)(2,1)}, bf16[512,256]{1,0:T(8,128)(2,1)}, f32[512,128]{1,0:T(8,128)}, f32[128,512]{1...) custom-call(s32[2]{0:T(128)} %fusion.21.at_ref, ...), custom_call_target="tpu_custom_call" | custom-call | flops 3750000128 | tf_op jit(solution)/shard_map/scan/pallas_call | solution.py:267
  49.7 1.1 broadcast_select_fusion.3
  51.6 12.3 %gate.2.gate_ref = bf16[5,512,512]{2,1,0:T(8,128)(2,1)} custom-call(bf16[528,2560]{1,0:T(8,128)(2,1)} %get-tuple-element.50.normed_ref, bf16[2560,5120]{1,0:T(8,128)(2,1)} %bitcast.26), custom_call_target="tpu_custom_call" | custom-call | flops 2000000000 | tf_op jit(solution)/shard_map/gate/pallas_call | solution.py:454
  67.8 10.5 %inner.2.y_ref = bf16[5,512,512]{2,1,0:T(8,128)(2,1)} custom-call(bf16[5,512,512]{2,1,0:T(8,128)(2,1)} %get-tuple-element.54.x_ref, bf16[512,256]{1,0:T(8,128)(2,1)} %get-tuple-element.55.bc_ref, f32[512,128]{1,0:T(8,128)} %get-tuple-element.56.acol_ref, f32[128,512]{1,0:T(8,128)} %get-tuple-element.57.arow_ref, f32[128,512]{1,0:T(8,128)} %get-tuple-element.58.srow_ref, ...), custom_call_target="tpu_custom_call" | custom-call | flops 2750000128 | tf_op jit(solution)/shard_map/inner/pallas_call | solution.py:414
  81.6 9.8 %outp.4 = (bf16[256,2560]{1,0:T(8,128)(2,1)}, f32[256,128]{1,0:T(8,128)}) custom-call(s32[2]{0:T(128)} %pad_add_fusion.at_ref, bf16[5,512,512]{2,1,0:T(8,128)(2,1)} %inner.2.y_ref, bf16[5,512,512]{2,1,0:T(8,128)(2,1)} %gate.2.gate_ref, bf16[512,256]{1,0:T(8,128)(2,1)} %get-tuple-element.55.bc_ref, bf16[512,128]{1,0:T(8,128)(2,1)} %get-tuple-element.63.eall_ref, ...), custom_call_target="tpu_custom_call" | custom-call | flops 1500000000 | tf_op jit(solution)/shard_map/outp/pallas_call | solution.py:534
  93.6 9.8 %outp.5 = (bf16[256,2560]{1,0:T(8,128)(2,1)}, f32[256,128]{1,0:T(8,128)}) custom-call(s32[2]{0:T(128)} %pad_add_fusion.1.at_ref, bf16[5,512,512]{2,1,0:T(8,128)(2,1)} %inner.2.y_ref, bf16[5,512,512]{2,1,0:T(8,128)(2,1)} %gate.2.gate_ref, bf16[512,256]{1,0:T(8,128)(2,1)} %get-tuple-element.55.bc_ref, bf16[512,128]{1,0:T(8,128)(2,1)} %get-tuple-element.63.eall_ref, ...), custom_call_target="tpu_custom_call" | custom-call | flops 1500000000 | tf_op jit(solution)/shard_map/outp/pallas_call | solution.py:534
  103.4 1.0 fusion.15
  104.4 1.9 add_convert_fusion.1
  106.3 1.3 collective-permute-start.10
  107.6 1.3 collective-permute-start.11
  110.3 34.0 %collective-permute-done.10.refs_0_ = bf16[256,2560]{1,0:T(8,128)(2,1)S(1)} collective-permute-done((bf16[256,2560]{1,0:T(8,128)(2,1)S(1)}, bf16[256,2560]{1,0:T(8,128)(2,1)S(1)}, u32[]{:S(2)}, u32[]{:S(2)}) %collective-permute-start.10) | collective-permute-done | bytes 1310752 | tf_op jit(solution)/shard_map/ppermute | solution.py:580
  144.4 15.8 %collective-permute-done.11.refs_1_ = bf16[256,2560]{1,0:T(8,128)(2,1)S(1)} collective-permute-done((bf16[256,2560]{1,0:T(8,128)(2,1)S(1)}, bf16[256,2560]{1,0:T(8,128)(2,1)S(1)}, u32[]{:S(2)}, u32[]{:S(2)}) %collective-permute-start.11) | collective-permute-done | bytes 1310752 | tf_op jit(solution)/shard_map/ppermute | solution.py:580
  160.2 1.1 copy-done.6
  161.3 23.2 %scan.3 = (bf16[528,2560]{1,0:T(8,128)(2,1)}, bf16[5,512,512]{2,1,0:T(8,128)(2,1)}, bf16[512,256]{1,0:T(8,128)(2,1)}, f32[512,128]{1,0:T(8,128)}, f32[128,512]{1...) custom-call(s32[2]{0:T(128)} %fusion.21.at_ref, ...), custom_call_target="tpu_custom_call" | custom-call | flops 3750000128 | tf_op jit(solution)/shard_map/scan/pallas_call | solution.py:267
  184.6 1.1 broadcast_select_fusion.1
  185.7 3.3 %collective-permute-start.14 = (bf16[144,1280]{1,0:T(8,128)(2,1)S(1)}, bf16[144,1280]{1,0:T(8,128)(2,1)S(1)}, u32[]{:S(2)}, u32[]{:S(2)}) collective-permute-start(bf16[144,1280]{1,0:T(8,128)(2,1)S(1)} %broadcast_select_fusion.1), channel_id=1, source_target_pairs={{16,18},{17,19},{18,16},{19,17},{20,22},{21,23},{22,20},{23,21},{2... | collective-permute-start | bytes 1105928 | tf_op jit(solution)/shard_map/ppermute | solution.py:580
  189.0 12.3 %gate.3.gate_ref = bf16[5,512,512]{2,1,0:T(8,128)(2,1)} custom-call(bf16[528,2560]{1,0:T(8,128)(2,1)} %get-tuple-element.72.normed_ref, bf16[2560,5120]{1,0:T(8,128)(2,1)} %bitcast.28), custom_call_target="tpu_custom_call" | custom-call | flops 2000000000 | tf_op jit(solution)/shard_map/gate/pallas_call | solution.py:454
  201.7 3.9 %collective-permute-start.15 = (bf16[144,1280]{1,0:T(8,128)(2,1)S(1)}, bf16[144,1280]{1,0:T(8,128)(2,1)S(1)}, u32[]{:S(2)}, u32[]{:S(2)}) collective-permute-start(bf16[144,1280]{1,0:T(8,128)(2,1)S(1)} %maximum_maximum_fusion.1), channel_id=1, source_target_pairs={{16,20},{17,21},{18,22},{19,23},{20,24},{21,25},{22,26},{23,27},{2... | collective-permute-start | bytes 1105928 | tf_op jit(solution)/shard_map/ppermute | solution.py:580
  205.6 5.0 %collective-permute-start.16 = (bf16[144,1280]{1,0:T(8,128)(2,1)S(1)}, bf16[144,1280]{1,0:T(8,128)(2,1)S(1)}, u32[]{:S(2)}, u32[]{:S(2)}) collective-permute-start(bf16[144,1280]{1,0:T(8,128)(2,1)S(1)} %maximum_maximum_fusion.1), channel_id=1, source_target_pairs={{16,24},{17,25},{18,26},{19,27},{20,28},{21,29},{22,30},{23,31}} | collective-permute-start | bytes 1105928 | tf_op jit(solution)/shard_map/ppermute | solution.py:580
  210.7 1.3 collective-permute-start.17
  212.0 10.5 %inner.3.y_ref = bf16[5,512,512]{2,1,0:T(8,128)(2,1)} custom-call(bf16[5,512,512]{2,1,0:T(8,128)(2,1)} %get-tuple-element.76.x_ref, bf16[512,256]{1,0:T(8,128)(2,1)} %get-tuple-element.77.bc_ref, f32[512,128]{1,0:T(8,128)} %get-tuple-element.78.acol_ref, f32[128,512]{1,0:T(8,128)} %get-tuple-element.79.arow_ref, f32[128,512]{1,0:T(8,128)} %get-tuple-element.80.srow_ref, ...), custom_call_target="tpu_custom_call" | custom-call | flops 2750000128 | tf_op jit(solution)/shard_map/inner/pallas_call | solution.py:414
  222.7 1.0 select_convert_fusion
  223.7 2.2 collective-permute-start.18
  225.9 5.6 %collective-permute-done.18.got_ref = bf16[128,1280]{1,0:T(8,128)(2,1)S(1)} collective-permute-done((bf16[128,1280]{1,0:T(8,128)(2,1)S(1)}, bf16[128,1280]{1,0:T(8,128)(2,1)S(1)}, u32[]{:S(2)}, u32[]{:S(2)}) %collective-permute-start.18) | collective-permute-done | bytes 327712 | tf_op jit(solution)/shard_map/ppermute | solution.py:580
  232.2 9.8 %outp.6 = (bf16[256,2560]{1,0:T(8,128)(2,1)}, f32[256,128]{1,0:T(8,128)}) custom-call(s32[2]{0:T(128)} %pad_add_fusion.at_ref, bf16[5,512,512]{2,1,0:T(8,128)(2,1)} %inner.3.y_ref, bf16[5,512,512]{2,1,0:T(8,128)(2,1)} %gate.3.gate_ref, bf16[512,256]{1,0:T(8,128)(2,1)} %get-tuple-element.77.bc_ref, bf16[512,128]{1,0:T(8,128)(2,1)} %get-tuple-element.85.eall_ref, ...), custom_call_target="tpu_custom_call" | custom-call | flops 1500000000 | tf_op jit(solution)/shard_map/outp/pallas_call | solution.py:534
  242.0 1.9 collective-permute-start.20
  243.9 3.5 %collective-permute-start.19 = (f32[256,128]{1,0:T(8,128)}, f32[256,128]{1,0:T(8,128)S(1)}, u32[]{:S(2)}, u32[]{:S(2)}) collective-permute-start(f32[256,128]{1,0:T(8,128)} %get-tuple-element.89), channel_id=1, source_target_pairs={{16,17},{17,16},{18,19},{19,18},{20,21},{21,20},{22,23},{23,22},{2... | collective-permute-start | bytes 393224 | tf_op jit(solution)/shard_map/ppermute | solution.py:580
  247.4 9.8 %outp.7 = (bf16[256,2560]{1,0:T(8,128)(2,1)}, f32[256,128]{1,0:T(8,128)}) custom-call(s32[2]{0:T(128)} %pad_add_fusion.1.at_ref, bf16[5,512,512]{2,1,0:T(8,128)(2,1)} %inner.3.y_ref, bf16[5,512,512]{2,1,0:T(8,128)(2,1)} %gate.3.gate_ref, bf16[512,256]{1,0:T(8,128)(2,1)} %get-tuple-element.77.bc_ref, bf16[512,128]{1,0:T(8,128)(2,1)} %get-tuple-element.85.eall_ref, ...), custom_call_target="tpu_custom_call" | custom-call | flops 1500000000 | tf_op jit(solution)/shard_map/outp/pallas_call | solution.py:534
  257.2 4.7 %collective-permute-done.19 = f32[256,128]{1,0:T(8,128)S(1)} collective-permute-done((f32[256,128]{1,0:T(8,128)}, f32[256,128]{1,0:T(8,128)S(1)}, u32[]{:S(2)}, u32[]{:S(2)}) %collective-permute-start.19) | collective-permute-done | bytes 131104 | tf_op jit(solution)/shard_map/ppermute | solution.py:580
  262.0 1.0 fusion.11
  263.0 3.2 %fusion.1 = bf16[1,1,256,2560]{3,2,1,0:T(8,128)(2,1)} fusion(bf16[256,2560]{1,0:T(8,128)(2,1)} %get-tuple-element.92, bf16[256,2560]{1,0:T(8,128)(2,1)S(1)} %collective-permute-done.20, bf16[256,2560]{1,0:T(8,128)(2,1)S(1)} %copy-done.2, bf16[256,2560]{1,0:T(8,128)(2,1)S(1)} %add_convert_fusion.1, f32[256]{0:T(256)S(1)} %fusion.11, pred[]{:T(512)S(6)} %eq.26, ...), kind=kLoop, calls=%fused_computation.3 | loop fusion | flops 5898240 | bytes 6554626 | tf_op jit(solution)/shard_map/broadcast_in_dim;stack | solution.py:783
  (100 shorter events, 20.8 us)
Async XLA Ops:
  0.0 25.3 %collective-permute-start = (bf16[256,2560]{1,0:T(8,128)(2,1)}, bf16[256,2560]{1,0:T(8,128)(2,1)S(1)}, u32[]{:S(2)}, u32[]{:S(2)}) collective-permute-start(bf16[256,2560]{1,0:T(8,128)(2,1)} %bitcast.34), channel_id=1, source_target_pairs={{1,0},{0,1},{3,2},{2,3},{5,4},{4,5},{7,6},{6,7},{9,8},{8,9},{11,10... | collective-permute-start | bytes 3932168 | tf_op jit(solution)/shard_map/ppermute | solution.py:580
  2.4 22.7 %collective-permute-start.1 = (bf16[32,2560]{1,0:T(8,128)(2,1)S(1)}, bf16[32,2560]{1,0:T(8,128)(2,1)S(1)}, u32[]{:S(2)}, u32[]{:S(2)}) collective-permute-start(bf16[32,2560]{1,0:T(8,128)(2,1)S(1)} %pad_maximum_fusion), channel_id=1, source_target_pairs={{1,2},{3,4},{5,6},{7,8},{9,10},{11,12},{13,14},{17,18},{19,20},{21... | collective-permute-start | bytes 491528 | tf_op jit(solution)/shard_map/ppermute | solution.py:580
  3.1 22.1 %collective-permute-start.2 = (bf16[32,2560]{1,0:T(8,128)(2,1)S(1)}, bf16[32,2560]{1,0:T(8,128)(2,1)S(1)}, u32[]{:S(2)}, u32[]{:S(2)}) collective-permute-start(bf16[32,2560]{1,0:T(8,128)(2,1)S(1)} %pad_maximum_fusion), channel_id=1, source_target_pairs={{1,3},{3,5},{5,7},{7,9},{9,11},{11,13},{13,15},{17,19},{19,21},{21... | collective-permute-start | bytes 491528 | tf_op jit(solution)/shard_map/ppermute | solution.py:580
  4.5 18.1 %copy-start.9 = (bf16[1,2560,40]{1,2,0:T(8,128)(2,1)S(1)}, bf16[1,2560,40]{1,2,0:T(8,128)(2,1)}, u32[]{:S(2)}) copy-start(bf16[1,2560,40]{1,2,0:T(8,128)(2,1)} %param.20) | copy-start | bytes 614404
  4.5 19.6 %copy-start.15 = (f32[1,40]{1,0:T(1,128)S(1)}, f32[1,40]{1,0:T(1,128)}, u32[]{:S(2)}) copy-start(f32[1,40]{1,0:T(1,128)} %param.25) | copy-start | bytes 484
  50.8 13.1 %collective-permute-start.3 = (bf16[144,1280]{1,0:T(8,128)(2,1)S(1)}, bf16[144,1280]{1,0:T(8,128)(2,1)S(1)}, u32[]{:S(2)}, u32[]{:S(2)}) collective-permute-start(bf16[144,1280]{1,0:T(8,128)(2,1)S(1)} %broadcast_select_fusion.3), channel_id=1, source_target_pairs={{0,2},{1,3},{2,0},{3,1},{4,6},{5,7},{6,4},{7,5},{8,10},{9,11},{10,... | collective-permute-start | bytes 1105928 | tf_op jit(solution)/shard_map/ppermute | solution.py:580
  51.6 12.3 %copy-start.3 = (bf16[144,2560]{1,0:T(8,128)(2,1)S(1)}, bf16[144,2560]{1,0:T(8,128)(2,1)}, u32[]{:S(2)}) copy-start(bf16[144,2560]{1,0:T(8,128)(2,1)} %get-tuple-element.49) | copy-start | bytes 2211844
  64.0 2.4 copy-start.14
  64.3 13.9 %collective-permute-start.4 = (bf16[144,1280]{1,0:T(8,128)(2,1)S(1)}, bf16[144,1280]{1,0:T(8,128)(2,1)S(1)}, u32[]{:S(2)}, u32[]{:S(2)}) collective-permute-start(bf16[144,1280]{1,0:T(8,128)(2,1)S(1)} %maximum_maximum_fusion), channel_id=1, source_target_pairs={{0,4},{1,5},{2,6},{3,7},{4,8},{5,9},{6,10},{7,11},{8,12},{9,13},{1... | collective-permute-start | bytes 1105928 | tf_op jit(solution)/shard_map/ppermute | solution.py:580
  65.0 13.3 %collective-permute-start.5 = (bf16[144,1280]{1,0:T(8,128)(2,1)S(1)}, bf16[144,1280]{1,0:T(8,128)(2,1)S(1)}, u32[]{:S(2)}, u32[]{:S(2)}) collective-permute-start(bf16[144,1280]{1,0:T(8,128)(2,1)S(1)} %maximum_maximum_fusion), channel_id=1, source_target_pairs={{0,8},{1,9},{2,10},{3,11},{4,12},{5,13},{6,14},{7,15}} | collective-permute-start | bytes 1105928 | tf_op jit(solution)/shard_map/ppermute | solution.py:580
  65.7 12.6 %collective-permute-start.6 = (bf16[144,1280]{1,0:T(8,128)(2,1)S(1)}, bf16[144,1280]{1,0:T(8,128)(2,1)S(1)}, u32[]{:S(2)}, u32[]{:S(2)}) collective-permute-start(bf16[144,1280]{1,0:T(8,128)(2,1)S(1)} %maximum_maximum_fusion), channel_id=1, source_target_pairs={{0,12},{1,13},{2,14},{3,15}} | collective-permute-start | bytes 1105928 | tf_op jit(solution)/shard_map/ppermute | solution.py:580
  79.4 1.5 collective-permute-start.7
  91.5 13.0 %collective-permute-start.9 = (bf16[256,2560]{1,0:T(8,128)(2,1)}, bf16[256,2560]{1,0:T(8,128)(2,1)S(1)}, u32[]{:S(2)}, u32[]{:S(2)}) collective-permute-start(bf16[256,2560]{1,0:T(8,128)(2,1)} %get-tuple-element.69), channel_id=1, source_target_pairs={{0,1},{1,0},{2,3},{3,2},{4,5},{5,4},{6,7},{7,6},{8,9},{9,8},{10,11... | collective-permute-start | bytes 3932168 | tf_op jit(solution)/shard_map/ppermute | solution.py:580
  92.8 11.6 %copy-start = (bf16[1,256,2560]{2,1,0:T(8,128)(2,1)S(1)}, bf16[1,256,2560]{2,1,0:T(8,128)(2,1)}, u32[]{:S(2)}) copy-start(bf16[1,256,2560]{2,1,0:T(8,128)(2,1)} %param.15) | copy-start | bytes 3932164
  92.8 10.6 %collective-permute-start.8 = (f32[256,128]{1,0:T(8,128)}, f32[256,128]{1,0:T(8,128)S(1)}, u32[]{:S(2)}, u32[]{:S(2)}) collective-permute-start(f32[256,128]{1,0:T(8,128)} %get-tuple-element.67), channel_id=1, source_target_pairs={{0,1},{1,0},{2,3},{3,2},{4,5},{5,4},{6,7},{7,6},{8,9},{9,8},{10,11... | collective-permute-start | bytes 393224 | tf_op jit(solution)/shard_map/ppermute | solution.py:580
  106.3 38.1 %collective-permute-start.10 = (bf16[256,2560]{1,0:T(8,128)(2,1)S(1)}, bf16[256,2560]{1,0:T(8,128)(2,1)S(1)}, u32[]{:S(2)}, u32[]{:S(2)}) collective-permute-start(bf16[256,2560]{1,0:T(8,128)(2,1)S(1)} %add_convert_fusion.1), channel_id=1, source_target_pairs={{0,16},{1,17},{2,18},{3,19},{4,20},{5,21},{6,22},{7,23},{8,24},{9,... | collective-permute-start | bytes 3932168 | tf_op jit(solution)/shard_map/ppermute | solution.py:580
  107.6 52.5 %collective-permute-start.11 = (bf16[256,2560]{1,0:T(8,128)(2,1)S(1)}, bf16[256,2560]{1,0:T(8,128)(2,1)S(1)}, u32[]{:S(2)}, u32[]{:S(2)}) collective-permute-start(bf16[256,2560]{1,0:T(8,128)(2,1)S(1)} %add_convert_fusion.1), channel_id=1, source_target_pairs={{1,16},{0,17},{3,18},{2,19},{5,20},{4,21},{7,22},{6,23},{9,24},{8,... | collective-permute-start | bytes 3932168 | tf_op jit(solution)/shard_map/ppermute | solution.py:580
  109.0 1.4 collective-permute-start.12
  109.6 0.7 collective-permute-start.13
  110.3 49.8 %copy-start.12 = (bf16[16,2560]{1,0:T(8,128)(2,1)}, bf16[16,2560]{1,0:T(8,128)(2,1)S(1)}, u32[]{:S(2)}) copy-start(bf16[16,2560]{1,0:T(8,128)(2,1)S(1)} %collective-permute-done.12.refs_2_) | copy-start | bytes 245764
  110.3 49.8 %copy-start.13 = (bf16[16,2560]{1,0:T(8,128)(2,1)}, bf16[16,2560]{1,0:T(8,128)(2,1)S(1)}, u32[]{:S(2)}) copy-start(bf16[16,2560]{1,0:T(8,128)(2,1)S(1)} %collective-permute-done.13.refs_3_) | copy-start | bytes 245764
  144.4 15.8 %copy-start.1 = (bf16[256,2560]{1,0:T(8,128)(2,1)}, bf16[256,2560]{1,0:T(8,128)(2,1)S(1)}, u32[]{:S(2)}) copy-start(bf16[256,2560]{1,0:T(8,128)(2,1)S(1)} %collective-permute-done.10.refs_0_) | copy-start | bytes 3932164
  160.2 1.2 copy-start.6
  185.7 15.6 %collective-permute-start.14 = (bf16[144,1280]{1,0:T(8,128)(2,1)S(1)}, bf16[144,1280]{1,0:T(8,128)(2,1)S(1)}, u32[]{:S(2)}, u32[]{:S(2)}) collective-permute-start(bf16[144,1280]{1,0:T(8,128)(2,1)S(1)} %broadcast_select_fusion.1), channel_id=1, source_target_pairs={{16,18},{17,19},{18,16},{19,17},{20,22},{21,23},{22,20},{23,21},{2... | collective-permute-start | bytes 1105928 | tf_op jit(solution)/shard_map/ppermute | solution.py:580
  189.0 12.4 %copy-start.4 = (bf16[144,2560]{1,0:T(8,128)(2,1)S(1)}, bf16[144,2560]{1,0:T(8,128)(2,1)}, u32[]{:S(2)}) copy-start(bf16[144,2560]{1,0:T(8,128)(2,1)} %get-tuple-element.71) | copy-start | bytes 2211844
  201.7 20.8 %collective-permute-start.15 = (bf16[144,1280]{1,0:T(8,128)(2,1)S(1)}, bf16[144,1280]{1,0:T(8,128)(2,1)S(1)}, u32[]{:S(2)}, u32[]{:S(2)}) collective-permute-start(bf16[144,1280]{1,0:T(8,128)(2,1)S(1)} %maximum_maximum_fusion.1), channel_id=1, source_target_pairs={{16,20},{17,21},{18,22},{19,23},{20,24},{21,25},{22,26},{23,27},{2... | collective-permute-start | bytes 1105928 | tf_op jit(solution)/shard_map/ppermute | solution.py:580
  205.6 16.9 %collective-permute-start.16 = (bf16[144,1280]{1,0:T(8,128)(2,1)S(1)}, bf16[144,1280]{1,0:T(8,128)(2,1)S(1)}, u32[]{:S(2)}, u32[]{:S(2)}) collective-permute-start(bf16[144,1280]{1,0:T(8,128)(2,1)S(1)} %maximum_maximum_fusion.1), channel_id=1, source_target_pairs={{16,24},{17,25},{18,26},{19,27},{20,28},{21,29},{22,30},{23,31}} | collective-permute-start | bytes 1105928 | tf_op jit(solution)/shard_map/ppermute | solution.py:580
  210.7 11.9 %collective-permute-start.17 = (bf16[144,1280]{1,0:T(8,128)(2,1)S(1)}, bf16[144,1280]{1,0:T(8,128)(2,1)S(1)}, u32[]{:S(2)}, u32[]{:S(2)}) collective-permute-start(bf16[144,1280]{1,0:T(8,128)(2,1)S(1)} %maximum_maximum_fusion.1), channel_id=1, source_target_pairs={{16,28},{17,29},{18,30},{19,31}} | collective-permute-start | bytes 1105928 | tf_op jit(solution)/shard_map/ppermute | solution.py:580
  223.7 7.8 %collective-permute-start.18 = (bf16[128,1280]{1,0:T(8,128)(2,1)S(1)}, bf16[128,1280]{1,0:T(8,128)(2,1)S(1)}, u32[]{:S(2)}, u32[]{:S(2)}) collective-permute-start(bf16[128,1280]{1,0:T(8,128)(2,1)S(1)} %get-tuple-element.105), channel_id=1, source_target_pairs={{16,18},{17,19},{18,16},{19,17},{20,22},{21,23},{22,20},{23,21},{2... | collective-permute-start | bytes 983048 | tf_op jit(solution)/shard_map/ppermute | solution.py:580
  242.0 21.0 %collective-permute-start.20 = (bf16[256,2560]{1,0:T(8,128)(2,1)}, bf16[256,2560]{1,0:T(8,128)(2,1)S(1)}, u32[]{:S(2)}, u32[]{:S(2)}) collective-permute-start(bf16[256,2560]{1,0:T(8,128)(2,1)} %get-tuple-element.91), channel_id=1, source_target_pairs={{16,17},{17,16},{18,19},{19,18},{20,21},{21,20},{22,23},{23,22},{2... | collective-permute-start | bytes 3932168 | tf_op jit(solution)/shard_map/ppermute | solution.py:580
  243.9 19.1 %copy-start.2 = (bf16[256,2560]{1,0:T(8,128)(2,1)S(1)}, bf16[256,2560]{1,0:T(8,128)(2,1)}, u32[]{:S(2)}) copy-start(bf16[256,2560]{1,0:T(8,128)(2,1)} %copy-done.1) | copy-start | bytes 3932164
  243.9 18.0 %collective-permute-start.19 = (f32[256,128]{1,0:T(8,128)}, f32[256,128]{1,0:T(8,128)S(1)}, u32[]{:S(2)}, u32[]{:S(2)}) collective-permute-start(f32[256,128]{1,0:T(8,128)} %get-tuple-element.89), channel_id=1, source_target_pairs={{16,17},{17,16},{18,19},{19,18},{20,21},{21,20},{22,23},{23,22},{2... | collective-permute-start | bytes 393224 | tf_op jit(solution)/shard_map/ppermute | solution.py:580
  (5 other events, 4.8 us)
